TPU v7x, 32 devices: a whole 2x2x4 slice. The times are simulated.
32 devices in a mesh: dp: 16 (over z, y, core), level: 2 (over x).
Axes of the slice: x: 2, y: 2, z: 4, core: 2. Of those that a mesh axis runs over, the one named last changes fastest.
Arguments:
- token_ids: int32 [16, 2, 1536], P('dp', 'level'), may hold values from 0 to 1023
- decoded_mask: int32 [16, 2, 1536], P('dp', 'level'), may hold values 0 or 1
- levels_done: int32 [16], P('dp'), may hold values from 0 to 1
- code_tables: bfloat16 [2, 1024, 1024], P('level'), may hold values from -6 to 6
- mask_vectors: bfloat16 [2, 1024], P('level'), may hold values from -6 to 6
- w_qkv: bfloat16 [3, 1024, 1024], P(None, 'dp', 'level'), may hold values from -6 to 6
- w_out: bfloat16 [1024, 1024], P('level', 'dp'), may hold values from -0.1875 to 0.1875
- w_expand: bfloat16 [1024, 2048], P('dp'), may hold values from -0.1875 to 0.1875
- w_depth: bfloat16 [5, 1024], replicated, may hold values from -2.5 to 2.5
- w_project: bfloat16 [1024, 1024], P('dp'), may hold values from -0.1875 to 0.1875
- level_heads: bfloat16 [2, 1024, 1024], P('level'), may hold values from -0.1875 to 0.1875
Outputs:
- logits: bfloat16 [16, 2, 1536, 1024], P('dp', 'level')
Inputs may be any that keep to these rules, and one draw needn't show every extreme that they name: `levels_done`: levels below it are fully decoded; the level equal to it is the one being decoded.
All inputs are finite; a program needn't handle non-finite values. No bound on the sum of `decoded_mask` on one device may be relied on, other than what follows from the above.
Results may differ from a plain program's by a relative error of at most 0.006.
Values may be sent and summed in bfloat16 or wider, within the bound.
No kernel may reach another device: no remote copies, remote signals or barrier semaphores. Data moves between devices by JAX's collectives and lax.ppermute only.
A program may use at most 192 MiB of HBM per device.

v0:
```python
import jax
import jax.numpy as jnp
from jax import lax
from jax.sharding import PartitionSpec as P

HEADS = 16


def with_halo(x, sides, width):
    for axis, dim in sides:
        devices, length = (lax.axis_size(axis), x.shape[dim])
        up = [(i, (i + 1) % devices) for i in range(devices - 1)]
        down = [(j, i) for i, j in up]
        last = lax.slice_in_dim(x, length - width, length, axis=dim)
        leading = lax.slice_in_dim(x, 0, width, axis=dim)
        before = lax.ppermute(last, axis, up)
        after = lax.ppermute(leading, axis, down)
        x = jnp.concatenate([before, x, after], axis=dim)
    return x


def layer_norm(values):
    centered = values - jnp.mean(values, axis=-1, keepdims=True)
    variance = jnp.mean(centered * centered, axis=-1, keepdims=True)
    return centered * lax.rsqrt(variance + 1e-05)


def contract_with(left, shard_piece):
    return jnp.dot(left, shard_piece, preferred_element_type=jnp.float32)


def contract_three(left, shard_piece):
    return jnp.einsum("fk,jkc->jfc", left, shard_piece, preferred_element_type=jnp.float32)


def body(
    token_ids,
    decoded_mask,
    levels_done,
    code_tables,
    mask_vectors,
    w_qkv,
    w_out,
    w_expand,
    w_depth,
    w_project,
    level_heads,
):
    frames = token_ids.shape[2]
    model_width = code_tables.shape[2]
    groups = lax.axis_size("level")
    level_index = lax.axis_index("level")
    local_rows = frames // groups
    head_dim = model_width // HEADS
    scale = head_dim ** (-0.5)
    id_row = token_ids[0, 0]
    flag_row = decoded_mask[0, 0]
    done_count = levels_done[0]
    own_table = code_tables[0]
    fill_row = mask_vectors[0].astype(jnp.float32)
    all_live = level_index < done_count
    current = level_index == done_count
    use_token = all_live | current & (flag_row == 1)
    codes = lax.broadcasted_iota(jnp.int32, (frames, own_table.shape[0]), 1)
    onehot = (id_row[:, None] == codes).astype(jnp.bfloat16)
    picked = jnp.dot(onehot, own_table, preferred_element_type=jnp.float32)
    level_terms = (
        jnp.where(use_token[:, None], picked, fill_row[None, :])
        .astype(jnp.bfloat16)
        .reshape(groups, local_rows, model_width)
    )
    received = lax.all_to_all(level_terms, "level", split_axis=0, concat_axis=0, tiled=True)
    own_rows = jnp.sum(received, axis=0, dtype=jnp.float32)
    normed = layer_norm(own_rows).astype(jnp.bfloat16)
    full_columns = lax.all_gather(w_qkv, "level", axis=2, tiled=True)
    projected = contract_three(
        normed, lax.all_gather(full_columns, "dp", axis=1, tiled=True)
    ).astype(jnp.bfloat16)
    queries = projected[0].reshape(local_rows, HEADS, head_dim)
    running_max = jnp.full((HEADS, local_rows), -1e30, jnp.float32)
    accumulated = jnp.zeros((local_rows, HEADS, head_dim), jnp.float32)
    key_piece = lax.all_gather(projected[1], "level", axis=0, tiled=True)
    value_piece = lax.all_gather(projected[2], "level", axis=0, tiled=True)
    piece_rows = key_piece.shape[0]
    key_three = key_piece.reshape(piece_rows, HEADS, head_dim)
    value_three = value_piece.reshape(piece_rows, HEADS, head_dim)
    scores = (
        jnp.einsum("qhd,khd->hqk", queries, key_three, preferred_element_type=jnp.float32) * scale
    )
    new_max = jnp.maximum(running_max, jnp.max(scores, axis=-1))
    shrink = jnp.exp(running_max - new_max)
    weights = jnp.exp(scores - new_max[:, :, None])
    weight_sum = jnp.sum(weights, axis=-1)
    added = jnp.einsum(
        "hqk,khd->qhd",
        weights.astype(jnp.bfloat16),
        value_three,
        preferred_element_type=jnp.float32,
    )
    accumulated = accumulated * shrink.T[:, :, None] + added
    running_max, weight_sum, accumulated = (new_max, weight_sum, accumulated)
    attended = (
        (accumulated / weight_sum.T[:, :, None])
        .reshape(local_rows, model_width)
        .astype(jnp.bfloat16)
    )
    out_full = lax.all_gather(w_out, "level", axis=0, tiled=True)
    after_attn = own_rows + jnp.dot(
        attended,
        lax.all_gather(out_full, "dp", axis=1, tiled=True),
        preferred_element_type=jnp.float32,
    )
    normed_two = layer_norm(after_attn).astype(jnp.bfloat16)
    gate_linear = contract_with(normed_two, lax.all_gather(w_expand, "dp", axis=0, tiled=True))
    gated = (gate_linear[:, :model_width] * jax.nn.sigmoid(gate_linear[:, model_width:])).astype(
        jnp.bfloat16
    )
    half_width = w_depth.shape[0] // 2
    padded = with_halo(gated, (("level", 0),), half_width)
    conv = jnp.zeros((local_rows, model_width), jnp.float32)
    for tap_index in range(w_depth.shape[0]):
        conv = conv + padded[tap_index : tap_index + local_rows].astype(jnp.float32) * w_depth[
            tap_index
        ].astype(jnp.float32)
    activated = (conv * jax.nn.sigmoid(conv)).astype(jnp.bfloat16)
    after_conv = after_attn + contract_with(
        activated, lax.all_gather(w_project, "dp", axis=0, tiled=True)
    )
    final_norm = layer_norm(after_conv).astype(jnp.bfloat16)
    own_head = level_heads[0]
    logits = jnp.dot(
        lax.all_gather(final_norm, "level", axis=0, tiled=True),
        own_head,
        preferred_element_type=jnp.float32,
    ).astype(jnp.bfloat16)
    return logits[None, None]


def solution(mesh):
    return jax.shard_map(
        body,
        mesh=mesh,
        in_specs=(
            P("dp", "level", None),
            P("dp", "level", None),
            P("dp"),
            P("level", None, None),
            P("level", None),
            P(None, "dp", "level"),
            P("level", "dp"),
            P("dp", None),
            P(),
            P("dp", None),
            P("level", None, None),
        ),
        out_specs=P("dp", "level", None, None),
        check_vma=False,
    )
```

profile of v0, /device:TPU:14, one launch (start us, length us, event | category | flops | bytes accessed | tf_op | source)
XLA Modules:
  0.0 384.0 jit_solution(2967878390888933590)
XLA Ops:
  6.5 0.0 copy-start
  6.5 0.0 all-gather.10.cloned.1.call-start
  6.5 8.1 %all_gather.27 = bf16[3,64,1024]{2,1,0:T(8,128)(2,1)} all-gather(bf16[3,64,512]{2,1,0:T(8,128)(2,1)} %param.16), channel_id=1, replica_groups=mesh['dp'=16,'level'=2] {'level'}, dimensions={2}, use_global_device_ids=true | all-gather | bytes 589824 | tf_op jit(solution)/shard_map/all_gather | solution.py:75
  14.7 0.0 all-gather.10.cloned.1.call-update
  14.7 0.0 all-gather.20.cloned.1.call-start
  15.4 0.7 broadcast_in_dim.53
  16.1 0.7 reduce.2
  16.8 0.7 or_reduce_fusion
  17.5 0.0 copy-done
  17.6 4.3 %select_convert_fusion = bf16[1536,1024]{1,0:T(8,128)(2,1)S(1)} fusion(f32[1024]{0:T(1024)S(1)} %bitcast.56, s32[1536]{0:T(1024)S(1)} %reduce.2, pred[1536]{0:T(1024)(128)(4,1)S(1)} %or_reduce_fusion, bf16[1,1024,1024]{2,1,0:T(8,128)(2,1)S(1)} %copy-done), kind=kOutput, calls=%fused_computation.7 | convolution fusion | flops 3224371200 | bytes 5254656 | tf_op jit(solution)/shard_map/dot_general | solution.py:66
  21.8 38.2 %all_to_all.5 = bf16[2,768,1024]{2,1,0:T(8,128)(2,1)S(1)} all-to-all(bf16[2,768,1024]{2,1,0:T(8,128)(2,1)S(1)} %bitcast.48), channel_id=1, replica_groups=mesh['dp'=16,'level'=2] {'level'}, dimensions={0} | all-to-all | bytes 6291456 | tf_op jit(solution)/shard_map/all_to_all | solution.py:72
  60.0 0.7 convert_reduce_fusion
  60.7 0.0 copy-start.2
  60.7 0.4 multiply_reduce_fusion.3
  61.1 15.4 %all-gather.10.cloned.1.call-done = bf16[3,1024,1024]{2,1,0:T(8,128)(2,1)} async-done(((bf16[3,64,1024]{2,1,0:T(8,128)(2,1)}), bf16[3,1024,1024]{2,1,0:T(8,128)(2,1)}) %all-gather.10.cloned.1.call-update) | async-done | bytes 6291472 | tf_op jit(solution)/shard_map/all_gather | solution.py:77
  76.5 8.3 %convert_bitcast_fusion = bf16[3,768,1024]{2,1,0:T(8,128)(2,1)S(1)} fusion(bf16[3,1024,1024]{2,1,0:T(8,128)(2,1)} %all-gather.10.cloned.1.call-done, f32[768,1024]{1,0:T(8,128)S(1)} %get-tuple-element.6, f32[768]{0:T(1024)S(1)} %add_rsqrt_fusion.2, f32[768]{0:T(1024)S(1)} %broadcast_multiply_fusion.2), kind=kOutput, calls=%fused_computation.10 | convolution fusion | flops 4836556800 | bytes 14161920 | tf_op jit(solution)/shard_map/fk,jkc->jfc/dot_general | solution.py:33
  84.8 0.0 copy-done.2
  84.8 2.3 fusion.36
  87.1 0.0 copy-start.5
  87.1 0.0 copy-start.3
  87.1 0.0 all-gather.20.cloned.1.call-update
  87.1 0.0 all-gather.22.cloned.1.call-start
  87.2 0.7 all-gather.22.cloned.1.call-update
  87.9 0.0 all-gather.12.cloned.1.call-start
  87.9 0.0 copy-done.5
  87.9 5.0 %all_gather.31 = bf16[1024,64]{0,1:T(8,128)(2,1)} all-gather(bf16[512,64]{0,1:T(8,128)(2,1)S(1)} %copy-done.5), channel_id=1, replica_groups=mesh['dp'=16,'level'=2] {'level'}, dimensions={0}, use_global_device_ids=true | all-gather | bytes 196608 | tf_op jit(solution)/shard_map/all_gather | solution.py:107
  93.0 0.0 all-gather.12.cloned.1.call-update
  93.0 0.0 all-gather.14.cloned.1.call-start
  93.0 0.5 all-gather.14.cloned.1.call-update
  93.6 0.0 all-gather.16.cloned.1.call-start
  93.6 0.5 all-gather.16.cloned.1.call-update
  94.2 0.2 all-gather.18.cloned.1.call-start
  94.4 0.0 copy-done.3
  94.4 1.6 copy.15
  96.0 34.9 %all-gather.20.cloned.1.call-done = bf16[1,1536,1024]{2,1,0:T(8,128)(2,1)} async-done(((bf16[1,768,1024]{2,1,0:T(8,128)(2,1)}), bf16[1,1536,1024]{2,1,0:T(8,128)(2,1)}) %all-gather.20.cloned.1.call-update) | async-done | bytes 3145744 | tf_op jit(solution)/shard_map/all_gather | solution.py:82
  130.9 3.2 copy.16
  134.0 29.0 %multiply_reduce_fusion = (f32[16,768]{1,0:T(8,128)S(1)}, f32[16,768,1536]{2,1,0:T(8,128)}) fusion(bf16[768,16,64]{0,2,1:T(8,128)(2,1)} %bitcast.47, bf16[1536,16,64]{0,2,1:T(8,128)(2,1)S(1)} %bitcast.45), kind=kOutput, calls=%fused_computation.1 | convolution fusion | flops 2453655552 | bytes 80265216 | tf_op jit(solution)/shard_map/qhd,khd->hqk/dot_general | solution.py:88
  163.1 24.1 %fusion = f32[16,768]{1,0:T(8,128)S(1)} fusion(f32[16,768,1536]{2,1,0:T(8,128)} %get-tuple-element.20, f32[16,768]{1,0:T(8,128)S(1)} %get-tuple-element.13), kind=kLoop, calls=%fused_computation.2 | loop fusion | flops 56610816 | bytes 75595776 | tf_op jit(solution)/shard_map/reduce_sum | solution.py:93
  187.2 0.0 all-gather.22.cloned.1.call-done
  187.2 3.2 copy.17
  190.4 27.7 %fusion.11 = bf16[768,16,64]{0,2,1:T(8,128)(2,1)} fusion(bf16[1536,16,64]{0,2,1:T(8,128)(2,1)S(1)} %bitcast.46, f32[16,768,1536]{2,1,0:T(8,128)} %get-tuple-element.20, f32[16,768]{1,0:T(8,128)S(1)} %get-tuple-element.13, f32[768,16]{0,1:T(8,128)S(1)} %bitcast.50, f32[768,16]{0,1:T(8,128)S(1)} %get-tuple-element.12), kind=kOutput, calls=%fused_computation.20 | convolution fusion | flops 2474901504 | bytes 80363520 | tf_op jit(solution)/shard_map/hqk,khd->qhd/dot_general | solution.py:94
  218.1 1.6 all-gather.12.cloned.1.call-done
  219.7 4.9 %fusion.38 = (f32[768]{0:T(1024)S(1)}, f32[768,1024]{1,0:T(8,128)S(1)}) fusion(f32[768,1024]{1,0:T(8,128)} %copy-done.2, bf16[768,1024]{0,1:T(8,128)(2,1)} %bitcast.49, bf16[1024,1024]{0,1:T(8,128)(2,1)} %all-gather.12.cloned.1.call-done), kind=kOutput, calls=%fused_computation.73 | convolution fusion | flops 1612184832 | bytes 9964544 | tf_op jit(solution)/shard_map/dot_general | solution.py:108
  224.6 0.4 multiply_reduce_fusion.2
  225.1 47.0 %all-gather.14.cloned.1.call-done = bf16[1024,2048]{1,0:T(8,128)(2,1)} async-done(((bf16[64,2048]{1,0:T(8,128)(2,1)}), bf16[1024,2048]{1,0:T(8,128)(2,1)}) %all-gather.14.cloned.1.call-update) | async-done | bytes 4194320 | tf_op jit(solution)/shard_map/all_gather | solution.py:114
  272.1 5.3 %fusion.22 = f32[768,2048]{1,0:T(8,128)S(1)} fusion(bf16[1024,2048]{1,0:T(8,128)(2,1)} %all-gather.14.cloned.1.call-done, f32[768,1024]{1,0:T(8,128)S(1)} %get-tuple-element.22, f32[768]{0:T(1024)S(1)} %add_rsqrt_fusion.1, f32[768]{0:T(1024)S(1)} %broadcast_multiply_fusion.1), kind=kOutput, calls=%fused_computation.41 | convolution fusion | flops 3223584768 | bytes 13637632 | tf_op jit(solution)/shard_map/dot_general | solution.py:29
  277.4 0.0 copy-start.6
  277.4 0.9 fusion.13
  278.3 0.0 copy-start.4
  278.3 1.1 copy-done.4
  279.4 1.3 collective-permute-start
  280.7 4.8 %collective-permute-start.1 = (bf16[2,1024]{1,0:T(2,128)(2,1)S(1)}, bf16[2,1024]{1,0:T(2,128)(2,1)S(1)}, u32[]{:S(2)}, u32[]{:S(2)}) collective-permute-start(bf16[2,1024]{1,0:T(2,128)(2,1)S(1)} %get-tuple-element.11), channel_id=1, source_target_pairs={{1,0},{3,2},{5,4},{7,6},{9,8},{11,10},{13,12},{15,14},{17,16},{19,... | collective-permute-start | bytes 12296 | tf_op jit(solution)/shard_map/ppermute | solution.py:17
  285.5 0.0 copy-done.6
  285.5 27.4 %all-gather.16.cloned.1.call-done = bf16[1024,1024]{1,0:T(8,128)(2,1)} async-done(((bf16[64,1024]{1,0:T(8,128)(2,1)}), bf16[1024,1024]{1,0:T(8,128)(2,1)}) %all-gather.16.cloned.1.call-update) | async-done | bytes 2097168 | tf_op jit(solution)/shard_map/all_gather | solution.py:127
  312.9 0.0 collective-permute-done
  312.9 0.0 collective-permute-done.1
  312.9 9.5 %fusion.39 = (f32[768]{0:T(1024)S(1)}, f32[768,1024]{1,0:T(8,128)S(1)}) fusion(f32[768,1024]{1,0:T(8,128)S(1)} %get-tuple-element.22, bf16[1024,1024]{1,0:T(8,128)(2,1)} %all-gather.16.cloned.1.call-done, bf16[768,1024]{1,0:T(8,128)(2,1)} %copy-done.4, bf16[2,1024]{1,0:T(2,128)(2,1)S(1)} %collective-permute-done.1, ...), kind=kOutput, calls=%fused_computation.74 | convolution fusion | flops 1636564224 | bytes 9993216 | tf_op jit(solution)/shard_map/dot_general | solution.py:29
  322.4 0.4 multiply_reduce_fusion.1
  322.9 1.5 multiply_convert_fusion
  324.4 0.0 all-gather.18.cloned.1.call-update
  324.4 44.9 %all-gather.18.cloned.1.call-done = bf16[1536,1024]{1,0:T(8,128)(2,1)} async-done(((bf16[768,1024]{1,0:T(8,128)(2,1)}), bf16[1536,1024]{1,0:T(8,128)(2,1)}) %all-gather.18.cloned.1.call-update) | async-done | bytes 3145744 | tf_op jit(solution)/shard_map/all_gather | solution.py:132
  369.3 0.0 copy-start.1
  369.3 7.8 %fusion.5 = bf16[1,1,1536,1024]{3,2,1,0:T(8,128)(2,1)} fusion(bf16[1536,1024]{1,0:T(8,128)(2,1)} %all-gather.18.cloned.1.call-done, bf16[1,1024,1024]{2,1,0:T(8,128)(2,1)} %param.21), kind=kOutput, calls=%fused_computation.12 | convolution fusion | flops 3222798336 | bytes 8388608 | tf_op jit(solution)/shard_map/dot_general | solution.py:131
  377.1 0.0 copy-done.1
  (9 shorter events, 0.1 us)
Async XLA Ops:
  6.5 11.0 %copy-start = (bf16[1,1024,1024]{2,1,0:T(8,128)(2,1)S(1)}, bf16[1,1024,1024]{2,1,0:T(8,128)(2,1)}, u32[]{:S(2)}) copy-start(bf16[1,1024,1024]{2,1,0:T(8,128)(2,1)} %param.14) | copy-start | bytes 6291460
  6.5 70.0 %all-gather.10.cloned.1.call-start = ((), (), s32[]{:S(2)}) async-start(), calls=%async_computation.1 | async-start | bytes 6684672 | tf_op jit(solution)/shard_map/all_gather | solution.py:77
  14.7 116.2 %all-gather.20.cloned.1.call-start = ((), (), s32[]{:S(2)}) async-start(), calls=%async_computation.6 | async-start | bytes 4718592 | tf_op jit(solution)/shard_map/all_gather | solution.py:82
  60.7 24.2 %copy-start.2 = (f32[768,1024]{1,0:T(8,128)}, f32[768,1024]{1,0:T(8,128)S(1)}, u32[]{:S(2)}) copy-start(f32[768,1024]{1,0:T(8,128)S(1)} %get-tuple-element.6) | copy-start | bytes 9437188
  87.1 0.8 copy-start.5
  87.1 7.3 %copy-start.3 = (bf16[1,768,1024]{2,1,0:T(8,128)(2,1)S(1)}, bf16[1,768,1024]{2,1,0:T(8,128)(2,1)}, u32[]{:S(2)}) copy-start(bf16[1,768,1024]{2,1,0:T(8,128)(2,1)} %get-tuple-element.9) | copy-start | bytes 4718596
  87.1 100.1 %all-gather.22.cloned.1.call-start = ((), (), s32[]{:S(2)}) async-start(), calls=%async_computation.7 | async-start | bytes 4718592 | tf_op jit(solution)/shard_map/all_gather | solution.py:83
  87.9 131.8 %all-gather.12.cloned.1.call-start = ((), (), s32[]{:S(2)}) async-start(), calls=%async_computation.2 | async-start | bytes 2228224 | tf_op jit(solution)/shard_map/all_gather | solution.py:110
  93.0 179.1 %all-gather.14.cloned.1.call-start = ((), (), s32[]{:S(2)}) async-start(), calls=%async_computation.3 | async-start | bytes 4456448 | tf_op jit(solution)/shard_map/all_gather | solution.py:114
  93.6 219.3 %all-gather.16.cloned.1.call-start = ((), (), s32[]{:S(2)}) async-start(), calls=%async_computation.4 | async-start | bytes 2228224 | tf_op jit(solution)/shard_map/all_gather | solution.py:127
  94.2 275.2 %all-gather.18.cloned.1.call-start = ((), (), s32[]{:S(2)}) async-start(), calls=%async_computation.5 | async-start | bytes 4718592 | tf_op jit(solution)/shard_map/all_gather | solution.py:132
  277.4 8.1 %copy-start.6 = (bf16[5,1024]{1,0:T(8,128)(2,1)S(1)}, bf16[5,1024]{1,0:T(8,128)(2,1)}, u32[]{:S(2)}) copy-start(bf16[5,1024]{1,0:T(8,128)(2,1)} %param.19) | copy-start | bytes 30724
  278.3 1.1 copy-start.4
  279.4 33.5 %collective-permute-start = (bf16[2,1024]{1,0:T(2,128)(2,1)S(1)}, bf16[2,1024]{1,0:T(2,128)(2,1)S(1)}, u32[]{:S(2)}, u32[]{:S(2)}) collective-permute-start(bf16[2,1024]{1,0:T(2,128)(2,1)S(1)} %get-tuple-element.10), channel_id=1, source_target_pairs={{0,1},{2,3},{4,5},{6,7},{8,9},{10,11},{12,13},{14,15},{16,17},{18,... | collective-permute-start | bytes 12296 | tf_op jit(solution)/shard_map/ppermute | solution.py:16
  280.7 32.2 %collective-permute-start.1 = (bf16[2,1024]{1,0:T(2,128)(2,1)S(1)}, bf16[2,1024]{1,0:T(2,128)(2,1)S(1)}, u32[]{:S(2)}, u32[]{:S(2)}) collective-permute-start(bf16[2,1024]{1,0:T(2,128)(2,1)S(1)} %get-tuple-element.11), channel_id=1, source_target_pairs={{1,0},{3,2},{5,4},{7,6},{9,8},{11,10},{13,12},{15,14},{17,16},{19,... | collective-permute-start | bytes 12296 | tf_op jit(solution)/shard_map/ppermute | solution.py:17
  369.3 7.8 %copy-start.1 = (bf16[1,1024,1024]{2,1,0:T(8,128)(2,1)S(1)}, bf16[1,1024,1024]{2,1,0:T(8,128)(2,1)}, u32[]{:S(2)}) copy-start(bf16[1,1024,1024]{2,1,0:T(8,128)(2,1)} %param.14) | copy-start | bytes 6291460
Sparse Core Ops, SparseCore 0:
  14.8 61.6 all-gather.9
  87.3 43.5 all-gather.19
  132.4 44.8 all-gather.21
  179.4 40.2 all-gather.11
  221.7 50.3 all-gather.13
  274.1 38.7 all-gather.15
  324.5 44.7 all-gather.17
where the time goes:
time: 387 us; the launch traced here: 384 us
  waiting for transfers between devices  173 us (45%)
  matrix products  96.7 us (25%)
  blocking collectives  51.4 us (13%)
  other arithmetic  30.6 us (8%)
  between operations  14.4 us (4%)
  local copies, waits for them, and re-layouts  11.4 us (3%)
  starting transfers between devices  6.48 us (2%)
    all_gather x1, waiting for transfers between devices, body(): lax.all_gather(w_expand, 'dp', axis=0, tiled=True)  47 us
    all_gather x1, waiting for transfers between devices, body(): lax.all_gather(final_norm, 'level', axis=0, tiled=True)  44.9 us
    all_to_all x1, blocking collectives, body(): lax.all_to_all(level_terms, 'level', split_axis=0, concat_axis=0, tiled=T...  38.2 us
    all_gather x1, waiting for transfers between devices, body(): key_piece = lax.all_gather(projected[1], 'level', axis=0, tiled=True)  34.9 us
    dot_general x1, matrix products, body(): jnp.einsum('qhd,khd->hqk', queries, key_three, preferred_element_type=jnp...  29 us
    dot_general x1, matrix products, body(): jnp.einsum('hqk,khd->qhd', weights.astype(jnp.bfloat16), value_three, pre...  27.7 us
    all_gather x1, waiting for transfers between devices, body(): lax.all_gather(w_project, 'dp', axis=0, tiled=True)  27.4 us
    reduce_sum x1, other arithmetic, body(): weight_sum = jnp.sum(weights, axis=-1)  24.1 us
  transfers between devices with their start and end apart: 9, of which 6 were waited for; matrix products, arithmetic and copies ran while one was open for 28% of the time, Pallas kernels for 0%

commit v1 on v0

v1 whole, which is shorter than its diff:
```python
import functools

import jax
import jax.numpy as jnp
from jax import lax
from jax.experimental import pallas as pl
from jax.experimental.pallas import tpu as pltpu
from jax.sharding import PartitionSpec as P

HEADS = 16
LOG2E = 1.4426950408889634
BF16 = jnp.bfloat16
F32 = jnp.float32
ANY = pl.BlockSpec(memory_space=pl.ANY)
WIDE = pltpu.CompilerParams(vmem_limit_bytes=60 * 2**20)


def layer_norm(values):
    centered = values - jnp.mean(values, axis=-1, keepdims=True)
    variance = jnp.mean(centered * centered, axis=-1, keepdims=True)
    return centered * lax.rsqrt(variance + 1e-05)


def dot(left, right):
    return jnp.dot(left, right, preferred_element_type=F32)


def dot_t(left, right):
    return lax.dot_general(left, right, (((1,), (1,)), ((), ())), preferred_element_type=F32)


def swap(value, bit):
    devices = lax.axis_size("dp")
    return lax.ppermute(value, "dp", [(i, i ^ bit) for i in range(devices)])


def from_outer(value, back):
    devices = lax.axis_size("dp")
    outer = devices // 4
    return lax.ppermute(
        value, "dp", [(i, ((i // 4 + back) % outer) * 4 + i % 4) for i in range(devices)]
    )


def from_level(value, back):
    groups = lax.axis_size("level")
    return lax.ppermute(value, "level", [(i, (i + back) % groups) for i in range(groups)])


def gather_pieces(shard):
    outer = lax.axis_size("dp") // 4
    near = jnp.stack([shard] + [from_outer(shard, back) for back in range(1, outer)])
    far = swap(near, 2)
    crossed = swap(jnp.stack([near, far]), 1)
    return near, far, crossed


def piece_owner(back, pair, core):
    index, outer = lax.axis_index("dp"), lax.axis_size("dp") // 4
    source = lax.rem(index // 4 + outer - back, outer)
    low = lax.rem(index, 4)
    low = jnp.where(pair, 3 - low, low) if pair == core else jnp.where(pair, lax.rem(low + 2, 4), low + 1 - 2 * lax.rem(low, 2))
    return source * 4 + low


def embed_kernel(
    others, outer, rows_here, scale,
    ids_ref, mask_ref, table_ref, *refs,
):
    halves = refs[: 2 * others]
    near_ref, far_ref, crossed_ref = refs[2 * others : 2 * others + 3]
    embedded_ref, queries_ref, keys_ref, values_ref = refs[2 * others + 3 : 2 * others + 7]
    tables, weights, table_sems, weight_sems = refs[2 * others + 7 :]
    step = pl.program_id(0)
    codes = table_ref.shape[0]
    half = codes // 2
    core = lax.rem(lax.axis_index("dp"), 2)

    table_copies = [pltpu.make_async_copy(table_ref, tables.at[pl.ds(0, codes)], table_sems.at[0])]
    for back in range(others):
        base = (back + 1) * codes
        for side in range(2):
            place = base + (core if side == 0 else 1 - core) * half
            table_copies.append(
                pltpu.make_async_copy(
                    halves[2 * back + side],
                    tables.at[pl.ds(place, half)],
                    table_sems.at[1 + 2 * back + side],
                )
            )
    weight_copies = []
    for back in range(outer):
        for pair in range(2):
            for other_core in range(2):
                row = piece_owner(back, pair, other_core) * rows_here
                source = (
                    crossed_ref.at[pair, back] if other_core else (far_ref if pair else near_ref).at[back]
                )
                weight_copies.append(
                    pltpu.make_async_copy(
                        source,
                        weights.at[:, pl.ds(row, rows_here), :],
                        weight_sems.at[len(weight_copies)],
                    )
                )

    @pl.when(step == 0)
    def _():
        for copy in table_copies + weight_copies:
            copy.start()
        for copy in table_copies:
            copy.wait()

    frames = ids_ref.shape[0]
    code_row = lax.broadcasted_iota(jnp.int32, (frames, codes), 1)
    total = None
    for level in range(others + 1):
        ids = ids_ref[:, level : level + 1]
        onehot = jnp.where(ids == code_row, 1.0, 0.0).astype(BF16)
        term = dot(onehot, tables[level * codes : (level + 1) * codes, :])
        fill = mask_ref[level : level + 1, :].astype(F32)
        term = term + jnp.where(ids < 0, fill, 0.0)
        total = term if total is None else total + term
    embedded_ref[...] = total
    normed = layer_norm(total).astype(BF16)

    @pl.when(step == 0)
    def _():
        for copy in weight_copies:
            copy.wait()

    queries_ref[...] = (dot(normed, weights[0]) * scale).astype(BF16)
    keys_ref[...] = dot(normed, weights[1]).astype(BF16)
    values_ref[...] = dot(normed, weights[2]).astype(BF16)


def embed_and_project(ids, masks, table, halves, pieces, scale):
    frames, levels = ids.shape
    codes, width = table.shape
    near, far, crossed = pieces
    outer, three, rows_here, columns = near.shape
    tile = frames // 6
    others = levels - 1
    row_block = lambda i: (i, 0)
    kernel = functools.partial(embed_kernel, others, outer, rows_here, scale)
    flops = 2 * frames * width * (levels * codes + 3 * columns)
    return pl.pallas_call(
        kernel,
        grid=(frames // tile,),
        in_specs=[
            pl.BlockSpec((tile, levels), row_block),
            pl.BlockSpec(masks.shape, lambda i: (0, 0)),
        ]
        + [ANY] * (4 + 2 * others),
        out_specs=[pl.BlockSpec((tile, width), row_block)]
        + [pl.BlockSpec((tile, columns), row_block)] * 3,
        out_shape=[jax.ShapeDtypeStruct((frames, width), F32)]
        + [jax.ShapeDtypeStruct((frames, columns), BF16)] * 3,
        scratch_shapes=[
            pltpu.VMEM((levels * codes, width), BF16),
            pltpu.VMEM((three, width, columns), BF16),
            pltpu.SemaphoreType.DMA((1 + 2 * others,)),
            pltpu.SemaphoreType.DMA((4 * outer,)),
        ],
        compiler_params=WIDE,
        cost_estimate=pl.CostEstimate(flops=flops, bytes_accessed=20 * 2**20, transcendentals=0),
        name="embed_project",
    )(ids, masks, table, *halves, near, far, crossed)


def attention_kernel(head_dim, queries_ref, keys_ref, values_ref, out_ref):
    queries, keys, values = queries_ref[...], keys_ref[...], values_ref[...]
    lane = lax.broadcasted_iota(jnp.int32, (1, 2 * head_dim), 1)
    first = lane < head_dim
    owns = (first, lane >= head_dim)
    scores = [dot_t(jnp.where(own, queries, jnp.zeros_like(queries)), keys) for own in owns]
    sums = []
    for own, score in zip(owns, scores):
        blocks = [score[:, at : at + 128] for at in range(0, score.shape[1], 128)]
        top = functools.reduce(jnp.maximum, blocks)
        top = jnp.max(top, axis=1, keepdims=True)
        weights = jnp.exp2(score - top).astype(BF16)
        sums.append(dot(weights, jnp.where(own, values, jnp.ones_like(values))))
    mixed = jnp.where(first, sums[0], sums[1])
    total = pltpu.roll(jnp.where(first, sums[1], sums[0]), head_dim, 1)
    out_ref[...] = (mixed / total).astype(BF16)


def attend(queries, keys, values, pair, head_dim):
    frames = queries.shape[0]
    width = 2 * head_dim
    tile = frames // 2
    return pl.pallas_call(
        functools.partial(attention_kernel, head_dim),
        grid=(frames // tile,),
        in_specs=[
            pl.BlockSpec((tile, width), lambda i: (i, pair)),
            pl.BlockSpec((frames, width), lambda i: (0, pair)),
            pl.BlockSpec((frames, width), lambda i: (0, pair)),
        ],
        out_specs=pl.BlockSpec((tile, width), lambda i: (i, 0)),
        out_shape=jax.ShapeDtypeStruct((frames, width), BF16),
        compiler_params=WIDE,
        cost_estimate=pl.CostEstimate(
            flops=16 * frames * frames * width, bytes_accessed=2**21, transcendentals=2 * frames * frames
        ),
        name="attend",
    )(queries, keys, values)


def finish_kernel(
    tiles, parts, width,
    embedded_ref, *refs,
):
    att_refs = refs[:parts]
    packed_ref, depth_ref, head_ref, out_ref = refs[parts : parts + 4]
    attended, residual, gated, packed, head, sems = refs[parts + 4 :]
    step = pl.program_id(0)
    tile = embedded_ref.shape[0]
    taps = depth_ref.shape[0]
    reach = taps // 2
    edge = 8
    copies = [
        pltpu.make_async_copy(packed_ref, packed, sems.at[0]),
        pltpu.make_async_copy(head_ref, head, sems.at[1]),
    ]

    @pl.when(step == 0)
    def _():
        for copy in copies:
            copy.start()
        gated[...] = jnp.zeros_like(gated)
        residual[...] = jnp.zeros_like(residual)
        for copy in copies:
            copy.wait()

    before = gated[edge + tile - edge : edge + tile, :]
    previous = gated[edge + tile :, :]
    gated[0:edge, :] = before
    gated[edge : edge + tile, :] = previous
    last_residual = residual[...]

    piece = att_refs[0].shape[1]
    for part, ref in enumerate(att_refs):
        attended[:, part * piece : (part + 1) * piece] = ref[...]
    after = embedded_ref[...] + dot_t(attended[...], packed[:, :width])
    residual[...] = after
    linear = dot(layer_norm(after).astype(BF16), packed[:, width : 3 * width])
    fresh = (linear[:, :width] * jax.nn.sigmoid(linear[:, width:])).astype(BF16).astype(F32)
    fresh = jnp.where(step < tiles, fresh, 0.0)
    gated[edge + tile :, :] = fresh

    conv = None
    for tap in range(taps):
        start = edge - reach + tap
        term = gated[start : start + tile, :] * depth_ref[tap : tap + 1, :].astype(F32)
        conv = term if conv is None else conv + term
    activated = (conv * jax.nn.sigmoid(conv)).astype(BF16)
    after_conv = last_residual + dot(activated, packed[:, 3 * width :])
    out_ref[...] = dot(layer_norm(after_conv).astype(BF16), head[...]).astype(BF16)


def finish(embedded, attended, packed, w_depth, head):
    frames, width = embedded.shape
    codes = head.shape[1]
    tile = frames // 6
    tiles = frames // tile
    parts = len(attended)
    front = lambda i: (jnp.minimum(i, tiles - 1), 0)
    back = lambda i: (jnp.maximum(i - 1, 0), 0)
    flops = 2 * frames * width * (4 * width + codes)
    return pl.pallas_call(
        functools.partial(finish_kernel, tiles, parts, width),
        grid=(tiles + 1,),
        in_specs=[pl.BlockSpec((tile, width), front)]
        + [pl.BlockSpec((tile, part.shape[1]), front) for part in attended]
        + [ANY, pl.BlockSpec(w_depth.shape, lambda i: (0, 0)), ANY],
        out_specs=pl.BlockSpec((tile, codes), back),
        out_shape=jax.ShapeDtypeStruct((frames, codes), BF16),
        scratch_shapes=[
            pltpu.VMEM((tile, width), BF16),
            pltpu.VMEM((tile, width), F32),
            pltpu.VMEM((8 + 2 * tile, width), F32),
            pltpu.VMEM(packed.shape, BF16),
            pltpu.VMEM(head.shape, BF16),
            pltpu.SemaphoreType.DMA((2,)),
        ],
        compiler_params=WIDE,
        cost_estimate=pl.CostEstimate(flops=flops, bytes_accessed=20 * 2**20, transcendentals=0),
        name="finish",
    )(embedded, *attended, packed, w_depth, head)


def body(
    token_ids,
    decoded_mask,
    levels_done,
    code_tables,
    mask_vectors,
    w_qkv,
    w_out,
    w_expand,
    w_depth,
    w_project,
    level_heads,
):
    groups = lax.axis_size("level")
    level_index = lax.axis_index("level")
    table = code_tables[0]
    codes, width = table.shape
    head_dim = width // HEADS
    half = codes // 2
    core = lax.rem(lax.axis_index("dp"), 2)

    own_out = w_out.T
    columns = own_out.shape[1]
    small = jnp.concatenate([own_out, mask_vectors.reshape(-1, columns)], axis=0)
    smalls = [small] + [from_level(small, back) for back in range(1, groups)]
    rows = own_out.shape[0]
    packed = jnp.concatenate([s[:rows] for s in smalls] + [w_expand, w_project], axis=1)
    packed = lax.all_gather(packed, "dp", axis=0, tiled=True)
    masks = jnp.concatenate([s[rows:].reshape(1, width) for s in smalls], axis=0)

    done = levels_done[0]
    use_token = (level_index < done) | ((level_index == done) & (decoded_mask[0, 0] == 1))
    own_ids = jnp.where(use_token, token_ids[0, 0], -1)
    ids = jnp.stack([own_ids] + [from_level(own_ids, back) for back in range(1, groups)], axis=1)

    mine = lax.dynamic_slice_in_dim(table, core * half, half, 0)
    halves = []
    for back in range(1, groups):
        landed = from_level(mine, back)
        halves += [landed, swap(landed, 1)]
    pieces = gather_pieces(w_qkv)

    scale = head_dim ** (-0.5) * LOG2E
    embedded, queries, keys, values = embed_and_project(ids, masks, table, halves, pieces, scale)

    own_parts, far_parts = [], [[] for _ in range(groups - 1)]
    for pair in range(columns // (2 * head_dim)):
        part = attend(queries, keys, values, pair, head_dim)
        own_parts.append(part)
        for back in range(1, groups):
            far_parts[back - 1].append(from_level(part, back))
    attended = own_parts + [part for parts in far_parts for part in parts]
    logits = finish(embedded, attended, packed, w_depth, level_heads[0])
    return logits[None, None]


def solution(mesh):
    return jax.shard_map(
        body,
        mesh=mesh,
        in_specs=(
            P("dp", "level", None),
            P("dp", "level", None),
            P("dp"),
            P("level", None, None),
            P("level", None),
            P(None, "dp", "level"),
            P("level", "dp"),
            P("dp", None),
            P(),
            P("dp", None),
            P("level", None, None),
        ),
        out_specs=P("dp", "level", None, None),
        check_vma=False,
    )
```

time: 387 us -> 217 us (0.56)
  matrix products: 96.7 us -> 0 us
  Pallas kernels: 0 us -> 87.4 us
  waiting for transfers between devices: 173 us -> 92.8 us
  blocking collectives: 51.4 us -> 0 us
  other arithmetic: 30.6 us -> 5.53 us
  local copies, waits for them, and re-layouts: 11.4 us -> 5.15 us
  starting transfers between devices: 6.48 us -> 11.9 us
    all_gather x7 -> x1, waiting for transfers between devices: 171 us -> 0.01 us  [body(): packed = lax.all_gather(packed, 'dp', axis=0, tiled=True)]
    dot_general x8 -> x0, matrix products: 96.7 us -> none  [the longest x1 29 us: body(): jnp.einsum('qhd,khd->hqk', queries, key_three, preferred_element_type=jnp...]
    ppermute x2 -> x13, waiting for transfers between devices: 0.01 us -> 92.8 us  [the longest x7 38.1 us: from_level(): lax.ppermute(value, 'level', [(i, (i + back) % groups) for i in range(gro...]
    pallas_call x0 -> x6, Pallas kernels: none -> 87.4 us  [the longest x1 36.4 us: finish(): pl.pallas_call(functools.partial(finish_kernel, tiles, parts, width), gri...]
    all_to_all x1 -> x0, blocking collectives: 38.2 us -> none  [body(): lax.all_to_all(level_terms, 'level', split_axis=0, concat_axis=0, tiled=T...]
    reduce_sum x5 -> x0, other arithmetic: 26.1 us -> none  [the longest x1 24.1 us: body(): weight_sum = jnp.sum(weights, axis=-1)]
    all_gather x2 -> x0, blocking collectives: 13.2 us -> none  [the longest x1 8.14 us: body(): full_columns = lax.all_gather(w_qkv, 'level', axis=2, tiled=True)]
    all_gather x2 -> x0, local copies, waits for them, and re-layouts: 6.38 us -> none  [the longest x1 3.2 us: body(): value_piece = lax.all_gather(projected[2], 'level', axis=0, tiled=True)]
  transfers between devices with their start and end apart: 9 -> 14, of which waited for: 6 -> 10; matrix products, arithmetic and copies ran while one was open for 28% -> 2% of each run, Pallas kernels for 0% -> 23%
where the time goes in v1:
time: 217 us
  waiting for transfers between devices  92.8 us (43%)
  Pallas kernels  87.4 us (40%)
  between operations  14.2 us (7%)
  starting transfers between devices  11.9 us (5%)
  other arithmetic  5.53 us (3%)
  local copies, waits for them, and re-layouts  5.15 us (2%)
    ppermute x7, waiting for transfers between devices, from_level(): lax.ppermute(value, 'level', [(i, (i + back) % groups) for i in range(gro...  38.1 us
    pallas_call x1, Pallas kernels, finish(): pl.pallas_call(functools.partial(finish_kernel, tiles, parts, width), gri...  36.4 us
    pallas_call x4, Pallas kernels, attend(): pl.pallas_call(functools.partial(attention_kernel, head_dim), grid=(frame...  29.9 us
    ppermute x3, waiting for transfers between devices, from_outer(): lax.ppermute(value, 'dp', [(i, (i // 4 + back) % outer * 4 + i % 4) for i...  27.9 us
    ppermute x3, waiting for transfers between devices, swap(): return lax.ppermute(value, 'dp', [(i, i ^ bit) for i in range(devices)])  26.8 us
    pallas_call x1, Pallas kernels, embed_and_project(): pl.pallas_call(kernel, grid=(frames // tile,), in_specs=[pl.BlockSpec((ti...  21 us
    ppermute x7, starting transfers between devices, from_level(): lax.ppermute(value, 'level', [(i, (i + back) % groups) for i in range(gro...  6.08 us
    ppermute x3, starting transfers between devices, from_outer(): lax.ppermute(value, 'dp', [(i, (i // 4 + back) % outer * 4 + i % 4) for i...  4.67 us
  transfers between devices with their start and end apart: 14, of which 10 were waited for; matrix products, arithmetic and copies ran while one was open for 2% of the time, Pallas kernels for 23%

profile of v1, /device:TPU:14, one launch (start us, length us, event | category | flops | bytes accessed | tf_op | source)
XLA Modules:
  0.0 216.9 jit_solution(5972689783081577809)
XLA Ops:
  6.5 0.0 copy-start.2
  6.5 0.0 all-gather.2.cloned.1.call-start
  6.5 0.7 reduce.1
  7.3 0.8 pad_maximum_fusion.3
  8.1 0.5 collective-permute-start.1
  8.7 3.8 %collective-permute-done.1 = bf16[66,512]{1,0:T(8,128)(2,1)S(1)} collective-permute-done((bf16[66,512]{1,0:T(8,128)(2,1)S(1)}, bf16[66,512]{1,0:T(8,128)(2,1)S(1)}, u32[]{:S(2)}, u32[]{:S(2)}) %collective-permute-start.1) | collective-permute-done | bytes 67616 | tf_op jit(solution)/shard_map/ppermute | solution.py:47
  12.5 1.8 pad_maximum_fusion.2
  14.3 0.0 all-gather.2.cloned.1.call-update
  14.4 0.0 copy-done.2
  14.4 1.6 collective-permute-start.4
  16.0 1.2 collective-permute-start.5
  17.2 1.8 collective-permute-start.6
  19.1 15.9 %collective-permute-done.4 = bf16[3,64,512]{2,1,0:T(8,128)(2,1)S(1)} collective-permute-done((bf16[3,64,512]{2,1,0:T(8,128)(2,1)S(1)}, bf16[3,64,512]{2,1,0:T(8,128)(2,1)S(1)}, u32[]{:S(2)}, u32[]{:S(2)}) %collective-permute-start.4) | collective-permute-done | bytes 196640 | tf_op jit(solution)/shard_map/ppermute | solution.py:40
  34.9 11.1 %collective-permute-done.5 = bf16[3,64,512]{2,1,0:T(8,128)(2,1)S(1)} collective-permute-done((bf16[3,64,512]{2,1,0:T(8,128)(2,1)S(1)}, bf16[3,64,512]{2,1,0:T(8,128)(2,1)S(1)}, u32[]{:S(2)}, u32[]{:S(2)}) %collective-permute-start.5) | collective-permute-done | bytes 196640 | tf_op jit(solution)/shard_map/ppermute | solution.py:40
  46.1 0.9 collective-permute-done.6
  47.0 0.1 fusion
  47.1 0.0 copy-start
  47.1 0.5 collective-permute-start.7
  47.6 1.3 dynamic-slice_bitcast_fusion
  48.9 0.9 collective-permute-start.2
  49.9 26.8 %collective-permute-done.7.refs_3_ = bf16[4,3,64,512]{3,2,1,0:T(8,128)(2,1)S(1)} collective-permute-done((bf16[4,3,64,512]{3,2,1,0:T(8,128)(2,1)S(1)}, bf16[4,3,64,512]{3,2,1,0:T(8,128)(2,1)S(1)}, u32[]{:S(2)}, u32[]{:S(2)}) %collective-permute-start.7) | collective-permute-done | bytes 786464 | tf_op jit(solution)/shard_map/ppermute | solution.py:34
  76.7 0.0 copy-start.1
  76.7 0.9 copy-done.1
  77.6 0.0 copy-start.4
  77.6 0.0 copy-start.5
  77.6 1.3 pad_maximum_fusion
  78.9 0.0 copy-done
  78.9 0.1 collective-permute-start.8
  79.0 0.0 collective-permute-done.2.refs_0_
  79.0 0.5 collective-permute-start.3
  80.1 0.0 copy-done.4
  80.2 0.0 copy-done.5
  80.2 0.6 collective-permute-start
  80.8 3.2 %collective-permute-done = s32[1536]{0:T(1024)S(1)} collective-permute-done((s32[1536]{0:T(1024)S(1)}, s32[1536]{0:T(1024)S(1)}, u32[]{:S(2)}, u32[]{:S(2)}) %collective-permute-start) | collective-permute-done | bytes 6176 | tf_op jit(solution)/shard_map/ppermute | solution.py:47
  83.9 1.2 copy.14.ids_ref
  85.2 0.0 copy-done.3
  85.2 0.6 pad_maximum_fusion.4.mask_ref
  85.8 0.0 collective-permute-done.3.refs_1_
  85.8 0.0 copy-start.6
  85.8 0.0 collective-permute-done.8.refs_4_
  85.8 1.0 copy-done.6
  86.7 21.0 %embed_project.1 = (f32[1536,1024]{1,0:T(8,128)}, bf16[1536,512]{1,0:T(8,128)(2,1)}, bf16[1536,512]{1,0:T(8,128)(2,1)}, bf16[1536,512]{1,0:T(8,128)(2,1)}) custom-call(s32[1536,2]{1,0:T(8,128)} %copy.14.ids_ref, bf16[2,1024]{1,0:T(2,128)(2,1)} %pad_maximum_fusion.4.mask_ref, bf16[1024,1024]{1,0:T(8,128)(2,1)} %bitcast.22, ...), custom_call_target="tpu_custom_call" | custom-call | flops 11274289152 | bytes 20971520 | tf_op jit(solution)/shard_map/embed_project/pallas_call | solution.py:147
  107.8 7.4 %attend.7.refs_3_ = bf16[1536,128]{1,0:T(8,128)(2,1)} custom-call(bf16[1536,512]{1,0:T(8,128)(2,1)} %get-tuple-element.10.queries_ref, bf16[1536,512]{1,0:T(8,128)(2,1)} %get-tuple-element.11.keys_ref, bf16[1536,512]{1,0:T(8,128)(2,1)} %get-tuple-element.12.values_ref), custom_call_target="tpu_custom_call" | custom-call | flops 4831838208 | bytes 2097152 | tf_op jit(solution)/shard_map/attend/pallas_call | solution.py:193
  115.2 7.4 %attend.6.refs_2_ = bf16[1536,128]{1,0:T(8,128)(2,1)} custom-call(bf16[1536,512]{1,0:T(8,128)(2,1)} %get-tuple-element.10.queries_ref, bf16[1536,512]{1,0:T(8,128)(2,1)} %get-tuple-element.11.keys_ref, bf16[1536,512]{1,0:T(8,128)(2,1)} %get-tuple-element.12.values_ref), custom_call_target="tpu_custom_call" | custom-call | flops 4831838208 | bytes 2097152 | tf_op jit(solution)/shard_map/attend/pallas_call | solution.py:193
  122.6 7.4 %attend.5.refs_1_ = bf16[1536,128]{1,0:T(8,128)(2,1)} custom-call(bf16[1536,512]{1,0:T(8,128)(2,1)} %get-tuple-element.10.queries_ref, bf16[1536,512]{1,0:T(8,128)(2,1)} %get-tuple-element.11.keys_ref, bf16[1536,512]{1,0:T(8,128)(2,1)} %get-tuple-element.12.values_ref), custom_call_target="tpu_custom_call" | custom-call | flops 4831838208 | bytes 2097152 | tf_op jit(solution)/shard_map/attend/pallas_call | solution.py:193
  130.0 0.0 copy-start.7
  130.0 0.0 copy-start.8
  130.0 7.7 %attend.4.refs_0_ = bf16[1536,128]{1,0:T(8,128)(2,1)} custom-call(bf16[1536,512]{1,0:T(8,128)(2,1)} %get-tuple-element.10.queries_ref, bf16[1536,512]{1,0:T(8,128)(2,1)} %get-tuple-element.11.keys_ref, bf16[1536,512]{1,0:T(8,128)(2,1)} %get-tuple-element.12.values_ref), custom_call_target="tpu_custom_call" | custom-call | flops 4831838208 | bytes 2097152 | tf_op jit(solution)/shard_map/attend/pallas_call | solution.py:193
  137.7 0.0 copy-done.7
  137.7 0.5 collective-permute-start.12
  138.2 0.0 copy-done.8
  138.2 1.6 collective-permute-start.11
  139.7 0.0 copy-done.9
  139.7 0.5 collective-permute-start.10
  140.2 1.6 collective-permute-start.9
  141.8 7.9 %collective-permute-done.12.refs_7_ = bf16[1536,128]{1,0:T(8,128)(2,1)S(1)} collective-permute-done((bf16[1536,128]{1,0:T(8,128)(2,1)S(1)}, bf16[1536,128]{1,0:T(8,128)(2,1)S(1)}, u32[]{:S(2)}, u32[]{:S(2)}) %collective-permute-start.12) | collective-permute-done | bytes 393248 | tf_op jit(solution)/shard_map/ppermute | solution.py:47
  149.7 8.4 %collective-permute-done.11.refs_6_ = bf16[1536,128]{1,0:T(8,128)(2,1)S(1)} collective-permute-done((bf16[1536,128]{1,0:T(8,128)(2,1)S(1)}, bf16[1536,128]{1,0:T(8,128)(2,1)S(1)}, u32[]{:S(2)}, u32[]{:S(2)}) %collective-permute-start.11) | collective-permute-done | bytes 393248 | tf_op jit(solution)/shard_map/ppermute | solution.py:47
  158.1 8.4 %collective-permute-done.10.refs_5_ = bf16[1536,128]{1,0:T(8,128)(2,1)S(1)} collective-permute-done((bf16[1536,128]{1,0:T(8,128)(2,1)S(1)}, bf16[1536,128]{1,0:T(8,128)(2,1)S(1)}, u32[]{:S(2)}, u32[]{:S(2)}) %collective-permute-start.10) | collective-permute-done | bytes 393248 | tf_op jit(solution)/shard_map/ppermute | solution.py:47
  166.6 6.3 %collective-permute-done.9.refs_4_ = bf16[1536,128]{1,0:T(8,128)(2,1)S(1)} collective-permute-done((bf16[1536,128]{1,0:T(8,128)(2,1)}, bf16[1536,128]{1,0:T(8,128)(2,1)S(1)}, u32[]{:S(2)}, u32[]{:S(2)}) %collective-permute-start.9) | collective-permute-done | bytes 393248 | tf_op jit(solution)/shard_map/ppermute | solution.py:47
  172.9 0.0 copy-done.10
  172.9 0.0 copy-done.11
  172.9 0.0 copy-done.12
  172.9 0.7 copy-done.13
  173.7 36.4 %finish.1 = bf16[1536,1024]{1,0:T(8,128)(2,1)} custom-call(f32[1536,1024]{1,0:T(8,128)} %get-tuple-element.9.embedded_ref, bf16[1536,128]{1,0:T(8,128)(2,1)} %attend.4.refs_0_, bf16[1536,128]{1,0:T(8,128)(2,1)} %attend.5.refs_1_, bf16[1536,128]{1,0:T(8,128)(2,1)} %attend.6.refs_2_, bf16[1536,128]{1,0:T(8,128)(2,1)} %attend.7.refs_3_, ...), custom_call_target="tpu_custom_call" | custom-call | flops 16106127360 | bytes 20971520 | tf_op jit(solution)/shard_map/finish/pallas_call | solution.py:272
  (14 shorter events, 0.1 us)
Async XLA Ops:
  6.5 7.8 %copy-start.2 = (bf16[3,64,512]{2,1,0:T(8,128)(2,1)S(1)}, bf16[3,64,512]{2,1,0:T(8,128)(2,1)}, u32[]{:S(2)}) copy-start(bf16[3,64,512]{2,1,0:T(8,128)(2,1)} %param.16) | copy-start | bytes 589828
  6.5 166.4 %all-gather.2.cloned.1.call-start = ((), (), s32[]{:S(2)}) async-start(), calls=%async_computation | async-start | bytes 8912896 | tf_op jit(solution)/shard_map/all_gather | solution.py:321
  8.1 4.4 %collective-permute-start.1 = (bf16[66,512]{1,0:T(8,128)(2,1)S(1)}, bf16[66,512]{1,0:T(8,128)(2,1)S(1)}, u32[]{:S(2)}, u32[]{:S(2)}) collective-permute-start(bf16[66,512]{1,0:T(8,128)(2,1)S(1)} %pad_maximum_fusion.3), channel_id=1, source_target_pairs={{0,1},{1,0},{2,3},{3,2},{4,5},{5,4},{6,7},{7,6},{8,9},{9,8},{10,11... | collective-permute-start | bytes 202760 | tf_op jit(solution)/shard_map/ppermute | solution.py:47
  14.4 20.5 %collective-permute-start.4 = (bf16[3,64,512]{2,1,0:T(8,128)(2,1)S(1)}, bf16[3,64,512]{2,1,0:T(8,128)(2,1)S(1)}, u32[]{:S(2)}, u32[]{:S(2)}) collective-permute-start(bf16[3,64,512]{2,1,0:T(8,128)(2,1)S(1)} %copy-done.2), channel_id=1, source_target_pairs={{0,8},{2,10},{4,12},{6,14},{8,16},{10,18},{12,20},{14,22},{16,24},... | collective-permute-start | bytes 589832 | tf_op jit(solution)/shard_map/ppermute | solution.py:40
  16.0 30.0 %collective-permute-start.5 = (bf16[3,64,512]{2,1,0:T(8,128)(2,1)S(1)}, bf16[3,64,512]{2,1,0:T(8,128)(2,1)S(1)}, u32[]{:S(2)}, u32[]{:S(2)}) collective-permute-start(bf16[3,64,512]{2,1,0:T(8,128)(2,1)S(1)} %copy-done.2), channel_id=1, source_target_pairs={{0,16},{2,18},{4,20},{6,22},{8,24},{10,26},{12,28},{14,30},{16,0},... | collective-permute-start | bytes 589832 | tf_op jit(solution)/shard_map/ppermute | solution.py:40
  17.2 29.7 %collective-permute-start.6 = (bf16[3,64,512]{2,1,0:T(8,128)(2,1)S(1)}, bf16[3,64,512]{2,1,0:T(8,128)(2,1)S(1)}, u32[]{:S(2)}, u32[]{:S(2)}) collective-permute-start(bf16[3,64,512]{2,1,0:T(8,128)(2,1)S(1)} %copy-done.2), channel_id=1, source_target_pairs={{0,24},{2,26},{4,28},{6,30},{8,0},{10,2},{12,4},{14,6},{16,8},{18,... | collective-permute-start | bytes 589832 | tf_op jit(solution)/shard_map/ppermute | solution.py:40
  47.1 31.8 %copy-start = (bf16[4,3,64,512]{3,2,1,0:T(8,128)(2,1)}, bf16[4,3,64,512]{3,2,1,0:T(8,128)(2,1)S(1)}, u32[]{:S(2)}) copy-start(bf16[4,3,64,512]{3,2,1,0:T(8,128)(2,1)S(1)} %get-tuple-element.16.refs_2_) | copy-start | bytes 2359300
  47.1 29.6 %collective-permute-start.7 = (bf16[4,3,64,512]{3,2,1,0:T(8,128)(2,1)S(1)}, bf16[4,3,64,512]{3,2,1,0:T(8,128)(2,1)S(1)}, u32[]{:S(2)}, u32[]{:S(2)}) collective-permute-start(bf16[4,3,64,512]{3,2,1,0:T(8,128)(2,1)S(1)} %get-tuple-element.16.refs_2_), channel_id=1, source_target_pairs={{0,4},{2,6},{4,0},{6,2},{8,12},{10,14},{12,8},{14,10},{16,20},{18,... | collective-permute-start | bytes 2359304 | tf_op jit(solution)/shard_map/ppermute | solution.py:34
  48.9 30.1 %collective-permute-start.2 = (bf16[512,1024]{1,0:T(8,128)(2,1)S(1)}, bf16[512,1024]{1,0:T(8,128)(2,1)}, u32[]{:S(2)}, u32[]{:S(2)}) collective-permute-start(bf16[512,1024]{1,0:T(8,128)(2,1)S(1)} %dynamic-slice_bitcast_fusion), channel_id=1, source_target_pairs={{0,1},{1,0},{2,3},{3,2},{4,5},{5,4},{6,7},{7,6},{8,9},{9,8},{10,11... | collective-permute-start | bytes 3145736 | tf_op jit(solution)/shard_map/ppermute | solution.py:47
  76.7 0.9 copy-start.1
  77.6 2.6 %copy-start.4 = (s32[1,1,1536]{2,1,0:T(1,128)S(1)}, s32[1,1,1536]{2,1,0:T(1,128)}, u32[]{:S(2)}) copy-start(s32[1,1,1536]{2,1,0:T(1,128)} %param.11) | copy-start | bytes 18436
  77.6 2.6 %copy-start.5 = (s32[1,1,1536]{2,1,0:T(1,128)S(1)}, s32[1,1,1536]{2,1,0:T(1,128)}, u32[]{:S(2)}) copy-start(s32[1,1,1536]{2,1,0:T(1,128)} %param.12) | copy-start | bytes 18436
  77.6 7.6 %copy-start.3 = (bf16[1,1024]{1,0:T(2,128)(2,1)S(1)}, bf16[1,1024]{1,0:T(2,128)(2,1)}, u32[]{:S(2)}) copy-start(bf16[1,1024]{1,0:T(2,128)(2,1)} %param.15) | copy-start | bytes 6148
  78.9 6.9 %collective-permute-start.8 = (bf16[2,4,3,64,512]{4,3,2,1,0:T(8,128)(2,1)S(1)}, bf16[2,4,3,64,512]{4,3,2,1,0:T(8,128)(2,1)}, u32[]{:S(2)}, u32[]{:S(2)}) collective-permute-start(bf16[2,4,3,64,512]{4,3,2,1,0:T(8,128)(2,1)S(1)} %pad_maximum_fusion), channel_id=1, source_target_pairs={{0,2},{2,0},{4,6},{6,4},{8,10},{10,8},{12,14},{14,12},{16,18},{18,... | collective-permute-start | bytes 4718600 | tf_op jit(solution)/shard_map/ppermute | solution.py:34
  79.0 6.8 %collective-permute-start.3 = (bf16[512,1024]{1,0:T(8,128)(2,1)}, bf16[512,1024]{1,0:T(8,128)(2,1)S(1)}, u32[]{:S(2)}, u32[]{:S(2)}) collective-permute-start(bf16[512,1024]{1,0:T(8,128)(2,1)} %collective-permute-done.2.refs_0_), channel_id=1, source_target_pairs={{0,2},{2,0},{4,6},{6,4},{8,10},{10,8},{12,14},{14,12},{16,18},{18,... | collective-permute-start | bytes 3145736 | tf_op jit(solution)/shard_map/ppermute | solution.py:34
  80.2 3.7 %collective-permute-start = (s32[1536]{0:T(1024)S(1)}, s32[1536]{0:T(1024)S(1)}, u32[]{:S(2)}, u32[]{:S(2)}) collective-permute-start(s32[1536]{0:T(1024)S(1)} %get-tuple-element.13), channel_id=1, source_target_pairs={{0,1},{1,0},{2,3},{3,2},{4,5},{5,4},{6,7},{7,6},{8,9},{9,8},{10,11... | collective-permute-start | bytes 18440 | tf_op jit(solution)/shard_map/ppermute | solution.py:47
  85.8 1.0 copy-start.6
  130.0 7.7 %copy-start.7 = (bf16[1536,128]{1,0:T(8,128)(2,1)S(1)}, bf16[1536,128]{1,0:T(8,128)(2,1)}, u32[]{:S(2)}) copy-start(bf16[1536,128]{1,0:T(8,128)(2,1)} %attend.7.refs_3_) | copy-start | bytes 1179652
  130.0 8.1 %copy-start.8 = (bf16[1536,128]{1,0:T(8,128)(2,1)S(1)}, bf16[1536,128]{1,0:T(8,128)(2,1)}, u32[]{:S(2)}) copy-start(bf16[1536,128]{1,0:T(8,128)(2,1)} %attend.6.refs_2_) | copy-start | bytes 1179652
  130.0 9.7 %copy-start.9 = (bf16[1536,128]{1,0:T(8,128)(2,1)S(1)}, bf16[1536,128]{1,0:T(8,128)(2,1)}, u32[]{:S(2)}) copy-start(bf16[1536,128]{1,0:T(8,128)(2,1)} %attend.5.refs_1_) | copy-start | bytes 1179652
  137.7 12.0 %collective-permute-start.12 = (bf16[1536,128]{1,0:T(8,128)(2,1)S(1)}, bf16[1536,128]{1,0:T(8,128)(2,1)S(1)}, u32[]{:S(2)}, u32[]{:S(2)}) collective-permute-start(bf16[1536,128]{1,0:T(8,128)(2,1)S(1)} %copy-done.7), channel_id=1, source_target_pairs={{0,1},{1,0},{2,3},{3,2},{4,5},{5,4},{6,7},{7,6},{8,9},{9,8},{10,11... | collective-permute-start | bytes 1179656 | tf_op jit(solution)/shard_map/ppermute | solution.py:47
  138.2 20.0 %collective-permute-start.11 = (bf16[1536,128]{1,0:T(8,128)(2,1)S(1)}, bf16[1536,128]{1,0:T(8,128)(2,1)S(1)}, u32[]{:S(2)}, u32[]{:S(2)}) collective-permute-start(bf16[1536,128]{1,0:T(8,128)(2,1)S(1)} %copy-done.8), channel_id=1, source_target_pairs={{0,1},{1,0},{2,3},{3,2},{4,5},{5,4},{6,7},{7,6},{8,9},{9,8},{10,11... | collective-permute-start | bytes 1179656 | tf_op jit(solution)/shard_map/ppermute | solution.py:47
  139.7 26.8 %collective-permute-start.10 = (bf16[1536,128]{1,0:T(8,128)(2,1)S(1)}, bf16[1536,128]{1,0:T(8,128)(2,1)S(1)}, u32[]{:S(2)}, u32[]{:S(2)}) collective-permute-start(bf16[1536,128]{1,0:T(8,128)(2,1)S(1)} %copy-done.9), channel_id=1, source_target_pairs={{0,1},{1,0},{2,3},{3,2},{4,5},{5,4},{6,7},{7,6},{8,9},{9,8},{10,11... | collective-permute-start | bytes 1179656 | tf_op jit(solution)/shard_map/ppermute | solution.py:47
  140.2 32.7 %collective-permute-start.9 = (bf16[1536,128]{1,0:T(8,128)(2,1)}, bf16[1536,128]{1,0:T(8,128)(2,1)S(1)}, u32[]{:S(2)}, u32[]{:S(2)}) collective-permute-start(bf16[1536,128]{1,0:T(8,128)(2,1)} %attend.4.refs_0_), channel_id=1, source_target_pairs={{0,1},{1,0},{2,3},{3,2},{4,5},{5,4},{6,7},{7,6},{8,9},{9,8},{10,11... | collective-permute-start | bytes 1179656 | tf_op jit(solution)/shard_map/ppermute | solution.py:47
  149.7 23.2 %copy-start.10 = (bf16[1536,128]{1,0:T(8,128)(2,1)}, bf16[1536,128]{1,0:T(8,128)(2,1)S(1)}, u32[]{:S(2)}) copy-start(bf16[1536,128]{1,0:T(8,128)(2,1)S(1)} %collective-permute-done.12.refs_7_) | copy-start | bytes 1179652
  158.1 14.8 %copy-start.11 = (bf16[1536,128]{1,0:T(8,128)(2,1)}, bf16[1536,128]{1,0:T(8,128)(2,1)S(1)}, u32[]{:S(2)}) copy-start(bf16[1536,128]{1,0:T(8,128)(2,1)S(1)} %collective-permute-done.11.refs_6_) | copy-start | bytes 1179652
  166.6 6.4 %copy-start.12 = (bf16[1536,128]{1,0:T(8,128)(2,1)}, bf16[1536,128]{1,0:T(8,128)(2,1)S(1)}, u32[]{:S(2)}) copy-start(bf16[1536,128]{1,0:T(8,128)(2,1)S(1)} %collective-permute-done.10.refs_5_) | copy-start | bytes 1179652
  172.9 0.8 copy-start.13
Sparse Core Ops, SparseCore 0:
  14.5 85.6 all-gather.1

commit v2 on v1

v2 whole, which is shorter than its diff:
```python
import functools

import jax
import jax.numpy as jnp
from jax import lax
from jax.experimental import pallas as pl
from jax.experimental.pallas import tpu as pltpu
from jax.sharding import PartitionSpec as P


HEADS = 16
LOG2E = 1.4426950408889634
BF16 = jnp.bfloat16
F32 = jnp.float32
ANY = pl.BlockSpec(memory_space=pl.ANY)
QUARTERS = 4
CHUNKS = 2
WIDE = pltpu.CompilerParams(vmem_limit_bytes=60 * 2**20)


def layer_norm(values):
    centered = values - jnp.mean(values, axis=-1, keepdims=True)
    variance = jnp.mean(centered * centered, axis=-1, keepdims=True)
    return centered * lax.rsqrt(variance + 1e-05)


def dot(left, right):
    return jnp.dot(left, right, preferred_element_type=F32)


def dot_t(left, right):
    return lax.dot_general(left, right, (((1,), (1,)), ((), ())), preferred_element_type=F32)


def swap(value, bit):
    devices = lax.axis_size("dp")
    return lax.ppermute(value, "dp", [(i, i ^ bit) for i in range(devices)])


def from_outer(value, back):
    devices = lax.axis_size("dp")
    outer = devices // 4
    return lax.ppermute(
        value, "dp", [(i, ((i // 4 + back) % outer) * 4 + i % 4) for i in range(devices)]
    )


def from_level(value, back):
    groups = lax.axis_size("level")
    return lax.ppermute(value, "level", [(i, (i + back) % groups) for i in range(groups)])


def gather_pieces(shard):
    outer = lax.axis_size("dp") // 4
    near = jnp.stack([shard] + [from_outer(shard, back) for back in range(1, outer)])
    far = swap(near, 2)
    crossed = swap(jnp.stack([near, far]), 1)
    return near, far, crossed


def piece_owner(back, pair, core):
    index, outer = lax.axis_index("dp"), lax.axis_size("dp") // 4
    source = lax.rem(index // 4 + outer - back, outer)
    own_pair, own_core = lax.rem(index // 2, 2), lax.rem(index, 2)
    return source * 4 + (1 - own_pair if pair else own_pair) * 2 + (1 - own_core if core else own_core)


def own_term_kernel(ids_ref, mask_ref, table_ref, out_ref):
    code_row = lax.broadcasted_iota(jnp.int32, (1, table_ref.shape[0]), 1)
    ids = ids_ref[:, :1]
    onehot = jnp.where(ids == code_row, 1.0, 0.0).astype(BF16)
    fill = jnp.where(ids < 0, mask_ref[...].astype(F32), 0.0)
    out_ref[...] = (dot(onehot, table_ref[...]) + fill).astype(BF16)


def own_term(ids, mask, table, tile):
    frames = ids.shape[0]
    codes, width = table.shape
    row_block = lambda i: (i, 0)
    return pl.pallas_call(
        own_term_kernel,
        grid=(frames // tile,),
        in_specs=[
            pl.BlockSpec((tile, 1), row_block),
            pl.BlockSpec((1, width), lambda i: (0, 0)),
            pl.BlockSpec((codes, width), lambda i: (0, 0)),
        ],
        out_specs=pl.BlockSpec((tile, width), row_block),
        out_shape=jax.ShapeDtypeStruct((frames, width), BF16),
        compiler_params=WIDE,
        cost_estimate=pl.CostEstimate(
            flops=2 * frames * codes * width, bytes_accessed=2**22, transcendentals=0
        ),
        name="own_term",
    )(ids, mask, table)


def embed_kernel(others, ids_ref, mask_ref, own_ref, *refs):
    halves = refs[: 2 * others]
    embedded_ref, normed_ref, tables, sems = refs[2 * others :]
    step = pl.program_id(0)
    half = halves[0].shape[0]
    codes = 2 * half
    core = lax.rem(lax.axis_index("dp"), 2)
    copies = []
    for index, source in enumerate(halves):
        base, side = (index // 2) * codes, index % 2
        place = base + (core if side == 0 else 1 - core) * half
        copies.append(
            pltpu.make_async_copy(source, tables.at[pl.ds(place, half)], sems.at[index])
        )

    @pl.when(step == 0)
    def _():
        for copy in copies:
            copy.start()
        for copy in copies:
            copy.wait()

    code_row = lax.broadcasted_iota(jnp.int32, (1, codes), 1)
    part = ids_ref.shape[0] // 2
    totals = []
    for sub in range(2):
        rows = slice(sub * part, (sub + 1) * part)
        total = own_ref[rows, :].astype(F32)
        for level in range(others):
            ids = ids_ref[rows, level : level + 1]
            onehot = jnp.where(ids == code_row, 1.0, 0.0).astype(BF16)
            total = total + dot(onehot, tables[level * codes : (level + 1) * codes, :])
            fill = mask_ref[level : level + 1, :].astype(F32)
            total = total + jnp.where(ids < 0, fill, 0.0)
        totals.append(total)
    for sub in range(2):
        rows = slice(sub * part, (sub + 1) * part)
        embedded_ref[rows, :] = totals[sub]
        normed_ref[rows, :] = layer_norm(totals[sub]).astype(BF16)


def embed(ids, masks, own, halves, tile):
    frames, others = ids.shape
    half, width = halves[0].shape
    row_block = lambda i: (i, 0)
    return pl.pallas_call(
        functools.partial(embed_kernel, others),
        grid=(frames // tile,),
        in_specs=[
            pl.BlockSpec((tile, others), row_block),
            pl.BlockSpec(masks.shape, lambda i: (0, 0)),
            pl.BlockSpec((tile, width), row_block),
        ]
        + [ANY] * (2 * others),
        out_specs=[pl.BlockSpec((tile, width), row_block)] * 2,
        out_shape=[
            jax.ShapeDtypeStruct((frames, width), F32),
            jax.ShapeDtypeStruct((frames, width), BF16),
        ],
        scratch_shapes=[
            pltpu.VMEM((2 * others * half, width), BF16),
            pltpu.SemaphoreType.DMA((2 * others,)),
        ],
        compiler_params=WIDE,
        cost_estimate=pl.CostEstimate(
            flops=4 * others * frames * half * width, bytes_accessed=12 * 2**20, transcendentals=0
        ),
        name="embed",
    )(ids, masks, own, *halves)


def project_kernel(chunks, outer, scale, normed_ref, *refs):
    pieces = refs[: 3 * chunks]
    queries_ref, keys_ref, values_ref, weights, sems = refs[3 * chunks :]
    rows_here, columns = pieces[0].shape[2:]
    copies = []
    for chunk in range(chunks):
        near_ref, far_ref, crossed_ref = pieces[3 * chunk : 3 * chunk + 3]
        for back in range(outer):
            for pair in range(2):
                for core in range(2):
                    row = piece_owner(back, pair, core) * rows_here
                    source = crossed_ref.at[pair, back] if core else (far_ref if pair else near_ref).at[back]
                    target = weights.at[chunk, :, pl.ds(row, rows_here), :]
                    copies.append(pltpu.make_async_copy(source, target, sems.at[len(copies)]))

    @pl.when(pl.program_id(0) == 0)
    def _():
        for copy in copies:
            copy.start()
        for copy in copies:
            copy.wait()

    normed = normed_ref[...]
    for chunk in range(chunks):
        at = slice(chunk * columns, (chunk + 1) * columns)
        queries_ref[:, at] = (dot(normed, weights[chunk, 0]) * scale).astype(BF16)
        keys_ref[:, at] = dot(normed, weights[chunk, 1]).astype(BF16)
        values_ref[:, at] = dot(normed, weights[chunk, 2]).astype(BF16)


def project(normed, pieces, scale, tile):
    frames, width = normed.shape
    chunks = len(pieces)
    outer, three, _, columns = pieces[0][0].shape
    row_block = lambda i: (i, 0)
    return pl.pallas_call(
        functools.partial(project_kernel, chunks, outer, scale),
        grid=(frames // tile,),
        in_specs=[pl.BlockSpec((tile, width), row_block)] + [ANY] * (3 * chunks),
        out_specs=[pl.BlockSpec((tile, chunks * columns), row_block)] * 3,
        out_shape=[jax.ShapeDtypeStruct((frames, chunks * columns), BF16)] * 3,
        scratch_shapes=[
            pltpu.VMEM((chunks, three, width, columns), BF16),
            pltpu.SemaphoreType.DMA((4 * outer * chunks,)),
        ],
        compiler_params=WIDE,
        cost_estimate=pl.CostEstimate(
            flops=2 * frames * width * three * columns * chunks, bytes_accessed=12 * 2**20, transcendentals=0
        ),
        name="project",
    )(normed, *[piece for chunk in pieces for piece in chunk])


def attention_kernel(head_dim, queries_ref, keys_ref, values_ref, out_ref):
    queries, keys, values = queries_ref[...], keys_ref[...], values_ref[...]
    lane = lax.broadcasted_iota(jnp.int32, (1, 2 * head_dim), 1)
    first = lane < head_dim
    owns = (first, lane >= head_dim)
    scores = [dot_t(jnp.where(own, queries, jnp.zeros_like(queries)), keys) for own in owns]
    sums = []
    for own, score in zip(owns, scores):
        blocks = [score[:, at : at + 128] for at in range(0, score.shape[1], 128)]
        top = functools.reduce(jnp.maximum, blocks)
        top = jnp.max(top, axis=1, keepdims=True)
        weights = jnp.exp2(score - top).astype(BF16)
        sums.append(dot(weights, jnp.where(own, values, jnp.ones_like(values))))
    mixed = jnp.where(first, sums[0], sums[1])
    total = pltpu.roll(jnp.where(first, sums[1], sums[0]), head_dim, 1)
    out_ref[...] = (mixed / total).astype(BF16)


def attend(queries, keys, values, quarter, tile, head_dim):
    frames, columns = queries.shape
    width = 2 * head_dim
    return pl.pallas_call(
        functools.partial(attention_kernel, head_dim),
        grid=(columns // width,),
        in_specs=[
            pl.BlockSpec((tile, width), lambda p: (quarter, p)),
            pl.BlockSpec((frames, width), lambda p: (0, p)),
            pl.BlockSpec((frames, width), lambda p: (0, p)),
        ],
        out_specs=pl.BlockSpec((tile, width), lambda p: (0, p)),
        out_shape=jax.ShapeDtypeStruct((tile, columns), BF16),
        compiler_params=WIDE,
        cost_estimate=pl.CostEstimate(
            flops=16 * tile * frames * columns, bytes_accessed=2**22, transcendentals=0
        ),
        name="attend",
    )(queries, keys, values)


def gate_kernel(quarters, groups, width, embedded_ref, *refs):
    att_refs = refs[: quarters * groups]
    packed_ref, after_ref, gated_ref, attended, packed, sems = refs[quarters * groups :]
    step = pl.program_id(0)
    copies = [
        pltpu.make_async_copy(packed_ref.at[:, pl.ds(0, width)], packed.at[:, pl.ds(0, width)], sems.at[0]),
        pltpu.make_async_copy(
            packed_ref.at[:, pl.ds(width, 2 * width)], packed.at[:, pl.ds(width, 2 * width)], sems.at[1]
        ),
    ]

    @pl.when(step == 0)
    def _():
        for copy in copies:
            copy.start()

    piece = att_refs[0].shape[1]
    for quarter in range(quarters):

        @pl.when(step == quarter)
        def _():
            for group in range(groups):
                attended[:, group * piece : (group + 1) * piece] = att_refs[quarter * groups + group][...]

    @pl.when(step == 0)
    def _():
        for copy in copies:
            copy.wait()

    part = embedded_ref.shape[0] // 2
    rows = [slice(sub * part, (sub + 1) * part) for sub in range(2)]
    afters = [embedded_ref[r, :] + dot_t(attended[r, :], packed[:, :width]) for r in rows]
    linears = []
    for r, after in zip(rows, afters):
        after_ref[r, :] = after
        linears.append(dot(layer_norm(after).astype(BF16), packed[:, width:]))
    for r, linear in zip(rows, linears):
        gated_ref[r, :] = (linear[:, :width] * jax.nn.sigmoid(linear[:, width:])).astype(BF16)


def gate(embedded, attended, packed, first, tile):
    width = embedded.shape[1]
    quarters, groups = len(attended), len(attended[0])
    flat = [part for parts in attended for part in parts]
    rows = quarters * tile
    return pl.pallas_call(
        functools.partial(gate_kernel, quarters, groups, width),
        grid=(quarters,),
        in_specs=[pl.BlockSpec((tile, width), lambda i: (first + i, 0))]
        + [pl.BlockSpec(part.shape, lambda i: (0, 0)) for part in flat]
        + [ANY],
        out_specs=[pl.BlockSpec((tile, width), lambda i: (i, 0))] * 2,
        out_shape=[
            jax.ShapeDtypeStruct((rows, width), F32),
            jax.ShapeDtypeStruct((rows, width), BF16),
        ],
        scratch_shapes=[
            pltpu.VMEM((tile, width), BF16),
            pltpu.VMEM((width, 3 * width), BF16),
            pltpu.SemaphoreType.DMA((2,)),
        ],
        compiler_params=WIDE,
        cost_estimate=pl.CostEstimate(
            flops=6 * rows * width * width, bytes_accessed=12 * 2**20, transcendentals=0
        ),
        name="gate",
    )(embedded, *flat, packed)


def finish_kernel(tiles, halves, *refs):
    gated_refs, after_refs = refs[: 3 * halves], refs[3 * halves : 4 * halves]
    packed_ref, depth_ref, head_ref, out_ref, window, residual, project, head, sems = refs[4 * halves :]
    step = pl.program_id(0)
    tile, width = residual.shape
    taps = depth_ref.shape[0]
    edge = 8
    copies = [
        pltpu.make_async_copy(packed_ref.at[:, pl.ds(3 * width, width)], project, sems.at[0]),
        pltpu.make_async_copy(head_ref, head, sems.at[1]),
    ]

    @pl.when(step == 0)
    def _():
        for copy in copies:
            copy.start()

    per_half = tiles // halves
    for half in range(halves):
        before_ref, here_ref, next_ref = gated_refs[3 * half : 3 * half + 3]

        @pl.when(step // per_half == half)
        def _():
            window[edge : edge + tile, :] = here_ref[...].astype(F32)
            residual[...] = after_refs[half][...]

        @pl.when((step > 0) & ((step - 1) // per_half == half))
        def _():
            window[:edge, :] = before_ref[...].astype(F32)[-edge:, :]

        @pl.when((step < tiles - 1) & ((step + 1) // per_half == half))
        def _():
            window[edge + tile :, :] = next_ref[...].astype(F32)[:edge, :]

    @pl.when(step == 0)
    def _():
        window[:edge, :] = jnp.zeros((edge, width), F32)

    @pl.when(step == tiles - 1)
    def _():
        window[edge + tile :, :] = jnp.zeros((edge, width), F32)

    @pl.when(step == 0)
    def _():
        for copy in copies:
            copy.wait()

    part = tile // 2
    rows = [slice(sub * part, (sub + 1) * part) for sub in range(2)]
    sums = []
    for r in rows:
        conv = None
        for tap in range(taps):
            start = r.start + edge - taps // 2 + tap
            term = window[start : start + part, :] * depth_ref[tap : tap + 1, :].astype(F32)
            conv = term if conv is None else conv + term
        activated = (conv * jax.nn.sigmoid(conv)).astype(BF16)
        sums.append(residual[r, :] + dot(activated, project[...]))
    for r, after_conv in zip(rows, sums):
        out_ref[r, :] = dot(layer_norm(after_conv).astype(BF16), head[...]).astype(BF16)


def finish(gated, after, packed, w_depth, head, tile):
    halves = len(gated)
    half_rows, width = gated[0].shape
    codes = head.shape[1]
    frames = halves * half_rows
    tiles = frames // tile
    per_half = half_rows // tile
    strip = 16
    per_tile = tile // strip

    def clip(index, half):
        return jnp.clip(index - half * per_half, 0, per_half - 1)

    specs = []
    for half in range(halves):
        specs += [
            pl.BlockSpec((strip, width), lambda i, half=half: (clip(i - 1, half) * per_tile + per_tile - 1, 0)),
            pl.BlockSpec((tile, width), lambda i, half=half: (clip(i, half), 0)),
            pl.BlockSpec((strip, width), lambda i, half=half: (clip(i + 1, half) * per_tile, 0)),
        ]
    for half in range(halves):
        specs.append(pl.BlockSpec((tile, width), lambda i, half=half: (clip(i, half), 0)))
    return pl.pallas_call(
        functools.partial(finish_kernel, tiles, halves),
        grid=(tiles,),
        in_specs=specs + [ANY, pl.BlockSpec(w_depth.shape, lambda i: (0, 0)), ANY],
        out_specs=pl.BlockSpec((tile, codes), lambda i: (i, 0)),
        out_shape=jax.ShapeDtypeStruct((frames, codes), BF16),
        scratch_shapes=[
            pltpu.VMEM((tile + 16, width), F32),
            pltpu.VMEM((tile, width), F32),
            pltpu.VMEM((width, width), BF16),
            pltpu.VMEM(head.shape, BF16),
            pltpu.SemaphoreType.DMA((2,)),
        ],
        compiler_params=WIDE,
        cost_estimate=pl.CostEstimate(
            flops=2 * frames * width * (width + codes), bytes_accessed=20 * 2**20, transcendentals=0
        ),
        name="finish",
    )(*[g for half in gated for g in (half, half, half)], *after, packed, w_depth, head)


def body(
    token_ids,
    decoded_mask,
    levels_done,
    code_tables,
    mask_vectors,
    w_qkv,
    w_out,
    w_expand,
    w_depth,
    w_project,
    level_heads,
):
    return step(
        token_ids[0, 0], decoded_mask[0, 0], levels_done[0], code_tables[0], mask_vectors,
        w_qkv, w_out, w_expand, w_depth, w_project, level_heads[0],
    )[None, None]


def step(
    token_ids, decoded_mask, done, table, own_mask, w_qkv, w_out, w_expand, w_depth, w_project, head,
):
    groups = lax.axis_size("level")
    level_index = lax.axis_index("level")
    frames = token_ids.shape[0]
    codes, width = table.shape
    head_dim = width // HEADS
    half = codes // 2
    core = lax.rem(lax.axis_index("dp"), 2)
    backs = range(1, groups)

    own_out = w_out.T
    rows, columns = own_out.shape
    small = jnp.concatenate([own_out, own_mask.reshape(-1, columns)], axis=0)
    smalls = [small] + [from_level(small, back) for back in backs]
    packed = jnp.concatenate([s[:rows] for s in smalls] + [w_expand, w_project], axis=1)
    packed = lax.all_gather(packed, "dp", axis=0, tiled=True)

    use_token = (level_index < done) | ((level_index == done) & (decoded_mask == 1))
    own_ids = jnp.where(use_token, token_ids, -1)
    ids = jnp.stack([from_level(own_ids, back) for back in backs], axis=1)
    masks = jnp.concatenate([s[rows:].reshape(1, width) for s in smalls[1:]], axis=0)

    mine = lax.dynamic_slice_in_dim(table, core * half, half, 0)
    halves = []
    for back in backs:
        landed = from_level(mine, back)
        halves += [landed, swap(landed, 1)]
    pieces = []
    chunk = columns // CHUNKS
    for at in range(CHUNKS):
        pieces.append(gather_pieces(w_qkv[:, :, at * chunk : (at + 1) * chunk]))

    tile = frames // QUARTERS
    own = own_term(own_ids[:, None], own_mask, table, tile)
    embedded, normed = embed(ids, masks, own, halves, tile)
    scale = head_dim ** (-0.5) * LOG2E
    queries, keys, values = project(normed, pieces, scale, tile)

    attended = []
    for quarter in range(QUARTERS):
        part = attend(queries, keys, values, quarter, tile, head_dim)
        attended.append([part] + [from_level(part, back) for back in backs])
    after, gated = [], []
    per_half = QUARTERS // 2
    for part in range(2):
        some = attended[part * per_half : (part + 1) * per_half]
        result = gate(embedded, some, packed, part * per_half, tile)
        after.append(result[0])
        gated.append(result[1])
    return finish(gated, after, packed, w_depth, head, tile)


def solution(mesh):
    return jax.shard_map(
        body,
        mesh=mesh,
        in_specs=(
            P("dp", "level", None),
            P("dp", "level", None),
            P("dp"),
            P("level", None, None),
            P("level", None),
            P(None, "dp", "level"),
            P("level", "dp"),
            P("dp", None),
            P(),
            P("dp", None),
            P("level", None, None),
        ),
        out_specs=P("dp", "level", None, None),
        check_vma=False,
    )
```

time: 217 us -> 181 us (0.83); the launches traced: 217 us -> 179 us
  waiting for transfers between devices: 92.8 us -> 35.4 us
  Pallas kernels: 87.4 us -> 104 us
  starting transfers between devices: 11.9 us -> 14.5 us
    ppermute x7, waiting for transfers between devices: 38.1 us -> 3.83 us  [from_level(): lax.ppermute(value, 'level', [(i, (i + back) % groups) for i in range(gro...]
    ppermute x3 -> x5, waiting for transfers between devices: 26.8 us -> 3.25 us  [swap(): return lax.ppermute(value, 'dp', [(i, i ^ bit) for i in range(devices)])]
    pallas_call x6 -> x10, Pallas kernels: 87.4 us -> 104 us  [the longest x4 33.3 us: attend(): pl.pallas_call(functools.partial(attention_kernel, head_dim), grid=(colum...]
    ppermute x3 -> x6, starting transfers between devices: 4.67 us -> 5.43 us  [from_outer(): lax.ppermute(value, 'dp', [(i, (i // 4 + back) % outer * 4 + i % 4) for i...]
    ppermute x3 -> x6, waiting for transfers between devices: 27.9 us -> 28.3 us  [from_outer(): lax.ppermute(value, 'dp', [(i, (i // 4 + back) % outer * 4 + i % 4) for i...]
  transfers between devices with their start and end apart: 14 -> 19, of which waited for: 10 -> 8; matrix products, arithmetic and copies ran while one was open for 2% -> 3% of each run, Pallas kernels for 23% -> 41%
where the time goes in v2:
time: 181 us; the launch traced here: 179 us
  Pallas kernels  104 us (57%)
  waiting for transfers between devices  35.4 us (20%)
  starting transfers between devices  14.5 us (8%)
  between operations  14.3 us (8%)
  local copies, waits for them, and re-layouts  6.65 us (4%)
  other arithmetic  3.76 us (2%)
    pallas_call x4, Pallas kernels, attend(): pl.pallas_call(functools.partial(attention_kernel, head_dim), grid=(colum...  33.3 us
    ppermute x6, waiting for transfers between devices, from_outer(): lax.ppermute(value, 'dp', [(i, (i // 4 + back) % outer * 4 + i % 4) for i...  28.3 us
    pallas_call x2, Pallas kernels, gate(): pl.pallas_call(functools.partial(gate_kernel, quarters, groups, width), g...  24.8 us
    pallas_call x1, Pallas kernels, finish(): pl.pallas_call(functools.partial(finish_kernel, tiles, halves), grid=(til...  18.6 us
    pallas_call x1, Pallas kernels, embed(): pl.pallas_call(functools.partial(embed_kernel, others), grid=(frames // t...  10.2 us
    pallas_call x1, Pallas kernels, project(): pl.pallas_call(functools.partial(project_kernel, chunks, outer, scale), g...  9.95 us
    ppermute x7, starting transfers between devices, from_level(): lax.ppermute(value, 'level', [(i, (i + back) % groups) for i in range(gro...  7.99 us
    pallas_call x1, Pallas kernels, own_term(): pl.pallas_call(own_term_kernel, grid=(frames // tile,), in_specs=[pl.Bloc...  7.07 us
  transfers between devices with their start and end apart: 19, of which 8 were waited for; matrix products, arithmetic and copies ran while one was open for 3% of the time, Pallas kernels for 41%

profile of v2, /device:TPU:14, one launch (start us, length us, event | category | flops | bytes accessed | tf_op | source)
XLA Modules:
  0.0 178.5 jit_solution(10730707861374969941)
XLA Ops:
  6.5 0.7 reduce.1
  7.3 0.8 pad_maximum_fusion.5
  8.1 0.5 collective-permute-start.1
  8.7 3.8 %collective-permute-done.1 = bf16[66,512]{1,0:T(8,128)(2,1)S(1)} collective-permute-done((bf16[66,512]{1,0:T(8,128)(2,1)S(1)}, bf16[66,512]{1,0:T(8,128)(2,1)S(1)}, u32[]{:S(2)}, u32[]{:S(2)}) %collective-permute-start.1) | collective-permute-done | bytes 67616 | tf_op jit(solution)/shard_map/ppermute | solution.py:50
  12.5 1.9 %pad_maximum_fusion.2 = bf16[64,4096]{1,0:T(8,128)(2,1)} fusion(bf16[64,1024]{1,0:T(8,128)(2,1)} %param.20, bf16[64,2048]{1,0:T(8,128)(2,1)} %param.18, bf16[64,512]{1,0:T(8,128)(2,1)S(1)} %slice.17, bf16[64,512]{1,0:T(8,128)(2,1)} %bitcast.35), kind=kLoop, calls=%fused_computation.3 | loop fusion | flops 2097152 | bytes 1048576 | tf_op jit(solution)/shard_map/concatenate | solution.py:470
  14.4 0.0 all-gather.2.cloned.1.call-update
  14.4 0.0 copy-start.5
  14.4 0.0 copy-start.6
  14.4 1.3 dynamic-slice_bitcast_fusion
  15.7 0.6 collective-permute-start.2
  16.4 1.6 collective-permute-start.9
  18.0 1.2 collective-permute-start.10
  19.2 1.8 %collective-permute-start.11 = (bf16[3,64,256]{2,1,0:T(8,128)(2,1)S(1)}, bf16[3,64,256]{2,1,0:T(8,128)(2,1)S(1)}, u32[]{:S(2)}, u32[]{:S(2)}) collective-permute-start(bf16[3,64,256]{2,1,0:T(8,128)(2,1)S(1)} %get-tuple-element.31), channel_id=1, source_target_pairs={{0,24},{2,26},{4,28},{6,30},{8,0},{10,2},{12,4},{14,6},{16,8},{18,... | collective-permute-start | bytes 294920 | tf_op jit(solution)/shard_map/ppermute | solution.py:43
  21.0 0.2 collective-permute-start.4
  21.3 3.0 %collective-permute-done.9 = bf16[3,64,256]{2,1,0:T(8,128)(2,1)S(1)} collective-permute-done((bf16[3,64,256]{2,1,0:T(8,128)(2,1)S(1)}, bf16[3,64,256]{2,1,0:T(8,128)(2,1)S(1)}, u32[]{:S(2)}, u32[]{:S(2)}) %collective-permute-start.9) | collective-permute-done | bytes 98336 | tf_op jit(solution)/shard_map/ppermute | solution.py:43
  24.2 0.5 collective-permute-start.5
  24.7 10.0 %collective-permute-done.10 = bf16[3,64,256]{2,1,0:T(8,128)(2,1)S(1)} collective-permute-done((bf16[3,64,256]{2,1,0:T(8,128)(2,1)S(1)}, bf16[3,64,256]{2,1,0:T(8,128)(2,1)S(1)}, u32[]{:S(2)}, u32[]{:S(2)}) %collective-permute-start.10) | collective-permute-done | bytes 98336 | tf_op jit(solution)/shard_map/ppermute | solution.py:43
  34.8 0.0 collective-permute-start.6
  34.8 3.7 %collective-permute-done.11 = bf16[3,64,256]{2,1,0:T(8,128)(2,1)S(1)} collective-permute-done((bf16[3,64,256]{2,1,0:T(8,128)(2,1)S(1)}, bf16[3,64,256]{2,1,0:T(8,128)(2,1)S(1)}, u32[]{:S(2)}, u32[]{:S(2)}) %collective-permute-start.11) | collective-permute-done | bytes 98336 | tf_op jit(solution)/shard_map/ppermute | solution.py:43
  38.5 0.1 fusion
  38.6 0.3 collective-permute-start.12
  38.9 2.3 %collective-permute-done.4 = bf16[3,64,256]{2,1,0:T(8,128)(2,1)S(1)} collective-permute-done((bf16[3,64,256]{2,1,0:T(8,128)(2,1)S(1)}, bf16[3,64,256]{2,1,0:T(8,128)(2,1)S(1)}, u32[]{:S(2)}, u32[]{:S(2)}) %collective-permute-start.4) | collective-permute-done | bytes 98336 | tf_op jit(solution)/shard_map/ppermute | solution.py:43
  41.2 6.3 %collective-permute-done.5 = bf16[3,64,256]{2,1,0:T(8,128)(2,1)S(1)} collective-permute-done((bf16[3,64,256]{2,1,0:T(8,128)(2,1)S(1)}, bf16[3,64,256]{2,1,0:T(8,128)(2,1)S(1)}, u32[]{:S(2)}, u32[]{:S(2)}) %collective-permute-start.5) | collective-permute-done | bytes 98336 | tf_op jit(solution)/shard_map/ppermute | solution.py:43
  47.5 3.0 %collective-permute-done.6 = bf16[3,64,256]{2,1,0:T(8,128)(2,1)S(1)} collective-permute-done((bf16[3,64,256]{2,1,0:T(8,128)(2,1)S(1)}, bf16[3,64,256]{2,1,0:T(8,128)(2,1)S(1)}, u32[]{:S(2)}, u32[]{:S(2)}) %collective-permute-start.6) | collective-permute-done | bytes 98336 | tf_op jit(solution)/shard_map/ppermute | solution.py:43
  50.5 0.1 fusion.1
  50.5 0.4 collective-permute-start.7
  51.0 0.0 collective-permute-done.2.refs_0_
  51.0 0.0 collective-permute-start.3
  51.7 2.1 %collective-permute-start = (s32[1536]{0:T(1024)S(1)}, s32[1536]{0:T(1024)S(1)}, u32[]{:S(2)}, u32[]{:S(2)}) collective-permute-start(s32[1536]{0:T(1024)S(1)} %get-tuple-element.23), channel_id=1, source_target_pairs={{0,1},{1,0},{2,3},{3,2},{4,5},{5,4},{6,7},{7,6},{8,9},{9,8},{10,11... | collective-permute-start | bytes 18440 | tf_op jit(solution)/shard_map/ppermute | solution.py:50
  53.8 1.2 copy.12.ids_ref
  55.0 0.0 collective-permute-done.12.refs_4_
  55.0 0.1 pad_maximum_fusion.1
  55.1 0.3 collective-permute-start.13
  55.3 3.2 %collective-permute-done.7.refs_1_ = bf16[4,3,64,256]{3,2,1,0:T(8,128)(2,1)S(1)} collective-permute-done((bf16[4,3,64,256]{3,2,1,0:T(8,128)(2,1)S(1)}, bf16[4,3,64,256]{3,2,1,0:T(8,128)(2,1)S(1)}, u32[]{:S(2)}, u32[]{:S(2)}) %collective-permute-start.7) | collective-permute-done | bytes 393248 | tf_op jit(solution)/shard_map/ppermute | solution.py:37
  58.6 0.1 pad_maximum_fusion
  58.7 0.1 collective-permute-start.8
  58.8 7.1 %own_term.1.own_ref = bf16[1536,1024]{1,0:T(8,128)(2,1)} custom-call(s32[1536,1]{1,0:T(8,128)} %copy.12.ids_ref, bf16[1,1024]{1,0:T(2,128)(2,1)} %mask_ref.1, bf16[1024,1024]{1,0:T(8,128)(2,1)} %bitcast.31), custom_call_target="tpu_custom_call" | custom-call | flops 3221225472 | bytes 4194304 | tf_op jit(solution)/shard_map/own_term/pallas_call | solution.py:80
  65.8 0.0 collective-permute-done
  65.8 1.2 stack.68.ids_ref
  67.0 0.6 copy.14
  67.6 0.0 collective-permute-done.3.refs_1_
  67.6 10.2 %embed.1 = (f32[1536,1024]{1,0:T(8,128)}, bf16[1536,1024]{1,0:T(8,128)(2,1)}) custom-call(s32[1536,1]{1,0:T(8,128)} %stack.68.ids_ref, bf16[1,1024]{1,0:T(2,128)(2,1)} %bitcast.43, bf16[1536,1024]{1,0:T(8,128)(2,1)} %own_term.1.own_ref, bf16[512,1024]{1,0:T(8,128)(2,1)} %collective-permute-done.2.refs_0_, bf16[512,1024]{1,0:T(8,128)(2,1)} %collective-permute-done.3.refs_1_), custom_call_target="tpu_custom_call" | custom-call | flops 3221225472 | bytes 12582912 | tf_op jit(solution)/shard_map/embed/pallas_call | solution.py:143
  77.8 0.0 collective-permute-done.8.refs_2_
  77.8 10.0 %project.1 = (bf16[1536,512]{1,0:T(8,128)(2,1)}, bf16[1536,512]{1,0:T(8,128)(2,1)}, bf16[1536,512]{1,0:T(8,128)(2,1)}) custom-call(bf16[1536,1024]{1,0:T(8,128)(2,1)} %get-tuple-element.15.normed_ref, bf16[4,3,64,256]{3,2,1,0:T(8,128)(2,1)} %copy-done.2, bf16[4,3,64,256]{3,2,1,0:T(8,128)(2,1)} %copy-done.3, ...), custom_call_target="tpu_custom_call" | custom-call | flops 4831838208 | bytes 12582912 | tf_op jit(solution)/shard_map/project/pallas_call | solution.py:204
  87.8 8.4 %attend.7.refs_2_ = bf16[384,512]{1,0:T(8,128)(2,1)} custom-call(bf16[1536,512]{1,0:T(8,128)(2,1)} %get-tuple-element.16.queries_ref, bf16[1536,512]{1,0:T(8,128)(2,1)} %get-tuple-element.17.keys_ref, bf16[1536,512]{1,0:T(8,128)(2,1)} %get-tuple-element.18.values_ref), custom_call_target="tpu_custom_call" | custom-call | flops 4831838208 | bytes 4194304 | tf_op jit(solution)/shard_map/attend/pallas_call | solution.py:243
  96.1 2.7 %collective-permute-start.17 = (bf16[384,512]{1,0:T(8,128)(2,1)}, bf16[384,512]{1,0:T(8,128)(2,1)S(1)}, u32[]{:S(2)}, u32[]{:S(2)}) collective-permute-start(bf16[384,512]{1,0:T(8,128)(2,1)} %attend.7.refs_2_), channel_id=1, source_target_pairs={{0,1},{1,0},{2,3},{3,2},{4,5},{5,4},{6,7},{7,6},{8,9},{9,8},{10,11... | collective-permute-start | bytes 1179656 | tf_op jit(solution)/shard_map/ppermute | solution.py:50
  98.9 8.3 %attend.6.refs_0_ = bf16[384,512]{1,0:T(8,128)(2,1)} custom-call(bf16[1536,512]{1,0:T(8,128)(2,1)} %get-tuple-element.16.queries_ref, bf16[1536,512]{1,0:T(8,128)(2,1)} %get-tuple-element.17.keys_ref, bf16[1536,512]{1,0:T(8,128)(2,1)} %get-tuple-element.18.values_ref), custom_call_target="tpu_custom_call" | custom-call | flops 4831838208 | bytes 4194304 | tf_op jit(solution)/shard_map/attend/pallas_call | solution.py:243
  107.2 0.0 collective-permute-start.16
  107.2 8.3 %attend.5.refs_2_ = bf16[384,512]{1,0:T(8,128)(2,1)} custom-call(bf16[1536,512]{1,0:T(8,128)(2,1)} %get-tuple-element.16.queries_ref, bf16[1536,512]{1,0:T(8,128)(2,1)} %get-tuple-element.17.keys_ref, bf16[1536,512]{1,0:T(8,128)(2,1)} %get-tuple-element.18.values_ref), custom_call_target="tpu_custom_call" | custom-call | flops 4831838208 | bytes 4194304 | tf_op jit(solution)/shard_map/attend/pallas_call | solution.py:243
  115.5 2.0 %collective-permute-start.15 = (bf16[384,512]{1,0:T(8,128)(2,1)}, bf16[384,512]{1,0:T(8,128)(2,1)S(1)}, u32[]{:S(2)}, u32[]{:S(2)}) collective-permute-start(bf16[384,512]{1,0:T(8,128)(2,1)} %attend.5.refs_2_), channel_id=1, source_target_pairs={{0,1},{1,0},{2,3},{3,2},{4,5},{5,4},{6,7},{7,6},{8,9},{9,8},{10,11... | collective-permute-start | bytes 1179656 | tf_op jit(solution)/shard_map/ppermute | solution.py:50
  117.5 8.3 %attend.4.refs_0_ = bf16[384,512]{1,0:T(8,128)(2,1)} custom-call(bf16[1536,512]{1,0:T(8,128)(2,1)} %get-tuple-element.16.queries_ref, bf16[1536,512]{1,0:T(8,128)(2,1)} %get-tuple-element.17.keys_ref, bf16[1536,512]{1,0:T(8,128)(2,1)} %get-tuple-element.18.values_ref), custom_call_target="tpu_custom_call" | custom-call | flops 4831838208 | bytes 4194304 | tf_op jit(solution)/shard_map/attend/pallas_call | solution.py:243
  125.8 0.0 collective-permute-start.14
  125.8 0.0 collective-permute-done.17.refs_3_
  125.8 0.0 copy-start.10
  125.8 0.0 all-gather.2.cloned.1.call-done.refs_4_.refs_8_
  125.9 0.7 copy-done.8
  126.6 0.1 copy-done.10
  126.7 12.4 %gate.3 = (f32[768,1024]{1,0:T(8,128)}, bf16[768,1024]{1,0:T(8,128)(2,1)}) custom-call(f32[1536,1024]{1,0:T(8,128)} %get-tuple-element.14.embedded_ref, bf16[384,512]{1,0:T(8,128)(2,1)} %attend.6.refs_0_, bf16[384,512]{1,0:T(8,128)(2,1)} %copy-done.10, bf16[384,512]{1,0:T(8,128)(2,1)} %attend.7.refs_2_, bf16[384,512]{1,0:T(8,128)(2,1)} %copy-done.8, ...), custom_call_target="tpu_custom_call" | custom-call | flops 4831838208 | bytes 12582912 | tf_op jit(solution)/shard_map/gate/pallas_call | solution.py:306
  139.1 0.0 collective-permute-done.15.refs_3_
  139.1 0.0 collective-permute-done.14.refs_1_
  139.2 0.7 copy-done.7
  139.9 0.7 copy-done.9
  140.7 12.4 %gate.2 = (f32[768,1024]{1,0:T(8,128)}, bf16[768,1024]{1,0:T(8,128)(2,1)}) custom-call(f32[1536,1024]{1,0:T(8,128)} %get-tuple-element.14.embedded_ref, bf16[384,512]{1,0:T(8,128)(2,1)} %attend.4.refs_0_, bf16[384,512]{1,0:T(8,128)(2,1)} %copy-done.9, bf16[384,512]{1,0:T(8,128)(2,1)} %attend.5.refs_2_, bf16[384,512]{1,0:T(8,128)(2,1)} %copy-done.7, ...), custom_call_target="tpu_custom_call" | custom-call | flops 4831838208 | bytes 12582912 | tf_op jit(solution)/shard_map/gate/pallas_call | solution.py:306
  153.1 18.6 %finish.1 = bf16[1536,1024]{1,0:T(8,128)(2,1)} custom-call(bf16[768,1024]{1,0:T(8,128)(2,1)} %get-tuple-element.19.refs_0_.refs_1_.refs_2_, bf16[768,1024]{1,0:T(8,128)(2,1)} %get-tuple-element.19.refs_0_.refs_1_.refs_2_, bf16[768,1024]{1,0:T(8,128)(2,1)} %get-tuple-element.19.refs_0_.refs_1_.refs_2_, ...), custom_call_target="tpu_custom_call" | custom-call | flops 6442450944 | bytes 20971520 | tf_op jit(solution)/shard_map/finish/pallas_call | solution.py:414
  (23 shorter events, 0.1 us)
Async XLA Ops:
  6.5 9.8 %copy-start.4 = (bf16[3,64,512]{2,1,0:T(8,128)(2,1)S(1)}, bf16[3,64,512]{2,1,0:T(8,128)(2,1)}, u32[]{:S(2)}) copy-start(bf16[3,64,512]{2,1,0:T(8,128)(2,1)} %param.16) | copy-start | bytes 589828
  6.5 119.3 %all-gather.2.cloned.1.call-start = ((), (), s32[]{:S(2)}) async-start(), calls=%async_computation | async-start | bytes 8912896 | tf_op jit(solution)/shard_map/all_gather | solution.py:471
  8.1 4.4 %collective-permute-start.1 = (bf16[66,512]{1,0:T(8,128)(2,1)S(1)}, bf16[66,512]{1,0:T(8,128)(2,1)S(1)}, u32[]{:S(2)}, u32[]{:S(2)}) collective-permute-start(bf16[66,512]{1,0:T(8,128)(2,1)S(1)} %pad_maximum_fusion.5), channel_id=1, source_target_pairs={{0,1},{1,0},{2,3},{3,2},{4,5},{5,4},{6,7},{7,6},{8,9},{9,8},{10,11... | collective-permute-start | bytes 202760 | tf_op jit(solution)/shard_map/ppermute | solution.py:50
  14.4 37.2 %copy-start.5 = (s32[1,1,1536]{2,1,0:T(1,128)S(1)}, s32[1,1,1536]{2,1,0:T(1,128)}, u32[]{:S(2)}) copy-start(s32[1,1,1536]{2,1,0:T(1,128)} %param.11) | copy-start | bytes 18436
  14.4 37.2 %copy-start.6 = (s32[1,1,1536]{2,1,0:T(1,128)S(1)}, s32[1,1,1536]{2,1,0:T(1,128)}, u32[]{:S(2)}) copy-start(s32[1,1,1536]{2,1,0:T(1,128)} %param.12) | copy-start | bytes 18436
  15.7 35.2 %collective-permute-start.2 = (bf16[512,1024]{1,0:T(8,128)(2,1)S(1)}, bf16[512,1024]{1,0:T(8,128)(2,1)}, u32[]{:S(2)}, u32[]{:S(2)}) collective-permute-start(bf16[512,1024]{1,0:T(8,128)(2,1)S(1)} %dynamic-slice_bitcast_fusion), channel_id=1, source_target_pairs={{0,1},{1,0},{2,3},{3,2},{4,5},{5,4},{6,7},{7,6},{8,9},{9,8},{10,11... | collective-permute-start | bytes 3145736 | tf_op jit(solution)/shard_map/ppermute | solution.py:50
  16.4 7.8 %collective-permute-start.9 = (bf16[3,64,256]{2,1,0:T(8,128)(2,1)S(1)}, bf16[3,64,256]{2,1,0:T(8,128)(2,1)S(1)}, u32[]{:S(2)}, u32[]{:S(2)}) collective-permute-start(bf16[3,64,256]{2,1,0:T(8,128)(2,1)S(1)} %get-tuple-element.31), channel_id=1, source_target_pairs={{0,8},{2,10},{4,12},{6,14},{8,16},{10,18},{12,20},{14,22},{16,24},... | collective-permute-start | bytes 294920 | tf_op jit(solution)/shard_map/ppermute | solution.py:43
  18.0 16.8 %collective-permute-start.10 = (bf16[3,64,256]{2,1,0:T(8,128)(2,1)S(1)}, bf16[3,64,256]{2,1,0:T(8,128)(2,1)S(1)}, u32[]{:S(2)}, u32[]{:S(2)}) collective-permute-start(bf16[3,64,256]{2,1,0:T(8,128)(2,1)S(1)} %get-tuple-element.31), channel_id=1, source_target_pairs={{0,16},{2,18},{4,20},{6,22},{8,24},{10,26},{12,28},{14,30},{16,0},... | collective-permute-start | bytes 294920 | tf_op jit(solution)/shard_map/ppermute | solution.py:43
  19.2 19.3 %collective-permute-start.11 = (bf16[3,64,256]{2,1,0:T(8,128)(2,1)S(1)}, bf16[3,64,256]{2,1,0:T(8,128)(2,1)S(1)}, u32[]{:S(2)}, u32[]{:S(2)}) collective-permute-start(bf16[3,64,256]{2,1,0:T(8,128)(2,1)S(1)} %get-tuple-element.31), channel_id=1, source_target_pairs={{0,24},{2,26},{4,28},{6,30},{8,0},{10,2},{12,4},{14,6},{16,8},{18,... | collective-permute-start | bytes 294920 | tf_op jit(solution)/shard_map/ppermute | solution.py:43
  21.0 20.2 %collective-permute-start.4 = (bf16[3,64,256]{2,1,0:T(8,128)(2,1)S(1)}, bf16[3,64,256]{2,1,0:T(8,128)(2,1)S(1)}, u32[]{:S(2)}, u32[]{:S(2)}) collective-permute-start(bf16[3,64,256]{2,1,0:T(8,128)(2,1)S(1)} %get-tuple-element.32), channel_id=1, source_target_pairs={{0,8},{2,10},{4,12},{6,14},{8,16},{10,18},{12,20},{14,22},{16,24},... | collective-permute-start | bytes 294920 | tf_op jit(solution)/shard_map/ppermute | solution.py:43
  24.2 23.3 %collective-permute-start.5 = (bf16[3,64,256]{2,1,0:T(8,128)(2,1)S(1)}, bf16[3,64,256]{2,1,0:T(8,128)(2,1)S(1)}, u32[]{:S(2)}, u32[]{:S(2)}) collective-permute-start(bf16[3,64,256]{2,1,0:T(8,128)(2,1)S(1)} %get-tuple-element.32), channel_id=1, source_target_pairs={{0,16},{2,18},{4,20},{6,22},{8,24},{10,26},{12,28},{14,30},{16,0},... | collective-permute-start | bytes 294920 | tf_op jit(solution)/shard_map/ppermute | solution.py:43
  34.8 15.7 %collective-permute-start.6 = (bf16[3,64,256]{2,1,0:T(8,128)(2,1)S(1)}, bf16[3,64,256]{2,1,0:T(8,128)(2,1)S(1)}, u32[]{:S(2)}, u32[]{:S(2)}) collective-permute-start(bf16[3,64,256]{2,1,0:T(8,128)(2,1)S(1)} %get-tuple-element.32), channel_id=1, source_target_pairs={{0,24},{2,26},{4,28},{6,30},{8,0},{10,2},{12,4},{14,6},{16,8},{18,... | collective-permute-start | bytes 294920 | tf_op jit(solution)/shard_map/ppermute | solution.py:43
  38.6 20.1 %copy-start = (bf16[4,3,64,256]{3,2,1,0:T(8,128)(2,1)}, bf16[4,3,64,256]{3,2,1,0:T(8,128)(2,1)S(1)}, u32[]{:S(2)}) copy-start(bf16[4,3,64,256]{3,2,1,0:T(8,128)(2,1)S(1)} %get-tuple-element.26.refs_3_) | copy-start | bytes 1179652
  38.6 16.4 %collective-permute-start.12 = (bf16[4,3,64,256]{3,2,1,0:T(8,128)(2,1)S(1)}, bf16[4,3,64,256]{3,2,1,0:T(8,128)(2,1)S(1)}, u32[]{:S(2)}, u32[]{:S(2)}) collective-permute-start(bf16[4,3,64,256]{3,2,1,0:T(8,128)(2,1)S(1)} %get-tuple-element.26.refs_3_), channel_id=1, source_target_pairs={{0,4},{2,6},{4,0},{6,2},{8,12},{10,14},{12,8},{14,10},{16,20},{18,... | collective-permute-start | bytes 1179656 | tf_op jit(solution)/shard_map/ppermute | solution.py:37
  50.5 15.3 %copy-start.2 = (bf16[4,3,64,256]{3,2,1,0:T(8,128)(2,1)}, bf16[4,3,64,256]{3,2,1,0:T(8,128)(2,1)S(1)}, u32[]{:S(2)}) copy-start(bf16[4,3,64,256]{3,2,1,0:T(8,128)(2,1)S(1)} %get-tuple-element.28.refs_0_) | copy-start | bytes 1179652
  50.5 8.0 %collective-permute-start.7 = (bf16[4,3,64,256]{3,2,1,0:T(8,128)(2,1)S(1)}, bf16[4,3,64,256]{3,2,1,0:T(8,128)(2,1)S(1)}, u32[]{:S(2)}, u32[]{:S(2)}) collective-permute-start(bf16[4,3,64,256]{3,2,1,0:T(8,128)(2,1)S(1)} %get-tuple-element.28.refs_0_), channel_id=1, source_target_pairs={{0,4},{2,6},{4,0},{6,2},{8,12},{10,14},{12,8},{14,10},{16,20},{18,... | collective-permute-start | bytes 1179656 | tf_op jit(solution)/shard_map/ppermute | solution.py:37
  51.0 16.6 %collective-permute-start.3 = (bf16[512,1024]{1,0:T(8,128)(2,1)}, bf16[512,1024]{1,0:T(8,128)(2,1)}, u32[]{:S(2)}, u32[]{:S(2)}) collective-permute-start(bf16[512,1024]{1,0:T(8,128)(2,1)} %collective-permute-done.2.refs_0_), channel_id=1, source_target_pairs={{0,2},{2,0},{4,6},{6,4},{8,10},{10,8},{12,14},{14,12},{16,18},{18,... | collective-permute-start | bytes 3145736 | tf_op jit(solution)/shard_map/ppermute | solution.py:37
  51.7 14.2 %collective-permute-start = (s32[1536]{0:T(1024)S(1)}, s32[1536]{0:T(1024)S(1)}, u32[]{:S(2)}, u32[]{:S(2)}) collective-permute-start(s32[1536]{0:T(1024)S(1)} %get-tuple-element.23), channel_id=1, source_target_pairs={{0,1},{1,0},{2,3},{3,2},{4,5},{5,4},{6,7},{7,6},{8,9},{9,8},{10,11... | collective-permute-start | bytes 18440 | tf_op jit(solution)/shard_map/ppermute | solution.py:50
  55.0 10.9 %copy-start.1 = (bf16[4,3,64,256]{3,2,1,0:T(8,128)(2,1)}, bf16[4,3,64,256]{3,2,1,0:T(8,128)(2,1)S(1)}, u32[]{:S(2)}) copy-start(bf16[4,3,64,256]{3,2,1,0:T(8,128)(2,1)S(1)} %collective-permute-done.12.refs_4_) | copy-start | bytes 1179652
  55.1 22.7 %collective-permute-start.13 = (bf16[2,4,3,64,256]{4,3,2,1,0:T(8,128)(2,1)S(1)}, bf16[2,4,3,64,256]{4,3,2,1,0:T(8,128)(2,1)}, u32[]{:S(2)}, u32[]{:S(2)}) collective-permute-start(bf16[2,4,3,64,256]{4,3,2,1,0:T(8,128)(2,1)S(1)} %pad_maximum_fusion.1), channel_id=1, source_target_pairs={{0,2},{2,0},{4,6},{6,4},{8,10},{10,8},{12,14},{14,12},{16,18},{18,... | collective-permute-start | bytes 2359304 | tf_op jit(solution)/shard_map/ppermute | solution.py:37
  58.6 7.2 %copy-start.3 = (bf16[4,3,64,256]{3,2,1,0:T(8,128)(2,1)}, bf16[4,3,64,256]{3,2,1,0:T(8,128)(2,1)S(1)}, u32[]{:S(2)}) copy-start(bf16[4,3,64,256]{3,2,1,0:T(8,128)(2,1)S(1)} %collective-permute-done.7.refs_1_) | copy-start | bytes 1179652
  58.7 19.1 %collective-permute-start.8 = (bf16[2,4,3,64,256]{4,3,2,1,0:T(8,128)(2,1)S(1)}, bf16[2,4,3,64,256]{4,3,2,1,0:T(8,128)(2,1)}, u32[]{:S(2)}, u32[]{:S(2)}) collective-permute-start(bf16[2,4,3,64,256]{4,3,2,1,0:T(8,128)(2,1)S(1)} %pad_maximum_fusion), channel_id=1, source_target_pairs={{0,2},{2,0},{4,6},{6,4},{8,10},{10,8},{12,14},{14,12},{16,18},{18,... | collective-permute-start | bytes 2359304 | tf_op jit(solution)/shard_map/ppermute | solution.py:37
  96.1 29.7 %collective-permute-start.17 = (bf16[384,512]{1,0:T(8,128)(2,1)}, bf16[384,512]{1,0:T(8,128)(2,1)S(1)}, u32[]{:S(2)}, u32[]{:S(2)}) collective-permute-start(bf16[384,512]{1,0:T(8,128)(2,1)} %attend.7.refs_2_), channel_id=1, source_target_pairs={{0,1},{1,0},{2,3},{3,2},{4,5},{5,4},{6,7},{7,6},{8,9},{9,8},{10,11... | collective-permute-start | bytes 1179656 | tf_op jit(solution)/shard_map/ppermute | solution.py:50
  107.2 18.6 %collective-permute-start.16 = (bf16[384,512]{1,0:T(8,128)(2,1)}, bf16[384,512]{1,0:T(8,128)(2,1)S(1)}, u32[]{:S(2)}, u32[]{:S(2)}) collective-permute-start(bf16[384,512]{1,0:T(8,128)(2,1)} %attend.6.refs_0_), channel_id=1, source_target_pairs={{0,1},{1,0},{2,3},{3,2},{4,5},{5,4},{6,7},{7,6},{8,9},{9,8},{10,11... | collective-permute-start | bytes 1179656 | tf_op jit(solution)/shard_map/ppermute | solution.py:50
  115.5 23.6 %collective-permute-start.15 = (bf16[384,512]{1,0:T(8,128)(2,1)}, bf16[384,512]{1,0:T(8,128)(2,1)S(1)}, u32[]{:S(2)}, u32[]{:S(2)}) collective-permute-start(bf16[384,512]{1,0:T(8,128)(2,1)} %attend.5.refs_2_), channel_id=1, source_target_pairs={{0,1},{1,0},{2,3},{3,2},{4,5},{5,4},{6,7},{7,6},{8,9},{9,8},{10,11... | collective-permute-start | bytes 1179656 | tf_op jit(solution)/shard_map/ppermute | solution.py:50
  125.8 13.3 %collective-permute-start.14 = (bf16[384,512]{1,0:T(8,128)(2,1)}, bf16[384,512]{1,0:T(8,128)(2,1)S(1)}, u32[]{:S(2)}, u32[]{:S(2)}) collective-permute-start(bf16[384,512]{1,0:T(8,128)(2,1)} %attend.4.refs_0_), channel_id=1, source_target_pairs={{0,1},{1,0},{2,3},{3,2},{4,5},{5,4},{6,7},{7,6},{8,9},{9,8},{10,11... | collective-permute-start | bytes 1179656 | tf_op jit(solution)/shard_map/ppermute | solution.py:50
  125.8 0.8 copy-start.8
  125.8 0.9 copy-start.10
  139.1 0.8 copy-start.7
  139.9 0.7 copy-start.9
Sparse Core Ops, SparseCore 0:
  14.5 82.9 all-gather.1

commit v3 on v2

v3 whole, which is shorter than its diff:
```python
import functools

import jax
import jax.numpy as jnp
from jax import lax
from jax.experimental import pallas as pl
from jax.experimental.pallas import tpu as pltpu
from jax.sharding import PartitionSpec as P


HEADS = 16
LOG2E = 1.4426950408889634
BF16 = jnp.bfloat16
F32 = jnp.float32
ANY = pl.BlockSpec(memory_space=pl.ANY)
QUARTERS = 4
CHUNKS = 2
STRIP = 16
SUBS = 3


def grant(mebibytes):
    return pltpu.CompilerParams(vmem_limit_bytes=mebibytes * 2**20)


def layer_norm(values):
    centered = values - jnp.mean(values, axis=-1, keepdims=True)
    variance = jnp.mean(centered * centered, axis=-1, keepdims=True)
    return centered * lax.rsqrt(variance + 1e-05)


def gate_of(values):
    return 0.5 * jnp.tanh(0.5 * values) + 0.5


def dot(left, right):
    return jnp.dot(left, right, preferred_element_type=F32)


def dot_t(left, right):
    return lax.dot_general(left, right, (((1,), (1,)), ((), ())), preferred_element_type=F32)


def swap(value, bit):
    devices = lax.axis_size("dp")
    return lax.ppermute(value, "dp", [(i, i ^ bit) for i in range(devices)])


def from_outer(value, back):
    devices = lax.axis_size("dp")
    outer = devices // 4
    return lax.ppermute(
        value, "dp", [(i, ((i // 4 + back) % outer) * 4 + i % 4) for i in range(devices)]
    )


def from_level(value, back):
    groups = lax.axis_size("level")
    return lax.ppermute(value, "level", [(i, (i + back) % groups) for i in range(groups)])


def gather_pieces(shard):
    outer = lax.axis_size("dp") // 4
    near = [shard] + [from_outer(shard, back) for back in range(1, outer)]
    near = jnp.stack(near)
    far = swap(near, 2)
    return near, far, swap(near, 1), swap(far, 1)


def piece_copies(pieces, place, sems):
    outer, rows_here = pieces[0].shape[0], pieces[0].shape[-2]
    copies = []
    for side, piece in enumerate(pieces):
        for back in range(outer):
            row = piece_owner(back, side % 2, side // 2) * rows_here
            target = place(pl.ds(row, rows_here))
            copies.append(pltpu.make_async_copy(piece.at[back], target, sems.at[len(copies)]))
    return copies


def piece_owner(back, pair, core):
    index, outer = lax.axis_index("dp"), lax.axis_size("dp") // 4
    source = lax.rem(index // 4 + outer - back, outer)
    own_pair, own_core = lax.rem(index // 2, 2), lax.rem(index, 2)
    return source * 4 + (1 - own_pair if pair else own_pair) * 2 + (1 - own_core if core else own_core)


def own_term_kernel(ids_ref, mask_ref, table_ref, out_ref):
    code_row = lax.broadcasted_iota(jnp.int32, (1, table_ref.shape[0]), 1)
    ids = ids_ref[:, :1]
    onehot = jnp.where(ids == code_row, 1.0, 0.0).astype(BF16)
    fill = jnp.where(ids < 0, mask_ref[...].astype(F32), 0.0)
    out_ref[...] = (dot(onehot, table_ref[...]) + fill).astype(BF16)


def own_term(ids, mask, table, tile):
    frames = ids.shape[0]
    codes, width = table.shape
    row_block = lambda i: (i, 0)
    return pl.pallas_call(
        own_term_kernel,
        grid=(frames // tile,),
        in_specs=[
            pl.BlockSpec((tile, 1), row_block),
            pl.BlockSpec((1, width), lambda i: (0, 0)),
            pl.BlockSpec((codes, width), lambda i: (0, 0)),
        ],
        out_specs=pl.BlockSpec((tile, width), row_block),
        out_shape=jax.ShapeDtypeStruct((frames, width), BF16),
        compiler_params=grant(14),
        cost_estimate=pl.CostEstimate(
            flops=2 * frames * codes * width, bytes_accessed=2**22, transcendentals=0
        ),
        name="own_term",
    )(ids, mask, table)


def project_kernel(others, chunks, scale, ids_ref, mask_ref, own_ref, *refs):
    halves, pieces = refs[: 2 * others], refs[2 * others : 2 * others + 4 * chunks]
    embedded_ref, queries_ref, keys_ref, values_ref = refs[2 * others + 4 * chunks :][:4]
    tables, weights, table_sems, weight_sems = refs[2 * others + 4 * chunks + 4 :]
    codes = tables.shape[0] // others
    half = codes // 2
    core = lax.rem(lax.axis_index("dp"), 2)
    copies = []
    for index, source in enumerate(halves):
        base, side = (index // 2) * codes, index % 2
        place = base + (core if side == 0 else 1 - core) * half
        target = tables.at[pl.ds(place, half)]
        copies.append(
            pltpu.make_async_copy(source.at[pl.ds(0, half)], target, table_sems.at[index])
        )
    columns = pieces[0].shape[-1]
    for chunk in range(chunks):
        lanes = pl.ds(chunk * columns, columns)
        copies += piece_copies(
            pieces[4 * chunk : 4 * chunk + 4],
            lambda rows, lanes=lanes: weights.at[:, rows, lanes],
            weight_sems.at[chunk],
        )

    @pl.when(pl.program_id(0) == 0)
    def _():
        for copy in copies:
            copy.start()
        for copy in copies:
            copy.wait()

    code_row = lax.broadcasted_iota(jnp.int32, (1, codes), 1)
    part = ids_ref.shape[0] // 2
    rows = [slice(sub * part, (sub + 1) * part) for sub in range(2)]
    totals = []
    for r in rows:
        total = own_ref[r, :].astype(F32)
        for level in range(others):
            ids = ids_ref[r, level : level + 1]
            onehot = jnp.where(ids == code_row, 1.0, 0.0).astype(BF16)
            total = total + dot(onehot, tables[level * codes : (level + 1) * codes, :])
            fill = mask_ref[level : level + 1, :].astype(F32)
            total = total + jnp.where(ids < 0, fill, 0.0)
        totals.append(total)
    for r, total in zip(rows, totals):
        embedded_ref[r, :] = total
        normed = layer_norm(total).astype(BF16)
        queries_ref[r, :] = (dot(normed, weights[0]) * scale).astype(BF16)
        keys_ref[r, :] = dot(normed, weights[1]).astype(BF16)
        values_ref[r, :] = dot(normed, weights[2]).astype(BF16)


def embed_and_project(ids, masks, own, halves, half, pieces, scale, tile):
    frames, others = ids.shape
    width = own.shape[1]
    chunks = len(pieces)
    outer, three, _, columns = pieces[0][0].shape
    columns *= chunks
    row_block = lambda i: (i, 0)
    return pl.pallas_call(
        functools.partial(project_kernel, others, chunks, scale),
        grid=(frames // tile,),
        in_specs=[
            pl.BlockSpec((tile, others), row_block),
            pl.BlockSpec(masks.shape, lambda i: (0, 0)),
            pl.BlockSpec((tile, width), row_block),
        ]
        + [ANY] * (2 * others + 4 * chunks),
        out_specs=[pl.BlockSpec((tile, width), row_block)]
        + [pl.BlockSpec((tile, columns), row_block)] * 3,
        out_shape=[jax.ShapeDtypeStruct((frames, width), F32)]
        + [jax.ShapeDtypeStruct((frames, columns), BF16)] * 3,
        scratch_shapes=[
            pltpu.VMEM((2 * others * half, width), BF16),
            pltpu.VMEM((three, width, columns), BF16),
            pltpu.SemaphoreType.DMA((2 * others,)),
            pltpu.SemaphoreType.DMA((chunks, 4 * outer)),
        ],
        compiler_params=grant(24 if others == 1 else 44),
        cost_estimate=pl.CostEstimate(
            flops=2 * frames * width * (2 * half * others + three * columns),
            bytes_accessed=20 * 2**20,
            transcendentals=0,
        ),
        name="project",
    )(ids, masks, own, *halves, *[piece for chunk in pieces for piece in chunk])


def attention_kernel(head_dim, queries_ref, keys_ref, values_ref, out_ref):
    queries, keys, values = queries_ref[...], keys_ref[...], values_ref[...]
    lane = lax.broadcasted_iota(jnp.int32, (1, 2 * head_dim), 1)
    first = lane < head_dim
    owns = (first, lane >= head_dim)
    scores = [dot_t(jnp.where(own, queries, jnp.zeros_like(queries)), keys) for own in owns]
    sums = []
    for own, score in zip(owns, scores):
        blocks = [score[:, at : at + 128] for at in range(0, score.shape[1], 128)]
        top = functools.reduce(jnp.maximum, blocks)
        top = jnp.max(top, axis=1, keepdims=True)
        weights = jnp.exp2(score - top).astype(BF16)
        sums.append(dot(weights, jnp.where(own, values, jnp.ones_like(values))))
    mixed = jnp.where(first, sums[0], sums[1])
    total = pltpu.roll(jnp.where(first, sums[1], sums[0]), head_dim, 1)
    out_ref[...] = (mixed / total).astype(BF16)


def attend(queries, keys, values, quarter, tile, head_dim):
    frames, columns = queries.shape
    width = 2 * head_dim
    return pl.pallas_call(
        functools.partial(attention_kernel, head_dim),
        grid=(columns // width,),
        in_specs=[
            pl.BlockSpec((tile, width), lambda p: (quarter, p)),
            pl.BlockSpec((frames, width), lambda p: (0, p)),
            pl.BlockSpec((frames, width), lambda p: (0, p)),
        ],
        out_specs=pl.BlockSpec((tile, width), lambda p: (0, p)),
        out_shape=jax.ShapeDtypeStruct((tile, columns), BF16),
        compiler_params=grant(20),
        cost_estimate=pl.CostEstimate(
            flops=16 * tile * frames * columns, bytes_accessed=2**22, transcendentals=0
        ),
        name="attend",
    )(queries, keys, values)


def gate_kernel(quarters, groups, width, embedded_ref, *refs):
    att_refs = refs[: quarters * groups]
    late = refs[quarters * groups :][:8]
    after_ref, gated_ref, attended, packed, sems = refs[quarters * groups + 8 :]
    step = pl.program_id(0)
    first = piece_copies(late[:4], lambda rows: packed.at[rows, pl.ds(0, 2 * width)], sems.at[0])
    second = piece_copies(
        [ref.at[:, :, pl.ds(0, width)] for ref in late[4:]],
        lambda rows: packed.at[rows, pl.ds(2 * width, width)],
        sems.at[1],
    )
    copies = first + second

    @pl.when(step == 0)
    def _():
        for copy in copies:
            copy.start()

    piece = att_refs[0].shape[1]
    for quarter in range(quarters):

        @pl.when(step == quarter)
        def _():
            for group in range(groups):
                attended[:, group * piece : (group + 1) * piece] = att_refs[quarter * groups + group][...]

    @pl.when(step == 0)
    def _():
        for copy in copies:
            copy.wait()

    part = embedded_ref.shape[0] // 2
    rows = [slice(sub * part, (sub + 1) * part) for sub in range(2)]
    afters = [embedded_ref[r, :] + dot_t(attended[r, :], packed[:, :width]) for r in rows]
    linears = []
    for r, after in zip(rows, afters):
        after_ref[r, :] = after
        linears.append(dot(layer_norm(after).astype(BF16), packed[:, width:]))
    for r, linear in zip(rows, linears):
        gated_ref[r, :] = (linear[:, :width] * gate_of(linear[:, width:])).astype(BF16)


def gate(embedded, attended, late, first, tile):
    width = embedded.shape[1]
    quarters, groups = len(attended), len(attended[0])
    flat = [part for parts in attended for part in parts]
    rows = quarters * tile
    return pl.pallas_call(
        functools.partial(gate_kernel, quarters, groups, width),
        grid=(quarters,),
        in_specs=[pl.BlockSpec((tile, width), lambda i: (first + i, 0))]
        + [pl.BlockSpec(part.shape, lambda i: (0, 0)) for part in flat]
        + [ANY] * len(late),
        out_specs=[pl.BlockSpec((tile, width), lambda i: (i, 0))] * 2,
        out_shape=[
            jax.ShapeDtypeStruct((rows, width), F32),
            jax.ShapeDtypeStruct((rows, width), BF16),
        ],
        scratch_shapes=[
            pltpu.VMEM((tile, width), BF16),
            pltpu.VMEM((width, 3 * width), BF16),
            pltpu.SemaphoreType.DMA((2, 4 * late[0].shape[0])),
        ],
        compiler_params=grant(22),
        cost_estimate=pl.CostEstimate(
            flops=6 * rows * width * width, bytes_accessed=12 * 2**20, transcendentals=0
        ),
        name="gate",
    )(embedded, *flat, *late)


def finish_kernel(tiles, halves, *refs):
    gated_refs, after_refs = refs[: 3 * halves], refs[3 * halves : 4 * halves]
    late = refs[4 * halves :][:4]
    depth_ref, head_ref, out_ref, window, residual, project, head, sems, head_sem = refs[4 * halves + 4 :]
    step = pl.program_id(0)
    tile, width = residual.shape
    taps = depth_ref.shape[0]
    edge = 8
    copies = piece_copies(
        [ref.at[:, :, pl.ds(width, width)] for ref in late], lambda rows: project.at[rows], sems
    )
    copies.append(pltpu.make_async_copy(head_ref, head, head_sem))

    @pl.when(step == 0)
    def _():
        for copy in copies:
            copy.start()

    per_half = tiles // halves
    for half in range(halves):
        before_ref, here_ref, next_ref = gated_refs[3 * half : 3 * half + 3]

        @pl.when(step // per_half == half)
        def _():
            window[edge : edge + tile, :] = here_ref[...].astype(F32)
            residual[...] = after_refs[half][...]

        @pl.when((step > 0) & ((step - 1) // per_half == half))
        def _():
            window[:edge, :] = before_ref[...].astype(F32)[-edge:, :]

        @pl.when((step < tiles - 1) & ((step + 1) // per_half == half))
        def _():
            window[edge + tile :, :] = next_ref[...].astype(F32)[:edge, :]

    @pl.when(step == 0)
    def _():
        window[:edge, :] = jnp.zeros((edge, width), F32)

    @pl.when(step == tiles - 1)
    def _():
        window[edge + tile :, :] = jnp.zeros((edge, width), F32)

    @pl.when(step == 0)
    def _():
        for copy in copies:
            copy.wait()

    part = tile // SUBS

    def activate(first):
        blocks = []
        for at in range(0, width, 128):
            lanes = slice(at, at + 128)
            near = window[first : first + part + 2 * edge, lanes]
            conv = None
            for tap in range(taps):
                start = edge - taps // 2 + tap
                term = near[start : start + part] * depth_ref[tap : tap + 1, lanes].astype(F32)
                conv = term if conv is None else conv + term
            blocks.append((conv * gate_of(conv)).astype(BF16))
        return jnp.concatenate(blocks, axis=1)

    activated = activate(0)
    waiting = None
    for sub in range(SUBS + 1):
        mixed = None
        if sub < SUBS:
            mixed = dot(activated, project[...])
            if sub + 1 < SUBS:
                activated = activate((sub + 1) * part)
        if sub > 0:
            r = slice((sub - 1) * part, sub * part)
            normed = layer_norm(residual[r, :] + waiting).astype(BF16)
            out_ref[r, :] = dot(normed, head[...]).astype(BF16)
        waiting = mixed


def finish(gated, after, late, w_depth, head, tile):
    halves = len(gated)
    half_rows, width = gated[0].shape
    codes = head.shape[1]
    frames = halves * half_rows
    tiles = frames // tile
    per_half = half_rows // tile
    strip = STRIP
    per_tile = tile // strip

    def clip(index, half):
        return jnp.clip(index - half * per_half, 0, per_half - 1)

    specs = []
    for half in range(halves):
        specs += [
            pl.BlockSpec((strip, width), lambda i, half=half: (clip(i - 1, half) * per_tile + per_tile - 1, 0)),
            pl.BlockSpec((tile, width), lambda i, half=half: (clip(i, half), 0)),
            pl.BlockSpec((strip, width), lambda i, half=half: (clip(i + 1, half) * per_tile, 0)),
        ]
    for half in range(halves):
        specs.append(pl.BlockSpec((tile, width), lambda i, half=half: (clip(i, half), 0)))
    return pl.pallas_call(
        functools.partial(finish_kernel, tiles, halves),
        grid=(tiles,),
        in_specs=specs + [ANY] * 4 + [pl.BlockSpec(w_depth.shape, lambda i: (0, 0)), ANY],
        out_specs=pl.BlockSpec((tile, codes), lambda i: (i, 0)),
        out_shape=jax.ShapeDtypeStruct((frames, codes), BF16),
        scratch_shapes=[
            pltpu.VMEM((tile + 16, width), F32),
            pltpu.VMEM((tile, width), F32),
            pltpu.VMEM((width, width), BF16),
            pltpu.VMEM(head.shape, BF16),
            pltpu.SemaphoreType.DMA((4 * late[0].shape[0],)),
            pltpu.SemaphoreType.DMA,
        ],
        compiler_params=grant(22),
        cost_estimate=pl.CostEstimate(
            flops=2 * frames * width * (width + codes), bytes_accessed=20 * 2**20, transcendentals=0
        ),
        name="finish",
    )(*[g for half in gated for g in (half, half, half)], *after, *late, w_depth, head)


def body(
    token_ids,
    decoded_mask,
    levels_done,
    code_tables,
    mask_vectors,
    w_qkv,
    w_out,
    w_expand,
    w_depth,
    w_project,
    level_heads,
):
    return step(
        token_ids[0, 0], decoded_mask[0, 0], levels_done[0], code_tables[0], mask_vectors,
        w_qkv, w_out, w_expand, w_depth, w_project, level_heads[0],
    )[None, None]


def step(
    token_ids, decoded_mask, done, table, own_mask, w_qkv, w_out, w_expand, w_depth, w_project, head,
):
    groups = lax.axis_size("level")
    level_index = lax.axis_index("level")
    frames = token_ids.shape[0]
    codes, width = table.shape
    head_dim = width // HEADS
    half = codes // 2
    core = lax.rem(lax.axis_index("dp"), 2)
    backs = range(1, groups)

    own_out = w_out.T
    columns = own_out.shape[1]
    outs = [own_out] + [from_level(own_out, back) for back in backs]
    late_shards = (
        jnp.concatenate(outs + [w_expand[:, :width]], axis=1),
        jnp.concatenate([w_expand[:, width:], w_project], axis=1),
    )

    use_token = (level_index < done) | ((level_index == done) & (decoded_mask == 1))
    own_ids = jnp.where(use_token, token_ids, -1)
    ids = jnp.stack([from_level(own_ids, back) for back in backs], axis=1)

    mine = lax.dynamic_slice_in_dim(table, core * half, half, 0)
    mine = jnp.concatenate([mine, jnp.broadcast_to(own_mask, (STRIP, width))], axis=0)
    halves, masks = [], []
    for back in backs:
        landed = from_level(mine, back)
        masks.append(landed[half : half + 1])
        halves += [landed, swap(landed, 1)]
    pieces = []
    chunk = columns // CHUNKS if columns % (128 * CHUNKS) == 0 else columns
    for at in range(columns // chunk):
        pieces.append(gather_pieces(w_qkv[:, :, at * chunk : (at + 1) * chunk]))
    late = [gather_pieces(shard) for shard in late_shards]

    tile = frames // QUARTERS
    own = own_term(own_ids[:, None], own_mask, table, tile)
    scale = head_dim ** (-0.5) * LOG2E
    embedded, queries, keys, values = embed_and_project(
        ids, jnp.concatenate(masks), own, halves, half, pieces, scale, tile
    )

    attended = []
    for quarter in range(QUARTERS):
        part = attend(queries, keys, values, quarter, tile, head_dim)
        attended.append([part] + [from_level(part, back) for back in backs])
    after, gated = [], []
    per_half = QUARTERS // 2
    for part in range(2):
        some = attended[part * per_half : (part + 1) * per_half]
        result = gate(embedded, some, late[0] + late[1], part * per_half, tile)
        after.append(result[0])
        gated.append(result[1])
    return finish(gated, after, late[1], w_depth, head, tile)


def solution(mesh):
    return jax.shard_map(
        body,
        mesh=mesh,
        in_specs=(
            P("dp", "level", None),
            P("dp", "level", None),
            P("dp"),
            P("level", None, None),
            P("level", None),
            P(None, "dp", "level"),
            P("level", "dp"),
            P("dp", None),
            P(),
            P("dp", None),
            P("level", None, None),
        ),
        out_specs=P("dp", "level", None, None),
        check_vma=False,
    )
```

time: 181 us -> 238 us (1.31)
  waiting for transfers between devices: 35.4 us -> 109 us
  Pallas kernels: 104 us -> 77.2 us
  starting transfers between devices: 14.5 us -> 38.8 us
  between operations: 14.3 us -> 1.19 us
    ppermute x5 -> x13, waiting for transfers between devices: 3.25 us -> 39.9 us  [swap(): return lax.ppermute(value, 'dp', [(i, i ^ bit) for i in range(devices)])]
    ppermute x7, waiting for transfers between devices: 3.83 us -> 33.5 us  [from_level(): lax.ppermute(value, 'level', [(i, (i + back) % groups) for i in range(gro...]
    ppermute x6 -> x12, starting transfers between devices: 5.43 us -> 27.5 us  [from_outer(): lax.ppermute(value, 'dp', [(i, (i // 4 + back) % outer * 4 + i % 4) for i...]
    ppermute x6 -> x12, waiting for transfers between devices: 28.3 us -> 36.1 us  [from_outer(): lax.ppermute(value, 'dp', [(i, (i // 4 + back) % outer * 4 + i % 4) for i...]
    pallas_call x2, Pallas kernels: 24.8 us -> 17 us  [gate(): pl.pallas_call(functools.partial(gate_kernel, quarters, groups, width), g...]
    pallas_call x2 -> x1, Pallas kernels: 20.1 us -> 12.4 us  [embed_and_project(): pl.pallas_call(functools.partial(project_kernel, others, chunks, scale),...]
    pallas_call x4, Pallas kernels: 33.3 us -> 28.4 us  [attend(): pl.pallas_call(functools.partial(attention_kernel, head_dim), grid=(colum...]
    pallas_call x1, Pallas kernels: 18.6 us -> 14.9 us  [finish(): pl.pallas_call(functools.partial(finish_kernel, tiles, halves), grid=(til...]
  transfers between devices with their start and end apart: 19 -> 32, of which waited for: 8 -> 11; matrix products, arithmetic and copies ran while one was open for 3% -> 2% of each run, Pallas kernels for 41% -> 23%
where the time goes in v3:
time: 238 us; the launch traced here: 237 us
  waiting for transfers between devices  109 us (46%)
  Pallas kernels  77.2 us (32%)
  starting transfers between devices  38.8 us (16%)
  local copies, waits for them, and re-layouts  8.79 us (4%)
    ppermute x13, waiting for transfers between devices, swap(): return lax.ppermute(value, 'dp', [(i, i ^ bit) for i in range(devices)])  39.9 us
    ppermute x12, waiting for transfers between devices, from_outer(): lax.ppermute(value, 'dp', [(i, (i // 4 + back) % outer * 4 + i % 4) for i...  36.1 us
    ppermute x7, waiting for transfers between devices, from_level(): lax.ppermute(value, 'level', [(i, (i + back) % groups) for i in range(gro...  33.5 us
    pallas_call x4, Pallas kernels, attend(): pl.pallas_call(functools.partial(attention_kernel, head_dim), grid=(colum...  28.4 us
    ppermute x12, starting transfers between devices, from_outer(): lax.ppermute(value, 'dp', [(i, (i // 4 + back) % outer * 4 + i % 4) for i...  27.5 us
    pallas_call x2, Pallas kernels, gate(): pl.pallas_call(functools.partial(gate_kernel, quarters, groups, width), g...  17 us
    pallas_call x1, Pallas kernels, finish(): pl.pallas_call(functools.partial(finish_kernel, tiles, halves), grid=(til...  14.9 us
    pallas_call x1, Pallas kernels, embed_and_project(): pl.pallas_call(functools.partial(project_kernel, others, chunks, scale),...  12.4 us
  transfers between devices with their start and end apart: 32, of which 11 were waited for; matrix products, arithmetic and copies ran while one was open for 2% of the time, Pallas kernels for 23%

profile of v3, /device:TPU:14, one launch (start us, length us, event | category | flops | bytes accessed | tf_op | source)
XLA Modules:
  0.0 237.0 jit_solution(6020774393309799079)
XLA Ops:
  0.0 1.0 slice_bitcast_fusion
  1.0 2.7 %collective-permute-start.10 = (bf16[3,64,256]{2,1,0:T(8,128)(2,1)S(1)}, bf16[3,64,256]{2,1,0:T(8,128)(2,1)S(1)}, u32[]{:S(2)}, u32[]{:S(2)}) collective-permute-start(bf16[3,64,256]{2,1,0:T(8,128)(2,1)S(1)} %get-tuple-element.31), channel_id=1, source_target_pairs={{0,16},{2,18},{4,20},{6,22},{8,24},{10,26},{12,28},{14,30},{16,0},... | collective-permute-start | bytes 294920 | tf_op jit(solution)/shard_map/ppermute | solution.py:52
  3.6 0.4 collective-permute-start.11
  4.1 1.6 collective-permute-start.9
  5.7 1.3 dynamic-slice_bitcast_fusion
  7.0 0.0 copy-start.16
  7.1 0.0 copy-start.17
  7.1 1.1 pad_maximum_fusion
  8.2 0.5 collective-permute-start.1
  8.7 1.5 collective-permute-start.17
  10.9 23.6 %collective-permute-done.17 = bf16[64,512]{1,0:T(8,128)(2,1)S(1)} collective-permute-done((bf16[64,512]{1,0:T(8,128)(2,1)S(1)}, bf16[64,512]{1,0:T(8,128)(2,1)S(1)}, u32[]{:S(2)}, u32[]{:S(2)}) %collective-permute-start.17) | collective-permute-done | bytes 65568 | tf_op jit(solution)/shard_map/ppermute | solution.py:59
  34.5 0.3 collective-permute-start.3
  34.9 2.6 %collective-permute-start.4 = (bf16[3,64,256]{2,1,0:T(8,128)(2,1)S(1)}, bf16[3,64,256]{2,1,0:T(8,128)(2,1)S(1)}, u32[]{:S(2)}, u32[]{:S(2)}) collective-permute-start(bf16[3,64,256]{2,1,0:T(8,128)(2,1)S(1)} %get-tuple-element.32), channel_id=1, source_target_pairs={{0,16},{2,18},{4,20},{6,22},{8,24},{10,26},{12,28},{14,30},{16,0},... | collective-permute-start | bytes 294920 | tf_op jit(solution)/shard_map/ppermute | solution.py:52
  37.5 0.7 collective-permute-start.24
  38.1 3.0 %collective-permute-start.25 = (bf16[64,2048]{1,0:T(8,128)(2,1)S(1)}, bf16[64,2048]{1,0:T(8,128)(2,1)S(1)}, u32[]{:S(2)}, u32[]{:S(2)}) collective-permute-start(bf16[64,2048]{1,0:T(8,128)(2,1)S(1)} %get-tuple-element.24), channel_id=1, source_target_pairs={{0,16},{2,18},{4,20},{6,22},{8,24},{10,26},{12,28},{14,30},{16,0},... | collective-permute-start | bytes 786440 | tf_op jit(solution)/shard_map/ppermute | solution.py:52
  41.2 0.9 collective-permute-start.26
  42.1 0.5 collective-permute-done.4
  42.6 13.3 %collective-permute-start.5 = (bf16[3,64,256]{2,1,0:T(8,128)(2,1)S(1)}, bf16[3,64,256]{2,1,0:T(8,128)(2,1)S(1)}, u32[]{:S(2)}, u32[]{:S(2)}) collective-permute-start(bf16[3,64,256]{2,1,0:T(8,128)(2,1)S(1)} %get-tuple-element.32), channel_id=1, source_target_pairs={{0,24},{2,26},{4,28},{6,30},{8,0},{10,2},{12,4},{14,6},{16,8},{18,... | collective-permute-start | bytes 294920 | tf_op jit(solution)/shard_map/ppermute | solution.py:52
  55.9 0.1 pad_maximum_fusion.4.refs_6_
  55.9 16.8 %collective-permute-done.5 = bf16[3,64,256]{2,1,0:T(8,128)(2,1)S(1)} collective-permute-done((bf16[3,64,256]{2,1,0:T(8,128)(2,1)S(1)}, bf16[3,64,256]{2,1,0:T(8,128)(2,1)S(1)}, u32[]{:S(2)}, u32[]{:S(2)}) %collective-permute-start.5) | collective-permute-done | bytes 98336 | tf_op jit(solution)/shard_map/ppermute | solution.py:52
  72.7 2.1 collective-permute-start.20
  74.8 0.1 pad_maximum_fusion.3.refs_2_
  74.9 0.6 collective-permute-start
  75.5 0.1 pad_maximum_fusion.2.refs_8_
  75.6 6.3 %collective-permute-done.18 = bf16[64,2048]{1,0:T(8,128)(2,1)S(1)} collective-permute-done((bf16[64,2048]{1,0:T(8,128)(2,1)S(1)}, bf16[64,2048]{1,0:T(8,128)(2,1)S(1)}, u32[]{:S(2)}, u32[]{:S(2)}) %collective-permute-start.18) | collective-permute-done | bytes 262176 | tf_op jit(solution)/shard_map/ppermute | solution.py:52
  81.9 0.5 collective-permute-start.12
  82.4 12.6 %collective-permute-done.19 = bf16[64,2048]{1,0:T(8,128)(2,1)S(1)} collective-permute-done((bf16[64,2048]{1,0:T(8,128)(2,1)S(1)}, bf16[64,2048]{1,0:T(8,128)(2,1)S(1)}, u32[]{:S(2)}, u32[]{:S(2)}) %collective-permute-start.19) | collective-permute-done | bytes 262176 | tf_op jit(solution)/shard_map/ppermute | solution.py:52
  95.0 0.5 collective-permute-start.6
  95.5 1.5 collective-permute-start.27
  97.0 0.1 pad_maximum_fusion.1.refs_4_
  97.2 0.6 collective-permute-start.21
  97.7 0.2 collective-permute-start.13
  98.0 9.1 %collective-permute-done.6.refs_3_ = bf16[4,3,64,256]{3,2,1,0:T(8,128)(2,1)} collective-permute-done((bf16[4,3,64,256]{3,2,1,0:T(8,128)(2,1)S(1)}, bf16[4,3,64,256]{3,2,1,0:T(8,128)(2,1)}, u32[]{:S(2)}, u32[]{:S(2)}) %collective-permute-start.6) | collective-permute-done | bytes 393248 | tf_op jit(solution)/shard_map/ppermute | solution.py:46
  107.1 0.7 copy-done.7
  107.8 0.5 collective-permute-start.14
  108.3 0.5 collective-permute-done.7.refs_4_
  108.8 0.7 copy-done.9
  109.5 0.1 collective-permute-start.8
  109.7 1.2 copy.12.ids_ref
  110.9 1.1 copy-done.1
  112.0 1.6 copy-done.2
  113.6 4.5 %own_term.1.own_ref = bf16[1536,1024]{1,0:T(8,128)(2,1)S(1)} custom-call(s32[1536,1]{1,0:T(8,128)S(1)} %copy-done.1, bf16[1,1024]{1,0:T(2,128)(2,1)S(1)} %copy-done.6, bf16[1024,1024]{1,0:T(8,128)(2,1)S(1)} %bitcast.31), custom_call_target="tpu_custom_call" | custom-call | flops 3221225472 | bytes 4194304 | tf_op jit(solution)/shard_map/own_term/pallas_call | solution.py:100
  118.1 0.3 stack.84.ids_ref
  118.3 0.7 slice.20.mask_ref
  119.1 0.4 collective-permute-start.28
  119.4 0.1 collective-permute-start.22
  119.6 9.8 %collective-permute-done.27.refs_9_ = bf16[4,64,2048]{2,1,0:T(8,128)(2,1)S(1)} collective-permute-done((bf16[4,64,2048]{2,1,0:T(8,128)(2,1)S(1)}, bf16[4,64,2048]{2,1,0:T(8,128)(2,1)S(1)}, u32[]{:S(2)}, u32[]{:S(2)}) %collective-permute-start.27) | collective-permute-done | bytes 1048608 | tf_op jit(solution)/shard_map/ppermute | solution.py:46
  129.4 20.4 %collective-permute-done.21.refs_5_ = bf16[4,64,2048]{2,1,0:T(8,128)(2,1)} collective-permute-done((bf16[4,64,2048]{2,1,0:T(8,128)(2,1)S(1)}, bf16[4,64,2048]{2,1,0:T(8,128)(2,1)}, u32[]{:S(2)}, u32[]{:S(2)}) %collective-permute-start.21) | collective-permute-done | bytes 1048608 | tf_op jit(solution)/shard_map/ppermute | solution.py:46
  149.9 12.4 %project.1 = (f32[1536,1024]{1,0:T(8,128)S(1)}, bf16[1536,512]{1,0:T(8,128)(2,1)S(1)}, bf16[1536,512]{1,0:T(8,128)(2,1)S(1)}, bf16[1536,512]{1,0:T(8,128)(2,1)S(1)}) custom-call(s32[1536,1]{1,0:T(8,128)S(1)} %stack.84.ids_ref, bf16[1,1024]{1,0:T(2,128)(2,1)S(1)} %slice.20.mask_ref, bf16[1536,1024]{1,0:T(8,128)(2,1)S(1)} %own_term.1.own_ref, ...), custom_call_target="tpu_custom_call" | custom-call | flops 8053063680 | bytes 20971520 | tf_op jit(solution)/shard_map/project/pallas_call | solution.py:177
  162.3 7.1 %attend.7.refs_2_ = bf16[384,512]{1,0:T(8,128)(2,1)S(1)} custom-call(bf16[1536,512]{1,0:T(8,128)(2,1)S(1)} %get-tuple-element.14.queries_ref, bf16[1536,512]{1,0:T(8,128)(2,1)S(1)} %get-tuple-element.15.keys_ref, bf16[1536,512]{1,0:T(8,128)(2,1)S(1)} %get-tuple-element.16.values_ref), custom_call_target="tpu_custom_call" | custom-call | flops 4831838208 | bytes 4194304 | tf_op jit(solution)/shard_map/attend/pallas_call | solution.py:227
  169.4 7.1 %attend.6.refs_0_ = bf16[384,512]{1,0:T(8,128)(2,1)S(1)} custom-call(bf16[1536,512]{1,0:T(8,128)(2,1)S(1)} %get-tuple-element.14.queries_ref, bf16[1536,512]{1,0:T(8,128)(2,1)S(1)} %get-tuple-element.15.keys_ref, bf16[1536,512]{1,0:T(8,128)(2,1)S(1)} %get-tuple-element.16.values_ref), custom_call_target="tpu_custom_call" | custom-call | flops 4831838208 | bytes 4194304 | tf_op jit(solution)/shard_map/attend/pallas_call | solution.py:227
  176.5 0.6 collective-permute-start.31
  177.2 7.1 %attend.5.refs_2_ = bf16[384,512]{1,0:T(8,128)(2,1)S(1)} custom-call(bf16[1536,512]{1,0:T(8,128)(2,1)S(1)} %get-tuple-element.14.queries_ref, bf16[1536,512]{1,0:T(8,128)(2,1)S(1)} %get-tuple-element.15.keys_ref, bf16[1536,512]{1,0:T(8,128)(2,1)S(1)} %get-tuple-element.16.values_ref), custom_call_target="tpu_custom_call" | custom-call | flops 4831838208 | bytes 4194304 | tf_op jit(solution)/shard_map/attend/pallas_call | solution.py:227
  184.3 1.5 collective-permute-start.30
  185.8 7.1 %attend.4.refs_0_ = bf16[384,512]{1,0:T(8,128)(2,1)S(1)} custom-call(bf16[1536,512]{1,0:T(8,128)(2,1)S(1)} %get-tuple-element.14.queries_ref, bf16[1536,512]{1,0:T(8,128)(2,1)S(1)} %get-tuple-element.15.keys_ref, bf16[1536,512]{1,0:T(8,128)(2,1)S(1)} %get-tuple-element.16.values_ref), custom_call_target="tpu_custom_call" | custom-call | flops 4831838208 | bytes 4194304 | tf_op jit(solution)/shard_map/attend/pallas_call | solution.py:227
  192.9 0.6 collective-permute-start.16
  193.6 1.5 collective-permute-start.15
  195.0 2.0 collective-permute-done.30.refs_1_
  197.0 8.5 %gate.3 = (f32[768,1024]{1,0:T(8,128)S(1)}, bf16[768,1024]{1,0:T(8,128)(2,1)S(1)}) custom-call(f32[1536,1024]{1,0:T(8,128)S(1)} %get-tuple-element.13.embedded_ref, bf16[384,512]{1,0:T(8,128)(2,1)S(1)} %attend.6.refs_0_, bf16[384,512]{1,0:T(8,128)(2,1)S(1)} %collective-permute-done.30.refs_1_, bf16[384,512]{1,0:T(8,128)(2,1)S(1)} %attend.7.refs_2_, ...), custom_call_target="tpu_custom_call" | custom-call | flops 4831838208 | bytes 12582912 | tf_op jit(solution)/shard_map/gate/pallas_call | solution.py:292
  205.5 0.0 copy-start
  205.5 0.0 copy-start.5
  205.5 7.9 %collective-permute-done.15.refs_1_ = bf16[384,512]{1,0:T(8,128)(2,1)S(1)} collective-permute-done((bf16[384,512]{1,0:T(8,128)(2,1)S(1)}, bf16[384,512]{1,0:T(8,128)(2,1)S(1)}, u32[]{:S(2)}, u32[]{:S(2)}) %collective-permute-start.15) | collective-permute-done | bytes 393248 | tf_op jit(solution)/shard_map/ppermute | solution.py:59
  213.4 8.5 %gate.2 = (f32[768,1024]{1,0:T(8,128)S(1)}, bf16[768,1024]{1,0:T(8,128)(2,1)S(1)}) custom-call(f32[1536,1024]{1,0:T(8,128)S(1)} %get-tuple-element.13.embedded_ref, bf16[384,512]{1,0:T(8,128)(2,1)S(1)} %attend.4.refs_0_, bf16[384,512]{1,0:T(8,128)(2,1)S(1)} %collective-permute-done.15.refs_1_, bf16[384,512]{1,0:T(8,128)(2,1)S(1)} %attend.5.refs_2_, ...), custom_call_target="tpu_custom_call" | custom-call | flops 4831838208 | bytes 12582912 | tf_op jit(solution)/shard_map/gate/pallas_call | solution.py:292
  221.9 14.9 %finish.1 = bf16[1536,1024]{1,0:T(8,128)(2,1)} custom-call(bf16[768,1024]{1,0:T(8,128)(2,1)S(1)} %get-tuple-element.17.refs_0_.refs_1_.refs_2_, bf16[768,1024]{1,0:T(8,128)(2,1)S(1)} %get-tuple-element.17.refs_0_.refs_1_.refs_2_, bf16[768,1024]{1,0:T(8,128)(2,1)S(1)} %get-tuple-element.17.refs_0_.refs_1_.refs_2_, ...), custom_call_target="tpu_custom_call" | custom-call | flops 6442450944 | bytes 20971520 | tf_op jit(solution)/shard_map/finish/pallas_call | solution.py:416
  (61 shorter events, 0.3 us)
Async XLA Ops:
  0.0 7.0 %copy-start.6 = (bf16[1,1024]{1,0:T(2,128)(2,1)S(1)}, bf16[1,1024]{1,0:T(2,128)(2,1)}, u32[]{:S(2)}) copy-start(bf16[1,1024]{1,0:T(2,128)(2,1)} %mask_ref.1) | copy-start | bytes 6148
  1.0 33.9 %collective-permute-start.10 = (bf16[3,64,256]{2,1,0:T(8,128)(2,1)S(1)}, bf16[3,64,256]{2,1,0:T(8,128)(2,1)S(1)}, u32[]{:S(2)}, u32[]{:S(2)}) collective-permute-start(bf16[3,64,256]{2,1,0:T(8,128)(2,1)S(1)} %get-tuple-element.31), channel_id=1, source_target_pairs={{0,16},{2,18},{4,20},{6,22},{8,24},{10,26},{12,28},{14,30},{16,0},... | collective-permute-start | bytes 294920 | tf_op jit(solution)/shard_map/ppermute | solution.py:52
  3.6 33.8 %collective-permute-start.11 = (bf16[3,64,256]{2,1,0:T(8,128)(2,1)S(1)}, bf16[3,64,256]{2,1,0:T(8,128)(2,1)S(1)}, u32[]{:S(2)}, u32[]{:S(2)}) collective-permute-start(bf16[3,64,256]{2,1,0:T(8,128)(2,1)S(1)} %get-tuple-element.31), channel_id=1, source_target_pairs={{0,24},{2,26},{4,28},{6,30},{8,0},{10,2},{12,4},{14,6},{16,8},{18,... | collective-permute-start | bytes 294920 | tf_op jit(solution)/shard_map/ppermute | solution.py:52
  4.1 34.0 %collective-permute-start.9 = (bf16[3,64,256]{2,1,0:T(8,128)(2,1)S(1)}, bf16[3,64,256]{2,1,0:T(8,128)(2,1)S(1)}, u32[]{:S(2)}, u32[]{:S(2)}) collective-permute-start(bf16[3,64,256]{2,1,0:T(8,128)(2,1)S(1)} %get-tuple-element.31), channel_id=1, source_target_pairs={{0,8},{2,10},{4,12},{6,14},{8,16},{10,18},{12,20},{14,22},{16,24},... | collective-permute-start | bytes 294920 | tf_op jit(solution)/shard_map/ppermute | solution.py:52
  5.7 3.0 %copy-start.13 = (bf16[512,64]{0,1:T(8,128)(2,1)S(1)}, bf16[512,64]{0,1:T(8,128)(2,1)}, u32[]{:S(2)}) copy-start(bf16[512,64]{0,1:T(8,128)(2,1)} %param.17) | copy-start | bytes 196612
  5.7 4.5 %copy-start.11 = (bf16[64,2048]{1,0:T(8,128)(2,1)S(1)}, bf16[64,2048]{1,0:T(8,128)(2,1)}, u32[]{:S(2)}) copy-start(bf16[64,2048]{1,0:T(8,128)(2,1)} %param.18) | copy-start | bytes 786436
  5.7 4.5 %copy-start.12 = (bf16[64,1024]{1,0:T(8,128)(2,1)S(1)}, bf16[64,1024]{1,0:T(8,128)(2,1)}, u32[]{:S(2)}) copy-start(bf16[64,1024]{1,0:T(8,128)(2,1)} %param.20) | copy-start | bytes 393220
  7.0 27.8 %copy-start.16 = (s32[1,1,1536]{2,1,0:T(1,128)S(1)}, s32[1,1,1536]{2,1,0:T(1,128)}, u32[]{:S(2)}) copy-start(s32[1,1,1536]{2,1,0:T(1,128)} %param.11) | copy-start | bytes 18436
  7.1 27.8 %copy-start.17 = (s32[1,1,1536]{2,1,0:T(1,128)S(1)}, s32[1,1,1536]{2,1,0:T(1,128)}, u32[]{:S(2)}) copy-start(s32[1,1,1536]{2,1,0:T(1,128)} %param.12) | copy-start | bytes 18436
  8.2 88.8 %collective-permute-start.1 = (bf16[528,1024]{1,0:T(8,128)(2,1)}, bf16[528,1024]{1,0:T(8,128)(2,1)}, u32[]{:S(2)}, u32[]{:S(2)}) collective-permute-start(bf16[528,1024]{1,0:T(8,128)(2,1)} %pad_maximum_fusion), channel_id=1, source_target_pairs={{0,1},{1,0},{2,3},{3,2},{4,5},{5,4},{6,7},{7,6},{8,9},{9,8},{10,11... | collective-permute-start | bytes 3244040 | tf_op jit(solution)/shard_map/ppermute | solution.py:59
  8.7 25.8 %collective-permute-start.17 = (bf16[64,512]{1,0:T(8,128)(2,1)S(1)}, bf16[64,512]{1,0:T(8,128)(2,1)S(1)}, u32[]{:S(2)}, u32[]{:S(2)}) collective-permute-start(bf16[64,512]{1,0:T(8,128)(2,1)S(1)} %bitcast.44), channel_id=1, source_target_pairs={{0,1},{1,0},{2,3},{3,2},{4,5},{5,4},{6,7},{7,6},{8,9},{9,8},{10,11... | collective-permute-start | bytes 196616 | tf_op jit(solution)/shard_map/ppermute | solution.py:59
  34.5 6.7 %collective-permute-start.3 = (bf16[3,64,256]{2,1,0:T(8,128)(2,1)S(1)}, bf16[3,64,256]{2,1,0:T(8,128)(2,1)S(1)}, u32[]{:S(2)}, u32[]{:S(2)}) collective-permute-start(bf16[3,64,256]{2,1,0:T(8,128)(2,1)S(1)} %get-tuple-element.32), channel_id=1, source_target_pairs={{0,8},{2,10},{4,12},{6,14},{8,16},{10,18},{12,20},{14,22},{16,24},... | collective-permute-start | bytes 294920 | tf_op jit(solution)/shard_map/ppermute | solution.py:52
  34.9 7.8 %collective-permute-start.4 = (bf16[3,64,256]{2,1,0:T(8,128)(2,1)S(1)}, bf16[3,64,256]{2,1,0:T(8,128)(2,1)S(1)}, u32[]{:S(2)}, u32[]{:S(2)}) collective-permute-start(bf16[3,64,256]{2,1,0:T(8,128)(2,1)S(1)} %get-tuple-element.32), channel_id=1, source_target_pairs={{0,16},{2,18},{4,20},{6,22},{8,24},{10,26},{12,28},{14,30},{16,0},... | collective-permute-start | bytes 294920 | tf_op jit(solution)/shard_map/ppermute | solution.py:52
  37.5 35.3 %collective-permute-start.24 = (bf16[64,2048]{1,0:T(8,128)(2,1)S(1)}, bf16[64,2048]{1,0:T(8,128)(2,1)S(1)}, u32[]{:S(2)}, u32[]{:S(2)}) collective-permute-start(bf16[64,2048]{1,0:T(8,128)(2,1)S(1)} %get-tuple-element.24), channel_id=1, source_target_pairs={{0,8},{2,10},{4,12},{6,14},{8,16},{10,18},{12,20},{14,22},{16,24},... | collective-permute-start | bytes 786440 | tf_op jit(solution)/shard_map/ppermute | solution.py:52
  38.1 34.6 %collective-permute-start.25 = (bf16[64,2048]{1,0:T(8,128)(2,1)S(1)}, bf16[64,2048]{1,0:T(8,128)(2,1)S(1)}, u32[]{:S(2)}, u32[]{:S(2)}) collective-permute-start(bf16[64,2048]{1,0:T(8,128)(2,1)S(1)} %get-tuple-element.24), channel_id=1, source_target_pairs={{0,16},{2,18},{4,20},{6,22},{8,24},{10,26},{12,28},{14,30},{16,0},... | collective-permute-start | bytes 786440 | tf_op jit(solution)/shard_map/ppermute | solution.py:52
  41.2 33.7 %collective-permute-start.26 = (bf16[64,2048]{1,0:T(8,128)(2,1)S(1)}, bf16[64,2048]{1,0:T(8,128)(2,1)S(1)}, u32[]{:S(2)}, u32[]{:S(2)}) collective-permute-start(bf16[64,2048]{1,0:T(8,128)(2,1)S(1)} %get-tuple-element.24), channel_id=1, source_target_pairs={{0,24},{2,26},{4,28},{6,30},{8,0},{10,2},{12,4},{14,6},{16,8},{18,... | collective-permute-start | bytes 786440 | tf_op jit(solution)/shard_map/ppermute | solution.py:52
  42.6 30.1 %collective-permute-start.5 = (bf16[3,64,256]{2,1,0:T(8,128)(2,1)S(1)}, bf16[3,64,256]{2,1,0:T(8,128)(2,1)S(1)}, u32[]{:S(2)}, u32[]{:S(2)}) collective-permute-start(bf16[3,64,256]{2,1,0:T(8,128)(2,1)S(1)} %get-tuple-element.32), channel_id=1, source_target_pairs={{0,24},{2,26},{4,28},{6,30},{8,0},{10,2},{12,4},{14,6},{16,8},{18,... | collective-permute-start | bytes 294920 | tf_op jit(solution)/shard_map/ppermute | solution.py:52
  72.7 9.2 %collective-permute-start.18 = (bf16[64,2048]{1,0:T(8,128)(2,1)S(1)}, bf16[64,2048]{1,0:T(8,128)(2,1)S(1)}, u32[]{:S(2)}, u32[]{:S(2)}) collective-permute-start(bf16[64,2048]{1,0:T(8,128)(2,1)S(1)} %get-tuple-element.28), channel_id=1, source_target_pairs={{0,8},{2,10},{4,12},{6,14},{8,16},{10,18},{12,20},{14,22},{16,24},... | collective-permute-start | bytes 786440 | tf_op jit(solution)/shard_map/ppermute | solution.py:52
  72.7 22.3 %collective-permute-start.19 = (bf16[64,2048]{1,0:T(8,128)(2,1)S(1)}, bf16[64,2048]{1,0:T(8,128)(2,1)S(1)}, u32[]{:S(2)}, u32[]{:S(2)}) collective-permute-start(bf16[64,2048]{1,0:T(8,128)(2,1)S(1)} %get-tuple-element.28), channel_id=1, source_target_pairs={{0,16},{2,18},{4,20},{6,22},{8,24},{10,26},{12,28},{14,30},{16,0},... | collective-permute-start | bytes 786440 | tf_op jit(solution)/shard_map/ppermute | solution.py:52
  72.7 22.7 %collective-permute-start.20 = (bf16[64,2048]{1,0:T(8,128)(2,1)S(1)}, bf16[64,2048]{1,0:T(8,128)(2,1)S(1)}, u32[]{:S(2)}, u32[]{:S(2)}) collective-permute-start(bf16[64,2048]{1,0:T(8,128)(2,1)S(1)} %get-tuple-element.28), channel_id=1, source_target_pairs={{0,24},{2,26},{4,28},{6,30},{8,0},{10,2},{12,4},{14,6},{16,8},{18,... | collective-permute-start | bytes 786440 | tf_op jit(solution)/shard_map/ppermute | solution.py:52
  74.9 32.2 %copy-start.3 = (bf16[4,3,64,256]{3,2,1,0:T(8,128)(2,1)}, bf16[4,3,64,256]{3,2,1,0:T(8,128)(2,1)S(1)}, u32[]{:S(2)}) copy-start(bf16[4,3,64,256]{3,2,1,0:T(8,128)(2,1)S(1)} %pad_maximum_fusion.3.refs_2_) | copy-start | bytes 1179652
  74.9 22.3 %collective-permute-start = (s32[1536]{0:T(1024)S(1)}, s32[1536]{0:T(1024)S(1)}, u32[]{:S(2)}, u32[]{:S(2)}) collective-permute-start(s32[1536]{0:T(1024)S(1)} %get-tuple-element.21), channel_id=1, source_target_pairs={{0,1},{1,0},{2,3},{3,2},{4,5},{5,4},{6,7},{7,6},{8,9},{9,8},{10,11... | collective-permute-start | bytes 18440 | tf_op jit(solution)/shard_map/ppermute | solution.py:59
  81.9 15.8 %collective-permute-start.12 = (bf16[4,3,64,256]{3,2,1,0:T(8,128)(2,1)S(1)}, bf16[4,3,64,256]{3,2,1,0:T(8,128)(2,1)}, u32[]{:S(2)}, u32[]{:S(2)}) collective-permute-start(bf16[4,3,64,256]{3,2,1,0:T(8,128)(2,1)S(1)} %pad_maximum_fusion.4.refs_6_), channel_id=1, source_target_pairs={{0,4},{2,6},{4,0},{6,2},{8,12},{10,14},{12,8},{14,10},{16,20},{18,... | collective-permute-start | bytes 1179656 | tf_op jit(solution)/shard_map/ppermute | solution.py:46
  95.0 12.1 %collective-permute-start.6 = (bf16[4,3,64,256]{3,2,1,0:T(8,128)(2,1)S(1)}, bf16[4,3,64,256]{3,2,1,0:T(8,128)(2,1)}, u32[]{:S(2)}, u32[]{:S(2)}) collective-permute-start(bf16[4,3,64,256]{3,2,1,0:T(8,128)(2,1)S(1)} %pad_maximum_fusion.3.refs_2_), channel_id=1, source_target_pairs={{0,4},{2,6},{4,0},{6,2},{8,12},{10,14},{12,8},{14,10},{16,20},{18,... | collective-permute-start | bytes 1179656 | tf_op jit(solution)/shard_map/ppermute | solution.py:46
  95.5 33.9 %collective-permute-start.27 = (bf16[4,64,2048]{2,1,0:T(8,128)(2,1)S(1)}, bf16[4,64,2048]{2,1,0:T(8,128)(2,1)S(1)}, u32[]{:S(2)}, u32[]{:S(2)}) collective-permute-start(bf16[4,64,2048]{2,1,0:T(8,128)(2,1)S(1)} %pad_maximum_fusion.2.refs_8_), channel_id=1, source_target_pairs={{0,4},{2,6},{4,0},{6,2},{8,12},{10,14},{12,8},{14,10},{16,20},{18,... | collective-permute-start | bytes 3145736 | tf_op jit(solution)/shard_map/ppermute | solution.py:46
  97.0 52.9 %collective-permute-start.2 = (bf16[528,1024]{1,0:T(8,128)(2,1)}, bf16[528,1024]{1,0:T(8,128)(2,1)}, u32[]{:S(2)}, u32[]{:S(2)}) collective-permute-start(bf16[528,1024]{1,0:T(8,128)(2,1)} %collective-permute-done.1.refs_0_), channel_id=1, source_target_pairs={{0,2},{2,0},{4,6},{6,4},{8,10},{10,8},{12,14},{14,12},{16,18},{18,... | collective-permute-start | bytes 3244040 | tf_op jit(solution)/shard_map/ppermute | solution.py:46
  97.2 11.6 %copy-start.14 = (s32[1536]{0:T(1024)}, s32[1536]{0:T(1024)S(1)}, u32[]{:S(2)}) copy-start(s32[1536]{0:T(1024)S(1)} %collective-permute-done) | copy-start | bytes 18436
  97.2 52.7 %collective-permute-start.21 = (bf16[4,64,2048]{2,1,0:T(8,128)(2,1)S(1)}, bf16[4,64,2048]{2,1,0:T(8,128)(2,1)}, u32[]{:S(2)}, u32[]{:S(2)}) collective-permute-start(bf16[4,64,2048]{2,1,0:T(8,128)(2,1)S(1)} %pad_maximum_fusion.1.refs_4_), channel_id=1, source_target_pairs={{0,4},{2,6},{4,0},{6,2},{8,12},{10,14},{12,8},{14,10},{16,20},{18,... | collective-permute-start | bytes 3145736 | tf_op jit(solution)/shard_map/ppermute | solution.py:46
  97.7 9.3 %collective-permute-start.13 = (bf16[4,3,64,256]{3,2,1,0:T(8,128)(2,1)S(1)}, bf16[4,3,64,256]{3,2,1,0:T(8,128)(2,1)S(1)}, u32[]{:S(2)}, u32[]{:S(2)}) collective-permute-start(bf16[4,3,64,256]{3,2,1,0:T(8,128)(2,1)S(1)} %pad_maximum_fusion.4.refs_6_), channel_id=1, source_target_pairs={{0,2},{2,0},{4,6},{6,4},{8,10},{10,8},{12,14},{14,12},{16,18},{18,... | collective-permute-start | bytes 1179656 | tf_op jit(solution)/shard_map/ppermute | solution.py:46
  107.1 1.7 collective-permute-start.7
  107.1 0.7 copy-start.7
  107.8 11.2 %collective-permute-start.14 = (bf16[4,3,64,256]{3,2,1,0:T(8,128)(2,1)}, bf16[4,3,64,256]{3,2,1,0:T(8,128)(2,1)}, u32[]{:S(2)}, u32[]{:S(2)}) collective-permute-start(bf16[4,3,64,256]{3,2,1,0:T(8,128)(2,1)} %collective-permute-done.12.refs_7_), channel_id=1, source_target_pairs={{0,2},{2,0},{4,6},{6,4},{8,10},{10,8},{12,14},{14,12},{16,18},{18,... | collective-permute-start | bytes 1179656 | tf_op jit(solution)/shard_map/ppermute | solution.py:46
  108.8 0.7 copy-start.9
  109.5 9.9 %collective-permute-start.8 = (bf16[4,3,64,256]{3,2,1,0:T(8,128)(2,1)}, bf16[4,3,64,256]{3,2,1,0:T(8,128)(2,1)}, u32[]{:S(2)}, u32[]{:S(2)}) collective-permute-start(bf16[4,3,64,256]{3,2,1,0:T(8,128)(2,1)} %collective-permute-done.6.refs_3_), channel_id=1, source_target_pairs={{0,2},{2,0},{4,6},{6,4},{8,10},{10,8},{12,14},{14,12},{16,18},{18,... | collective-permute-start | bytes 1179656 | tf_op jit(solution)/shard_map/ppermute | solution.py:46
  110.9 1.1 copy-start.1
  112.0 1.6 copy-start.2
  113.6 4.5 %copy-start.15 = (s32[1536]{0:T(1024)S(1)}, s32[1536]{0:T(1024)}, u32[]{:S(2)}) copy-start(s32[1536]{0:T(1024)} %copy-done.14) | copy-start | bytes 18436
  113.6 36.3 %copy-start.4 = (bf16[4,3,64,256]{3,2,1,0:T(8,128)(2,1)S(1)}, bf16[4,3,64,256]{3,2,1,0:T(8,128)(2,1)}, u32[]{:S(2)}) copy-start(bf16[4,3,64,256]{3,2,1,0:T(8,128)(2,1)} %copy-done.3) | copy-start | bytes 1179652
  113.6 36.3 %copy-start.8 = (bf16[4,3,64,256]{3,2,1,0:T(8,128)(2,1)S(1)}, bf16[4,3,64,256]{3,2,1,0:T(8,128)(2,1)}, u32[]{:S(2)}) copy-start(bf16[4,3,64,256]{3,2,1,0:T(8,128)(2,1)} %copy-done.7) | copy-start | bytes 1179652
  113.6 36.3 %copy-start.10 = (bf16[4,3,64,256]{3,2,1,0:T(8,128)(2,1)S(1)}, bf16[4,3,64,256]{3,2,1,0:T(8,128)(2,1)}, u32[]{:S(2)}) copy-start(bf16[4,3,64,256]{3,2,1,0:T(8,128)(2,1)} %copy-done.9) | copy-start | bytes 1179652
  119.1 65.2 %collective-permute-start.28 = (bf16[4,64,2048]{2,1,0:T(8,128)(2,1)S(1)}, bf16[4,64,2048]{2,1,0:T(8,128)(2,1)S(1)}, u32[]{:S(2)}, u32[]{:S(2)}) collective-permute-start(bf16[4,64,2048]{2,1,0:T(8,128)(2,1)S(1)} %pad_maximum_fusion.2.refs_8_), channel_id=1, source_target_pairs={{0,2},{2,0},{4,6},{6,4},{8,10},{10,8},{12,14},{14,12},{16,18},{18,... | collective-permute-start | bytes 3145736 | tf_op jit(solution)/shard_map/ppermute | solution.py:46
  119.4 73.5 %collective-permute-start.22 = (bf16[4,64,2048]{2,1,0:T(8,128)(2,1)S(1)}, bf16[4,64,2048]{2,1,0:T(8,128)(2,1)S(1)}, u32[]{:S(2)}, u32[]{:S(2)}) collective-permute-start(bf16[4,64,2048]{2,1,0:T(8,128)(2,1)S(1)} %pad_maximum_fusion.1.refs_4_), channel_id=1, source_target_pairs={{0,2},{2,0},{4,6},{6,4},{8,10},{10,8},{12,14},{14,12},{16,18},{18,... | collective-permute-start | bytes 3145736 | tf_op jit(solution)/shard_map/ppermute | solution.py:46
  129.4 64.1 %collective-permute-start.29 = (bf16[4,64,2048]{2,1,0:T(8,128)(2,1)S(1)}, bf16[4,64,2048]{2,1,0:T(8,128)(2,1)S(1)}, u32[]{:S(2)}, u32[]{:S(2)}) collective-permute-start(bf16[4,64,2048]{2,1,0:T(8,128)(2,1)S(1)} %collective-permute-done.27.refs_9_), channel_id=1, source_target_pairs={{0,2},{2,0},{4,6},{6,4},{8,10},{10,8},{12,14},{14,12},{16,18},{18,... | collective-permute-start | bytes 3145736 | tf_op jit(solution)/shard_map/ppermute | solution.py:46
  149.9 45.2 %collective-permute-start.23 = (bf16[4,64,2048]{2,1,0:T(8,128)(2,1)}, bf16[4,64,2048]{2,1,0:T(8,128)(2,1)S(1)}, u32[]{:S(2)}, u32[]{:S(2)}) collective-permute-start(bf16[4,64,2048]{2,1,0:T(8,128)(2,1)} %collective-permute-done.21.refs_5_), channel_id=1, source_target_pairs={{0,2},{2,0},{4,6},{6,4},{8,10},{10,8},{12,14},{14,12},{16,18},{18,... | collective-permute-start | bytes 3145736 | tf_op jit(solution)/shard_map/ppermute | solution.py:46
  176.5 18.5 %collective-permute-start.31 = (bf16[384,512]{1,0:T(8,128)(2,1)S(1)}, bf16[384,512]{1,0:T(8,128)(2,1)S(1)}, u32[]{:S(2)}, u32[]{:S(2)}) collective-permute-start(bf16[384,512]{1,0:T(8,128)(2,1)S(1)} %attend.7.refs_2_), channel_id=1, source_target_pairs={{0,1},{1,0},{2,3},{3,2},{4,5},{5,4},{6,7},{7,6},{8,9},{9,8},{10,11... | collective-permute-start | bytes 1179656 | tf_op jit(solution)/shard_map/ppermute | solution.py:59
  184.3 12.7 %collective-permute-start.30 = (bf16[384,512]{1,0:T(8,128)(2,1)S(1)}, bf16[384,512]{1,0:T(8,128)(2,1)S(1)}, u32[]{:S(2)}, u32[]{:S(2)}) collective-permute-start(bf16[384,512]{1,0:T(8,128)(2,1)S(1)} %attend.6.refs_0_), channel_id=1, source_target_pairs={{0,1},{1,0},{2,3},{3,2},{4,5},{5,4},{6,7},{7,6},{8,9},{9,8},{10,11... | collective-permute-start | bytes 1179656 | tf_op jit(solution)/shard_map/ppermute | solution.py:59
  192.9 12.6 %collective-permute-start.16 = (bf16[384,512]{1,0:T(8,128)(2,1)S(1)}, bf16[384,512]{1,0:T(8,128)(2,1)S(1)}, u32[]{:S(2)}, u32[]{:S(2)}) collective-permute-start(bf16[384,512]{1,0:T(8,128)(2,1)S(1)} %attend.5.refs_2_), channel_id=1, source_target_pairs={{0,1},{1,0},{2,3},{3,2},{4,5},{5,4},{6,7},{7,6},{8,9},{9,8},{10,11... | collective-permute-start | bytes 1179656 | tf_op jit(solution)/shard_map/ppermute | solution.py:59
  193.6 19.9 %collective-permute-start.15 = (bf16[384,512]{1,0:T(8,128)(2,1)S(1)}, bf16[384,512]{1,0:T(8,128)(2,1)S(1)}, u32[]{:S(2)}, u32[]{:S(2)}) collective-permute-start(bf16[384,512]{1,0:T(8,128)(2,1)S(1)} %attend.4.refs_0_), channel_id=1, source_target_pairs={{0,1},{1,0},{2,3},{3,2},{4,5},{5,4},{6,7},{7,6},{8,9},{9,8},{10,11... | collective-permute-start | bytes 1179656 | tf_op jit(solution)/shard_map/ppermute | solution.py:59
  205.5 16.4 %copy-start = (bf16[1,1024,1024]{2,1,0:T(8,128)(2,1)S(1)}, bf16[1,1024,1024]{2,1,0:T(8,128)(2,1)}, u32[]{:S(2)}) copy-start(bf16[1,1024,1024]{2,1,0:T(8,128)(2,1)} %param.21) | copy-start | bytes 6291460
  205.5 16.4 %copy-start.5 = (bf16[5,1024]{1,0:T(8,128)(2,1)S(1)}, bf16[5,1024]{1,0:T(8,128)(2,1)}, u32[]{:S(2)}) copy-start(bf16[5,1024]{1,0:T(8,128)(2,1)} %refs_12_.1) | copy-start | bytes 30724

commit v4 on v3

--- a/solution.py
+++ b/solution.py
@@ -9,14 +9,15 @@
 
 
 HEADS = 16
+DP, LEVEL = "dp", "level"
 LOG2E = 1.4426950408889634
 BF16 = jnp.bfloat16
 F32 = jnp.float32
-ANY = pl.BlockSpec(memory_space=pl.ANY)
+WHOLE = pl.BlockSpec(memory_space=pltpu.VMEM)
 QUARTERS = 4
 CHUNKS = 2
 STRIP = 16
-SUBS = 3
+SUBS = 2
 
 
 def grant(mebibytes):
@@ -42,44 +43,44 @@
 
 
 def swap(value, bit):
-    devices = lax.axis_size("dp")
-    return lax.ppermute(value, "dp", [(i, i ^ bit) for i in range(devices)])
+    devices = lax.axis_size(DP)
+    return lax.ppermute(value, DP, [(i, i ^ bit) for i in range(devices)])
 
 
 def from_outer(value, back):
-    devices = lax.axis_size("dp")
+    devices = lax.axis_size(DP)
     outer = devices // 4
     return lax.ppermute(
-        value, "dp", [(i, ((i // 4 + back) % outer) * 4 + i % 4) for i in range(devices)]
+        value, DP, [(i, ((i // 4 + back) % outer) * 4 + i % 4) for i in range(devices)]
     )
 
 
 def from_level(value, back):
-    groups = lax.axis_size("level")
-    return lax.ppermute(value, "level", [(i, (i + back) % groups) for i in range(groups)])
-
-
-def gather_pieces(shard):
-    outer = lax.axis_size("dp") // 4
-    near = [shard] + [from_outer(shard, back) for back in range(1, outer)]
+    groups = lax.axis_size(LEVEL)
+    return lax.ppermute(value, LEVEL, [(i, (i + back) % groups) for i in range(groups)])
+
+
+def gather_outer(shard):
+    outer = lax.axis_size(DP) // 4
+    return [shard] + [from_outer(shard, back) for back in range(1, outer)]
+
+
+def gather_chip_pairs(near):
     near = jnp.stack(near)
     far = swap(near, 2)
     return near, far, swap(near, 1), swap(far, 1)
 
 
-def piece_copies(pieces, place, sems):
+def place_pieces(pieces, target, lanes):
     outer, rows_here = pieces[0].shape[0], pieces[0].shape[-2]
-    copies = []
     for side, piece in enumerate(pieces):
         for back in range(outer):
-            row = piece_owner(back, side % 2, side // 2) * rows_here
-            target = place(pl.ds(row, rows_here))
-            copies.append(pltpu.make_async_copy(piece.at[back], target, sems.at[len(copies)]))
-    return copies
+            row = pl.multiple_of(piece_owner(back, side % 2, side // 2) * rows_here, rows_here)
+            target[pl.ds(row, rows_here), lanes] = piece[back]
 
 
 def piece_owner(back, pair, core):
-    index, outer = lax.axis_index("dp"), lax.axis_size("dp") // 4
+    index, outer = lax.axis_index(DP), lax.axis_size(DP) // 4
     source = lax.rem(index // 4 + outer - back, outer)
     own_pair, own_core = lax.rem(index // 2, 2), lax.rem(index, 2)
     return source * 4 + (1 - own_pair if pair else own_pair) * 2 + (1 - own_core if core else own_core)
@@ -118,33 +119,23 @@
 def project_kernel(others, chunks, scale, ids_ref, mask_ref, own_ref, *refs):
     halves, pieces = refs[: 2 * others], refs[2 * others : 2 * others + 4 * chunks]
     embedded_ref, queries_ref, keys_ref, values_ref = refs[2 * others + 4 * chunks :][:4]
-    tables, weights, table_sems, weight_sems = refs[2 * others + 4 * chunks + 4 :]
+    tables, weights = refs[2 * others + 4 * chunks + 4 :]
     codes = tables.shape[0] // others
     half = codes // 2
-    core = lax.rem(lax.axis_index("dp"), 2)
-    copies = []
-    for index, source in enumerate(halves):
-        base, side = (index // 2) * codes, index % 2
-        place = base + (core if side == 0 else 1 - core) * half
-        target = tables.at[pl.ds(place, half)]
-        copies.append(
-            pltpu.make_async_copy(source.at[pl.ds(0, half)], target, table_sems.at[index])
-        )
-    columns = pieces[0].shape[-1]
-    for chunk in range(chunks):
-        lanes = pl.ds(chunk * columns, columns)
-        copies += piece_copies(
-            pieces[4 * chunk : 4 * chunk + 4],
-            lambda rows, lanes=lanes: weights.at[:, rows, lanes],
-            weight_sems.at[chunk],
-        )
+    core = lax.rem(lax.axis_index(DP), 2)
 
     @pl.when(pl.program_id(0) == 0)
     def _():
-        for copy in copies:
-            copy.start()
-        for copy in copies:
-            copy.wait()
+        for index, source in enumerate(halves):
+            side = core if index % 2 == 0 else 1 - core
+            place = pl.multiple_of((index // 2) * codes + side * half, half)
+            tables[pl.ds(place, half), :] = source[:half, :]
+        columns = pieces[0].shape[-1]
+        for chunk in range(chunks):
+            lanes = slice(chunk * columns, (chunk + 1) * columns)
+            for matrix in range(weights.shape[0]):
+                some = [ref.at[:, matrix] for ref in pieces[4 * chunk : 4 * chunk + 4]]
+                place_pieces(some, weights.at[matrix], lanes)
 
     code_row = lax.broadcasted_iota(jnp.int32, (1, codes), 1)
     part = ids_ref.shape[0] // 2
@@ -171,7 +162,7 @@
     frames, others = ids.shape
     width = own.shape[1]
     chunks = len(pieces)
-    outer, three, _, columns = pieces[0][0].shape
+    _, three, _, columns = pieces[0][0].shape
     columns *= chunks
     row_block = lambda i: (i, 0)
     return pl.pallas_call(
@@ -182,7 +173,7 @@
             pl.BlockSpec(masks.shape, lambda i: (0, 0)),
             pl.BlockSpec((tile, width), row_block),
         ]
-        + [ANY] * (2 * others + 4 * chunks),
+        + [WHOLE] * (2 * others + 4 * chunks),
         out_specs=[pl.BlockSpec((tile, width), row_block)]
         + [pl.BlockSpec((tile, columns), row_block)] * 3,
         out_shape=[jax.ShapeDtypeStruct((frames, width), F32)]
@@ -190,10 +181,8 @@
         scratch_shapes=[
             pltpu.VMEM((2 * others * half, width), BF16),
             pltpu.VMEM((three, width, columns), BF16),
-            pltpu.SemaphoreType.DMA((2 * others,)),
-            pltpu.SemaphoreType.DMA((chunks, 4 * outer)),
         ],
-        compiler_params=grant(24 if others == 1 else 44),
+        compiler_params=grant(24 if others == 1 else 60),
         cost_estimate=pl.CostEstimate(
             flops=2 * frames * width * (2 * half * others + three * columns),
             bytes_accessed=20 * 2**20,
@@ -203,8 +192,10 @@
     )(ids, masks, own, *halves, *[piece for chunk in pieces for piece in chunk])
 
 
-def attention_kernel(head_dim, queries_ref, keys_ref, values_ref, out_ref):
-    queries, keys, values = queries_ref[...], keys_ref[...], values_ref[...]
+def attention_kernel(head_dim, quarter, queries_ref, keys_ref, values_ref, out_ref):
+    width = out_ref.shape[1]
+    lanes = pl.ds(pl.multiple_of(pl.program_id(0) * width, width), width)
+    queries, keys, values = queries_ref[quarter, lanes], keys_ref[:, lanes], values_ref[:, lanes]
     lane = lax.broadcasted_iota(jnp.int32, (1, 2 * head_dim), 1)
     first = lane < head_dim
     owns = (first, lane >= head_dim)
@@ -225,13 +216,9 @@
     frames, columns = queries.shape
     width = 2 * head_dim
     return pl.pallas_call(
-        functools.partial(attention_kernel, head_dim),
+        functools.partial(attention_kernel, head_dim, slice(quarter * tile, (quarter + 1) * tile)),
         grid=(columns // width,),
-        in_specs=[
-            pl.BlockSpec((tile, width), lambda p: (quarter, p)),
-            pl.BlockSpec((frames, width), lambda p: (0, p)),
-            pl.BlockSpec((frames, width), lambda p: (0, p)),
-        ],
+        in_specs=[WHOLE] * 3,
         out_specs=pl.BlockSpec((tile, width), lambda p: (0, p)),
         out_shape=jax.ShapeDtypeStruct((tile, columns), BF16),
         compiler_params=grant(20),
@@ -245,20 +232,13 @@
 def gate_kernel(quarters, groups, width, embedded_ref, *refs):
     att_refs = refs[: quarters * groups]
     late = refs[quarters * groups :][:8]
-    after_ref, gated_ref, attended, packed, sems = refs[quarters * groups + 8 :]
+    after_ref, gated_ref, attended, packed = refs[quarters * groups + 8 :]
     step = pl.program_id(0)
-    first = piece_copies(late[:4], lambda rows: packed.at[rows, pl.ds(0, 2 * width)], sems.at[0])
-    second = piece_copies(
-        [ref.at[:, :, pl.ds(0, width)] for ref in late[4:]],
-        lambda rows: packed.at[rows, pl.ds(2 * width, width)],
-        sems.at[1],
-    )
-    copies = first + second
 
     @pl.when(step == 0)
     def _():
-        for copy in copies:
-            copy.start()
+        place_pieces(late[:4], packed, slice(0, 2 * width))
+        place_pieces(late[4:], packed, slice(2 * width, 3 * width))
 
     piece = att_refs[0].shape[1]
     for quarter in range(quarters):
@@ -267,11 +247,6 @@
         def _():
             for group in range(groups):
                 attended[:, group * piece : (group + 1) * piece] = att_refs[quarter * groups + group][...]
-
-    @pl.when(step == 0)
-    def _():
-        for copy in copies:
-            copy.wait()
 
     part = embedded_ref.shape[0] // 2
     rows = [slice(sub * part, (sub + 1) * part) for sub in range(2)]
@@ -294,7 +269,7 @@
         grid=(quarters,),
         in_specs=[pl.BlockSpec((tile, width), lambda i: (first + i, 0))]
         + [pl.BlockSpec(part.shape, lambda i: (0, 0)) for part in flat]
-        + [ANY] * len(late),
+        + [WHOLE] * len(late),
         out_specs=[pl.BlockSpec((tile, width), lambda i: (i, 0))] * 2,
         out_shape=[
             jax.ShapeDtypeStruct((rows, width), F32),
@@ -303,7 +278,6 @@
         scratch_shapes=[
             pltpu.VMEM((tile, width), BF16),
             pltpu.VMEM((width, 3 * width), BF16),
-            pltpu.SemaphoreType.DMA((2, 4 * late[0].shape[0])),
         ],
         compiler_params=grant(22),
         cost_estimate=pl.CostEstimate(
@@ -316,20 +290,15 @@
 def finish_kernel(tiles, halves, *refs):
     gated_refs, after_refs = refs[: 3 * halves], refs[3 * halves : 4 * halves]
     late = refs[4 * halves :][:4]
-    depth_ref, head_ref, out_ref, window, residual, project, head, sems, head_sem = refs[4 * halves + 4 :]
+    depth_ref, head, out_ref, window, residual, project = refs[4 * halves + 4 :]
     step = pl.program_id(0)
     tile, width = residual.shape
     taps = depth_ref.shape[0]
     edge = 8
-    copies = piece_copies(
-        [ref.at[:, :, pl.ds(width, width)] for ref in late], lambda rows: project.at[rows], sems
-    )
-    copies.append(pltpu.make_async_copy(head_ref, head, head_sem))
 
     @pl.when(step == 0)
     def _():
-        for copy in copies:
-            copy.start()
+        place_pieces(late, project, slice(None))
 
     per_half = tiles // halves
     for half in range(halves):
@@ -355,11 +324,6 @@
     @pl.when(step == tiles - 1)
     def _():
         window[edge + tile :, :] = jnp.zeros((edge, width), F32)
-
-    @pl.when(step == 0)
-    def _():
-        for copy in copies:
-            copy.wait()
 
     part = tile // SUBS
 
@@ -416,16 +380,13 @@
     return pl.pallas_call(
         functools.partial(finish_kernel, tiles, halves),
         grid=(tiles,),
-        in_specs=specs + [ANY] * 4 + [pl.BlockSpec(w_depth.shape, lambda i: (0, 0)), ANY],
+        in_specs=specs + [WHOLE] * 4 + [pl.BlockSpec(w_depth.shape, lambda i: (0, 0)), WHOLE],
         out_specs=pl.BlockSpec((tile, codes), lambda i: (i, 0)),
         out_shape=jax.ShapeDtypeStruct((frames, codes), BF16),
         scratch_shapes=[
             pltpu.VMEM((tile + 16, width), F32),
             pltpu.VMEM((tile, width), F32),
             pltpu.VMEM((width, width), BF16),
-            pltpu.VMEM(head.shape, BF16),
-            pltpu.SemaphoreType.DMA((4 * late[0].shape[0],)),
-            pltpu.SemaphoreType.DMA,
         ],
         compiler_params=grant(22),
         cost_estimate=pl.CostEstimate(
@@ -457,13 +418,13 @@
 def step(
     token_ids, decoded_mask, done, table, own_mask, w_qkv, w_out, w_expand, w_depth, w_project, head,
 ):
-    groups = lax.axis_size("level")
-    level_index = lax.axis_index("level")
+    groups = lax.axis_size(LEVEL)
+    level_index = lax.axis_index(LEVEL)
     frames = token_ids.shape[0]
     codes, width = table.shape
     head_dim = width // HEADS
     half = codes // 2
-    core = lax.rem(lax.axis_index("dp"), 2)
+    core = lax.rem(lax.axis_index(DP), 2)
     backs = range(1, groups)
 
     own_out = w_out.T
@@ -488,8 +449,13 @@
     pieces = []
     chunk = columns // CHUNKS if columns % (128 * CHUNKS) == 0 else columns
     for at in range(columns // chunk):
-        pieces.append(gather_pieces(w_qkv[:, :, at * chunk : (at + 1) * chunk]))
-    late = [gather_pieces(shard) for shard in late_shards]
+        near = gather_outer(w_qkv[:, :, at * chunk : (at + 1) * chunk])
+        pieces.append(gather_chip_pairs(near))
+    late = [gather_chip_pairs(gather_outer(late_shards[0]))]
+    near = gather_outer(late_shards[1])
+    for at in range(2):
+        part = [piece[:, at * width : (at + 1) * width] for piece in near]
+        late.append(gather_chip_pairs(part))
 
     tile = frames // QUARTERS
     own = own_term(own_ids[:, None], own_mask, table, tile)
@@ -509,7 +475,7 @@
         result = gate(embedded, some, late[0] + late[1], part * per_half, tile)
         after.append(result[0])
         gated.append(result[1])
-    return finish(gated, after, late[1], w_depth, head, tile)
+    return finish(gated, after, late[2], w_depth, head, tile)
 
 
 def solution(mesh):
@@ -517,18 +483,18 @@
         body,
         mesh=mesh,
         in_specs=(
-            P("dp", "level", None),
-            P("dp", "level", None),
-            P("dp"),
-            P("level", None, None),
-            P("level", None),
-            P(None, "dp", "level"),
-            P("level", "dp"),
-            P("dp", None),
+            P(DP, LEVEL, None),
+            P(DP, LEVEL, None),
+            P(DP),
+            P(LEVEL, None, None),
+            P(LEVEL, None),
+            P(None, DP, LEVEL),
+            P(LEVEL, DP),
+            P(DP, None),
             P(),
-            P("dp", None),
-            P("level", None, None),
+            P(DP, None),
+            P(LEVEL, None, None),
         ),
-        out_specs=P("dp", "level", None, None),
+        out_specs=P(DP, LEVEL, None, None),
         check_vma=False,
     )

time: 238 us -> 228 us (0.958)
  the two profiles are of different devices: /device:TPU:14 before, /device:TPU:24 now
where the time goes in v4:
time: 228 us
  waiting for transfers between devices  107 us (47%)
  Pallas kernels  74.3 us (33%)
  starting transfers between devices  36.9 us (16%)
  local copies, waits for them, and re-layouts  7.31 us (3%)
    ppermute x7, waiting for transfers between devices, from_level(): lax.ppermute(value, LEVEL, [(i, (i + back) % groups) for i in range(group...  41.7 us
    ppermute x12, waiting for transfers between devices, from_outer(): lax.ppermute(value, DP, [(i, (i // 4 + back) % outer * 4 + i % 4) for i i...  32.7 us
    ppermute x16, waiting for transfers between devices, swap(): return lax.ppermute(value, DP, [(i, i ^ bit) for i in range(devices)])  32.1 us
    pallas_call x4, Pallas kernels, attend(): pl.pallas_call(functools.partial(attention_kernel, head_dim, slice(quarte...  26.1 us
    ppermute x12, starting transfers between devices, from_outer(): lax.ppermute(value, DP, [(i, (i // 4 + back) % outer * 4 + i % 4) for i i...  21.3 us
    pallas_call x2, Pallas kernels, gate(): pl.pallas_call(functools.partial(gate_kernel, quarters, groups, width), g...  17.4 us
    pallas_call x1, Pallas kernels, finish(): pl.pallas_call(functools.partial(finish_kernel, tiles, halves), grid=(til...  14.4 us
    pallas_call x1, Pallas kernels, embed_and_project(): pl.pallas_call(functools.partial(project_kernel, others, chunks, scale),...  12.1 us
  transfers between devices with their start and end apart: 35, of which 11 were waited for; matrix products, arithmetic and copies ran while one was open for 3% of the time, Pallas kernels for 26%

profile of v4, /device:TPU:24, one launch (start us, length us, event | category | flops | bytes accessed | tf_op | source)
XLA Modules:
  0.0 227.6 jit_solution(3629042277731266155)
XLA Ops:
  0.0 1.0 slice_bitcast_fusion.6
  1.0 0.4 collective-permute-start.10
  1.4 0.2 collective-permute-start.11
  1.6 3.6 %collective-permute-start.9 = (bf16[3,64,256]{2,1,0:T(8,128)(2,1)S(1)}, bf16[3,64,256]{2,1,0:T(8,128)(2,1)S(1)}, u32[]{:S(2)}, u32[]{:S(2)}) collective-permute-start(bf16[3,64,256]{2,1,0:T(8,128)(2,1)S(1)} %get-tuple-element.36), channel_id=1, source_target_pairs={{0,8},{2,10},{4,12},{6,14},{8,16},{10,18},{12,20},{14,22},{16,24},... | collective-permute-start | bytes 294920 | tf_op jit(solution)/shard_map/ppermute | solution.py:53
  5.2 1.3 dynamic-slice_bitcast_fusion
  6.6 1.1 pad_maximum_fusion
  7.7 1.5 collective-permute-start.1
  9.2 0.5 collective-permute-start.17
  10.5 23.6 %collective-permute-done.17 = bf16[64,512]{1,0:T(8,128)(2,1)S(1)} collective-permute-done((bf16[64,512]{1,0:T(8,128)(2,1)S(1)}, bf16[64,512]{1,0:T(8,128)(2,1)S(1)}, u32[]{:S(2)}, u32[]{:S(2)}) %collective-permute-start.17) | collective-permute-done | bytes 65568 | tf_op jit(solution)/shard_map/ppermute | solution.py:60
  34.1 0.7 collective-permute-start.24
  34.8 1.6 collective-permute-start.3
  36.5 1.2 collective-permute-start.4
  37.7 0.1 pad_maximum_fusion.5.refs_6_
  37.8 8.1 %collective-permute-done.3 = bf16[3,64,256]{2,1,0:T(8,128)(2,1)S(1)} collective-permute-done((bf16[3,64,256]{2,1,0:T(8,128)(2,1)S(1)}, bf16[3,64,256]{2,1,0:T(8,128)(2,1)S(1)}, u32[]{:S(2)}, u32[]{:S(2)}) %collective-permute-start.3) | collective-permute-done | bytes 98336 | tf_op jit(solution)/shard_map/ppermute | solution.py:53
  45.8 1.8 collective-permute-start.18
  47.6 3.1 %collective-permute-done.4 = bf16[3,64,256]{2,1,0:T(8,128)(2,1)S(1)} collective-permute-done((bf16[3,64,256]{2,1,0:T(8,128)(2,1)S(1)}, bf16[3,64,256]{2,1,0:T(8,128)(2,1)S(1)}, u32[]{:S(2)}, u32[]{:S(2)}) %collective-permute-start.4) | collective-permute-done | bytes 98336 | tf_op jit(solution)/shard_map/ppermute | solution.py:53
  50.7 10.5 %collective-permute-start.20 = (bf16[64,2048]{1,0:T(8,128)(2,1)S(1)}, bf16[64,2048]{1,0:T(8,128)(2,1)S(1)}, u32[]{:S(2)}, u32[]{:S(2)}) collective-permute-start(bf16[64,2048]{1,0:T(8,128)(2,1)S(1)} %get-tuple-element.33), channel_id=1, source_target_pairs={{0,24},{2,26},{4,28},{6,30},{8,0},{10,2},{12,4},{14,6},{16,8},{18,... | collective-permute-start | bytes 786440 | tf_op jit(solution)/shard_map/ppermute | solution.py:53
  61.3 0.7 collective-permute-start.25
  62.0 0.7 slice_bitcast_fusion.2
  62.7 0.6 collective-permute-start.26
  63.3 21.4 %collective-permute-done.19 = bf16[64,2048]{1,0:T(8,128)(2,1)S(1)} collective-permute-done((bf16[64,2048]{1,0:T(8,128)(2,1)S(1)}, bf16[64,2048]{1,0:T(8,128)(2,1)S(1)}, u32[]{:S(2)}, u32[]{:S(2)}) %collective-permute-start.19) | collective-permute-done | bytes 262176 | tf_op jit(solution)/shard_map/ppermute | solution.py:53
  84.7 1.5 collective-permute-start
  86.2 1.5 collective-permute-start.12
  87.7 0.1 pad_maximum_fusion.1.refs_4_
  87.9 0.5 collective-permute-done
  88.4 1.5 collective-permute-start.6
  89.9 0.5 collective-permute-start.21
  90.4 0.7 slice_bitcast_fusion.1
  91.1 0.5 collective-permute-start.13
  91.6 6.6 %collective-permute-done.12.refs_7_ = bf16[4,3,64,256]{3,2,1,0:T(8,128)(2,1)S(1)} collective-permute-done((bf16[4,3,64,256]{3,2,1,0:T(8,128)(2,1)S(1)}, bf16[4,3,64,256]{3,2,1,0:T(8,128)(2,1)S(1)}, u32[]{:S(2)}, u32[]{:S(2)}) %collective-permute-start.12) | collective-permute-done | bytes 393248 | tf_op jit(solution)/shard_map/ppermute | solution.py:47
  98.2 0.7 slice_bitcast_fusion
  98.9 0.1 pad_maximum_fusion.2.refs_8_
  99.0 7.7 %collective-permute-done.6.refs_3_ = bf16[4,3,64,256]{3,2,1,0:T(8,128)(2,1)S(1)} collective-permute-done((bf16[4,3,64,256]{3,2,1,0:T(8,128)(2,1)S(1)}, bf16[4,3,64,256]{3,2,1,0:T(8,128)(2,1)S(1)}, u32[]{:S(2)}, u32[]{:S(2)}) %collective-permute-start.6) | collective-permute-done | bytes 393248 | tf_op jit(solution)/shard_map/ppermute | solution.py:47
  106.6 1.5 collective-permute-start.27
  108.2 0.3 copy.12.ids_ref
  108.5 0.1 collective-permute-start.14
  108.6 0.5 collective-permute-start.8
  109.0 1.6 copy-done
  110.7 4.3 %own_term.1.own_ref = bf16[1536,1024]{1,0:T(8,128)(2,1)S(1)} custom-call(s32[1536,1]{1,0:T(8,128)S(1)} %copy.12.ids_ref, bf16[1,1024]{1,0:T(2,128)(2,1)S(1)} %copy-done.1, bf16[1024,1024]{1,0:T(8,128)(2,1)S(1)} %bitcast.40), custom_call_target="tpu_custom_call" | custom-call | flops 3221225472 | bytes 4194304 | tf_op jit(solution)/shard_map/own_term/pallas_call | solution.py:101
  115.0 0.3 stack.104.ids_ref
  115.3 0.1 pad_maximum_fusion.3.refs_8_
  115.3 0.7 slice.44.mask_ref
  116.1 17.8 %collective-permute-done.27.refs_9_ = bf16[4,64,1024]{2,1,0:T(8,128)(2,1)} collective-permute-done((bf16[4,64,1024]{2,1,0:T(8,128)(2,1)S(1)}, bf16[4,64,1024]{2,1,0:T(8,128)(2,1)}, u32[]{:S(2)}, u32[]{:S(2)}) %collective-permute-start.27) | collective-permute-done | bytes 524320 | tf_op jit(solution)/shard_map/ppermute | solution.py:47
  133.9 1.5 collective-permute-start.32
  135.4 0.2 collective-permute-start.22
  135.6 0.3 collective-permute-start.29
  135.9 0.2 collective-permute-start.23
  136.1 12.1 %project.1 = (f32[1536,1024]{1,0:T(8,128)S(1)}, bf16[1536,512]{1,0:T(8,128)(2,1)S(1)}, bf16[1536,512]{1,0:T(8,128)(2,1)S(1)}, bf16[1536,512]{1,0:T(8,128)(2,1)S(1)}) custom-call(s32[1536,1]{1,0:T(8,128)S(1)} %stack.104.ids_ref, bf16[1,1024]{1,0:T(2,128)(2,1)S(1)} %slice.44.mask_ref, bf16[1536,1024]{1,0:T(8,128)(2,1)S(1)} %own_term.1.own_ref, ...), custom_call_target="tpu_custom_call" | custom-call | flops 8053063680 | bytes 20971520 | tf_op jit(solution)/shard_map/project/pallas_call | solution.py:168
  148.3 6.5 %attend.7.refs_2_ = bf16[384,512]{1,0:T(8,128)(2,1)S(1)} custom-call(bf16[1536,512]{1,0:T(8,128)(2,1)S(1)} %get-tuple-element.14.queries_ref, bf16[1536,512]{1,0:T(8,128)(2,1)S(1)} %get-tuple-element.15.keys_ref, bf16[1536,512]{1,0:T(8,128)(2,1)S(1)} %get-tuple-element.16.values_ref), custom_call_target="tpu_custom_call" | custom-call | flops 4831838208 | bytes 4194304 | tf_op jit(solution)/shard_map/attend/pallas_call | solution.py:218
  154.8 6.5 %attend.6.refs_0_ = bf16[384,512]{1,0:T(8,128)(2,1)S(1)} custom-call(bf16[1536,512]{1,0:T(8,128)(2,1)S(1)} %get-tuple-element.14.queries_ref, bf16[1536,512]{1,0:T(8,128)(2,1)S(1)} %get-tuple-element.15.keys_ref, bf16[1536,512]{1,0:T(8,128)(2,1)S(1)} %get-tuple-element.16.values_ref), custom_call_target="tpu_custom_call" | custom-call | flops 4831838208 | bytes 4194304 | tf_op jit(solution)/shard_map/attend/pallas_call | solution.py:218
  161.3 6.5 %attend.5.refs_2_ = bf16[384,512]{1,0:T(8,128)(2,1)S(1)} custom-call(bf16[1536,512]{1,0:T(8,128)(2,1)S(1)} %get-tuple-element.14.queries_ref, bf16[1536,512]{1,0:T(8,128)(2,1)S(1)} %get-tuple-element.15.keys_ref, bf16[1536,512]{1,0:T(8,128)(2,1)S(1)} %get-tuple-element.16.values_ref), custom_call_target="tpu_custom_call" | custom-call | flops 4831838208 | bytes 4194304 | tf_op jit(solution)/shard_map/attend/pallas_call | solution.py:218
  167.9 0.6 collective-permute-start.31
  168.4 1.5 collective-permute-start.30
  170.0 6.5 %attend.4.refs_0_ = bf16[384,512]{1,0:T(8,128)(2,1)S(1)} custom-call(bf16[1536,512]{1,0:T(8,128)(2,1)S(1)} %get-tuple-element.14.queries_ref, bf16[1536,512]{1,0:T(8,128)(2,1)S(1)} %get-tuple-element.15.keys_ref, bf16[1536,512]{1,0:T(8,128)(2,1)S(1)} %get-tuple-element.16.values_ref), custom_call_target="tpu_custom_call" | custom-call | flops 4831838208 | bytes 4194304 | tf_op jit(solution)/shard_map/attend/pallas_call | solution.py:218
  176.5 0.1 collective-permute-start.33
  176.6 0.5 collective-permute-start.34
  177.1 0.5 collective-permute-start.16
  177.6 2.3 %collective-permute-done.31.refs_3_ = bf16[384,512]{1,0:T(8,128)(2,1)S(1)} collective-permute-done((bf16[384,512]{1,0:T(8,128)(2,1)S(1)}, bf16[384,512]{1,0:T(8,128)(2,1)S(1)}, u32[]{:S(2)}, u32[]{:S(2)}) %collective-permute-start.31) | collective-permute-done | bytes 393248 | tf_op jit(solution)/shard_map/ppermute | solution.py:60
  179.9 0.5 collective-permute-start.15
  180.4 7.9 %collective-permute-done.30.refs_1_ = bf16[384,512]{1,0:T(8,128)(2,1)S(1)} collective-permute-done((bf16[384,512]{1,0:T(8,128)(2,1)S(1)}, bf16[384,512]{1,0:T(8,128)(2,1)S(1)}, u32[]{:S(2)}, u32[]{:S(2)}) %collective-permute-start.30) | collective-permute-done | bytes 393248 | tf_op jit(solution)/shard_map/ppermute | solution.py:60
  188.3 8.7 %gate.3 = (f32[768,1024]{1,0:T(8,128)S(1)}, bf16[768,1024]{1,0:T(8,128)(2,1)S(1)}) custom-call(f32[1536,1024]{1,0:T(8,128)S(1)} %get-tuple-element.13.embedded_ref, bf16[384,512]{1,0:T(8,128)(2,1)S(1)} %attend.6.refs_0_, bf16[384,512]{1,0:T(8,128)(2,1)S(1)} %collective-permute-done.30.refs_1_, bf16[384,512]{1,0:T(8,128)(2,1)S(1)} %attend.7.refs_2_, ...), custom_call_target="tpu_custom_call" | custom-call | flops 4831838208 | bytes 12582912 | tf_op jit(solution)/shard_map/gate/pallas_call | solution.py:267
  197.1 7.4 %collective-permute-done.15.refs_1_ = bf16[384,512]{1,0:T(8,128)(2,1)S(1)} collective-permute-done((bf16[384,512]{1,0:T(8,128)(2,1)S(1)}, bf16[384,512]{1,0:T(8,128)(2,1)S(1)}, u32[]{:S(2)}, u32[]{:S(2)}) %collective-permute-start.15) | collective-permute-done | bytes 393248 | tf_op jit(solution)/shard_map/ppermute | solution.py:60
  204.5 8.7 %gate.2 = (f32[768,1024]{1,0:T(8,128)S(1)}, bf16[768,1024]{1,0:T(8,128)(2,1)S(1)}) custom-call(f32[1536,1024]{1,0:T(8,128)S(1)} %get-tuple-element.13.embedded_ref, bf16[384,512]{1,0:T(8,128)(2,1)S(1)} %attend.4.refs_0_, bf16[384,512]{1,0:T(8,128)(2,1)S(1)} %collective-permute-done.15.refs_1_, bf16[384,512]{1,0:T(8,128)(2,1)S(1)} %attend.5.refs_2_, ...), custom_call_target="tpu_custom_call" | custom-call | flops 4831838208 | bytes 12582912 | tf_op jit(solution)/shard_map/gate/pallas_call | solution.py:267
  213.3 14.4 %finish.1 = bf16[1536,1024]{1,0:T(8,128)(2,1)} custom-call(bf16[768,1024]{1,0:T(8,128)(2,1)S(1)} %get-tuple-element.17.refs_0_.refs_1_.refs_2_, bf16[768,1024]{1,0:T(8,128)(2,1)S(1)} %get-tuple-element.17.refs_0_.refs_1_.refs_2_, bf16[768,1024]{1,0:T(8,128)(2,1)S(1)} %get-tuple-element.17.refs_0_.refs_1_.refs_2_, ...), custom_call_target="tpu_custom_call" | custom-call | flops 6442450944 | bytes 20971520 | tf_op jit(solution)/shard_map/finish/pallas_call | solution.py:380
  (69 shorter events, 0.4 us)
Async XLA Ops:
  0.0 6.6 %copy-start.1 = (bf16[1,1024]{1,0:T(2,128)(2,1)S(1)}, bf16[1,1024]{1,0:T(2,128)(2,1)}, u32[]{:S(2)}) copy-start(bf16[1,1024]{1,0:T(2,128)(2,1)} %mask_ref.1) | copy-start | bytes 6148
  1.0 33.8 %collective-permute-start.10 = (bf16[3,64,256]{2,1,0:T(8,128)(2,1)S(1)}, bf16[3,64,256]{2,1,0:T(8,128)(2,1)S(1)}, u32[]{:S(2)}, u32[]{:S(2)}) collective-permute-start(bf16[3,64,256]{2,1,0:T(8,128)(2,1)S(1)} %get-tuple-element.36), channel_id=1, source_target_pairs={{0,16},{2,18},{4,20},{6,22},{8,24},{10,26},{12,28},{14,30},{16,0},... | collective-permute-start | bytes 294920 | tf_op jit(solution)/shard_map/ppermute | solution.py:53
  1.4 35.1 %collective-permute-start.11 = (bf16[3,64,256]{2,1,0:T(8,128)(2,1)S(1)}, bf16[3,64,256]{2,1,0:T(8,128)(2,1)S(1)}, u32[]{:S(2)}, u32[]{:S(2)}) collective-permute-start(bf16[3,64,256]{2,1,0:T(8,128)(2,1)S(1)} %get-tuple-element.36), channel_id=1, source_target_pairs={{0,24},{2,26},{4,28},{6,30},{8,0},{10,2},{12,4},{14,6},{16,8},{18,... | collective-permute-start | bytes 294920 | tf_op jit(solution)/shard_map/ppermute | solution.py:53
  1.6 36.1 %collective-permute-start.9 = (bf16[3,64,256]{2,1,0:T(8,128)(2,1)S(1)}, bf16[3,64,256]{2,1,0:T(8,128)(2,1)S(1)}, u32[]{:S(2)}, u32[]{:S(2)}) collective-permute-start(bf16[3,64,256]{2,1,0:T(8,128)(2,1)S(1)} %get-tuple-element.36), channel_id=1, source_target_pairs={{0,8},{2,10},{4,12},{6,14},{8,16},{10,18},{12,20},{14,22},{16,24},... | collective-permute-start | bytes 294920 | tf_op jit(solution)/shard_map/ppermute | solution.py:53
  5.2 4.0 %copy-start.12 = (bf16[512,64]{0,1:T(8,128)(2,1)S(1)}, bf16[512,64]{0,1:T(8,128)(2,1)}, u32[]{:S(2)}) copy-start(bf16[512,64]{0,1:T(8,128)(2,1)} %param.17) | copy-start | bytes 196612
  5.2 5.2 %copy-start.11 = (bf16[64,2048]{1,0:T(8,128)(2,1)S(1)}, bf16[64,2048]{1,0:T(8,128)(2,1)}, u32[]{:S(2)}) copy-start(bf16[64,2048]{1,0:T(8,128)(2,1)} %param.18) | copy-start | bytes 786436
  5.2 5.2 %copy-start.6 = (bf16[64,1024]{1,0:T(8,128)(2,1)S(1)}, bf16[64,1024]{1,0:T(8,128)(2,1)}, u32[]{:S(2)}) copy-start(bf16[64,1024]{1,0:T(8,128)(2,1)} %param.20) | copy-start | bytes 393220
  6.6 3.9 %copy-start.15 = (s32[1,1,1536]{2,1,0:T(1,128)S(1)}, s32[1,1,1536]{2,1,0:T(1,128)}, u32[]{:S(2)}) copy-start(s32[1,1,1536]{2,1,0:T(1,128)} %param.11) | copy-start | bytes 18436
  6.6 3.9 %copy-start.16 = (s32[1,1,1536]{2,1,0:T(1,128)S(1)}, s32[1,1,1536]{2,1,0:T(1,128)}, u32[]{:S(2)}) copy-start(s32[1,1,1536]{2,1,0:T(1,128)} %param.12) | copy-start | bytes 18436
  7.7 82.7 %collective-permute-start.1 = (bf16[528,1024]{1,0:T(8,128)(2,1)}, bf16[528,1024]{1,0:T(8,128)(2,1)}, u32[]{:S(2)}, u32[]{:S(2)}) collective-permute-start(bf16[528,1024]{1,0:T(8,128)(2,1)} %pad_maximum_fusion), channel_id=1, source_target_pairs={{0,1},{1,0},{2,3},{3,2},{4,5},{5,4},{6,7},{7,6},{8,9},{9,8},{10,11... | collective-permute-start | bytes 3244040 | tf_op jit(solution)/shard_map/ppermute | solution.py:60
  9.2 24.9 %collective-permute-start.17 = (bf16[64,512]{1,0:T(8,128)(2,1)S(1)}, bf16[64,512]{1,0:T(8,128)(2,1)S(1)}, u32[]{:S(2)}, u32[]{:S(2)}) collective-permute-start(bf16[64,512]{1,0:T(8,128)(2,1)S(1)} %bitcast.52), channel_id=1, source_target_pairs={{0,1},{1,0},{2,3},{3,2},{4,5},{5,4},{6,7},{7,6},{8,9},{9,8},{10,11... | collective-permute-start | bytes 196616 | tf_op jit(solution)/shard_map/ppermute | solution.py:60
  34.1 27.2 %collective-permute-start.24 = (bf16[64,2048]{1,0:T(8,128)(2,1)S(1)}, bf16[64,2048]{1,0:T(8,128)(2,1)S(1)}, u32[]{:S(2)}, u32[]{:S(2)}) collective-permute-start(bf16[64,2048]{1,0:T(8,128)(2,1)S(1)} %pad_maximum_fusion.7), channel_id=1, source_target_pairs={{0,8},{2,10},{4,12},{6,14},{8,16},{10,18},{12,20},{14,22},{16,24},... | collective-permute-start | bytes 786440 | tf_op jit(solution)/shard_map/ppermute | solution.py:53
  34.8 11.0 %collective-permute-start.3 = (bf16[3,64,256]{2,1,0:T(8,128)(2,1)S(1)}, bf16[3,64,256]{2,1,0:T(8,128)(2,1)S(1)}, u32[]{:S(2)}, u32[]{:S(2)}) collective-permute-start(bf16[3,64,256]{2,1,0:T(8,128)(2,1)S(1)} %get-tuple-element.37), channel_id=1, source_target_pairs={{0,8},{2,10},{4,12},{6,14},{8,16},{10,18},{12,20},{14,22},{16,24},... | collective-permute-start | bytes 294920 | tf_op jit(solution)/shard_map/ppermute | solution.py:53
  36.5 14.3 %collective-permute-start.4 = (bf16[3,64,256]{2,1,0:T(8,128)(2,1)S(1)}, bf16[3,64,256]{2,1,0:T(8,128)(2,1)S(1)}, u32[]{:S(2)}, u32[]{:S(2)}) collective-permute-start(bf16[3,64,256]{2,1,0:T(8,128)(2,1)S(1)} %get-tuple-element.37), channel_id=1, source_target_pairs={{0,16},{2,18},{4,20},{6,22},{8,24},{10,26},{12,28},{14,30},{16,0},... | collective-permute-start | bytes 294920 | tf_op jit(solution)/shard_map/ppermute | solution.py:53
  37.7 13.0 %collective-permute-start.5 = (bf16[3,64,256]{2,1,0:T(8,128)(2,1)S(1)}, bf16[3,64,256]{2,1,0:T(8,128)(2,1)S(1)}, u32[]{:S(2)}, u32[]{:S(2)}) collective-permute-start(bf16[3,64,256]{2,1,0:T(8,128)(2,1)S(1)} %get-tuple-element.37), channel_id=1, source_target_pairs={{0,24},{2,26},{4,28},{6,30},{8,0},{10,2},{12,4},{14,6},{16,8},{18,... | collective-permute-start | bytes 294920 | tf_op jit(solution)/shard_map/ppermute | solution.py:53
  45.8 16.9 %collective-permute-start.18 = (bf16[64,2048]{1,0:T(8,128)(2,1)S(1)}, bf16[64,2048]{1,0:T(8,128)(2,1)S(1)}, u32[]{:S(2)}, u32[]{:S(2)}) collective-permute-start(bf16[64,2048]{1,0:T(8,128)(2,1)S(1)} %get-tuple-element.33), channel_id=1, source_target_pairs={{0,8},{2,10},{4,12},{6,14},{8,16},{10,18},{12,20},{14,22},{16,24},... | collective-permute-start | bytes 786440 | tf_op jit(solution)/shard_map/ppermute | solution.py:53
  50.7 34.0 %collective-permute-start.19 = (bf16[64,2048]{1,0:T(8,128)(2,1)S(1)}, bf16[64,2048]{1,0:T(8,128)(2,1)S(1)}, u32[]{:S(2)}, u32[]{:S(2)}) collective-permute-start(bf16[64,2048]{1,0:T(8,128)(2,1)S(1)} %get-tuple-element.33), channel_id=1, source_target_pairs={{0,16},{2,18},{4,20},{6,22},{8,24},{10,26},{12,28},{14,30},{16,0},... | collective-permute-start | bytes 786440 | tf_op jit(solution)/shard_map/ppermute | solution.py:53
  50.7 35.5 %collective-permute-start.20 = (bf16[64,2048]{1,0:T(8,128)(2,1)S(1)}, bf16[64,2048]{1,0:T(8,128)(2,1)S(1)}, u32[]{:S(2)}, u32[]{:S(2)}) collective-permute-start(bf16[64,2048]{1,0:T(8,128)(2,1)S(1)} %get-tuple-element.33), channel_id=1, source_target_pairs={{0,24},{2,26},{4,28},{6,30},{8,0},{10,2},{12,4},{14,6},{16,8},{18,... | collective-permute-start | bytes 786440 | tf_op jit(solution)/shard_map/ppermute | solution.py:53
  61.3 28.6 %collective-permute-start.25 = (bf16[64,2048]{1,0:T(8,128)(2,1)S(1)}, bf16[64,2048]{1,0:T(8,128)(2,1)S(1)}, u32[]{:S(2)}, u32[]{:S(2)}) collective-permute-start(bf16[64,2048]{1,0:T(8,128)(2,1)S(1)} %pad_maximum_fusion.7), channel_id=1, source_target_pairs={{0,16},{2,18},{4,20},{6,22},{8,24},{10,26},{12,28},{14,30},{16,0},... | collective-permute-start | bytes 786440 | tf_op jit(solution)/shard_map/ppermute | solution.py:53
  62.7 28.4 %collective-permute-start.26 = (bf16[64,2048]{1,0:T(8,128)(2,1)S(1)}, bf16[64,2048]{1,0:T(8,128)(2,1)S(1)}, u32[]{:S(2)}, u32[]{:S(2)}) collective-permute-start(bf16[64,2048]{1,0:T(8,128)(2,1)S(1)} %pad_maximum_fusion.7), channel_id=1, source_target_pairs={{0,24},{2,26},{4,28},{6,30},{8,0},{10,2},{12,4},{14,6},{16,8},{18,... | collective-permute-start | bytes 786440 | tf_op jit(solution)/shard_map/ppermute | solution.py:53
  84.7 3.7 %collective-permute-start = (s32[1536]{0:T(1024)S(1)}, s32[1536]{0:T(1024)S(1)}, u32[]{:S(2)}, u32[]{:S(2)}) collective-permute-start(s32[1536]{0:T(1024)S(1)} %get-tuple-element.21), channel_id=1, source_target_pairs={{0,1},{1,0},{2,3},{3,2},{4,5},{5,4},{6,7},{7,6},{8,9},{9,8},{10,11... | collective-permute-start | bytes 18440 | tf_op jit(solution)/shard_map/ppermute | solution.py:60
  86.2 12.0 %collective-permute-start.12 = (bf16[4,3,64,256]{3,2,1,0:T(8,128)(2,1)S(1)}, bf16[4,3,64,256]{3,2,1,0:T(8,128)(2,1)S(1)}, u32[]{:S(2)}, u32[]{:S(2)}) collective-permute-start(bf16[4,3,64,256]{3,2,1,0:T(8,128)(2,1)S(1)} %pad_maximum_fusion.5.refs_6_), channel_id=1, source_target_pairs={{0,4},{2,6},{4,0},{6,2},{8,12},{10,14},{12,8},{14,10},{16,20},{18,... | collective-permute-start | bytes 1179656 | tf_op jit(solution)/shard_map/ppermute | solution.py:47
  88.4 19.8 %copy-start.13 = (s32[1536]{0:T(1024)}, s32[1536]{0:T(1024)S(1)}, u32[]{:S(2)}) copy-start(s32[1536]{0:T(1024)S(1)} %collective-permute-done) | copy-start | bytes 18436
  88.4 18.3 %collective-permute-start.6 = (bf16[4,3,64,256]{3,2,1,0:T(8,128)(2,1)S(1)}, bf16[4,3,64,256]{3,2,1,0:T(8,128)(2,1)S(1)}, u32[]{:S(2)}, u32[]{:S(2)}) collective-permute-start(bf16[4,3,64,256]{3,2,1,0:T(8,128)(2,1)S(1)} %pad_maximum_fusion.4.refs_2_), channel_id=1, source_target_pairs={{0,4},{2,6},{4,0},{6,2},{8,12},{10,14},{12,8},{14,10},{16,20},{18,... | collective-permute-start | bytes 1179656 | tf_op jit(solution)/shard_map/ppermute | solution.py:47
  89.9 45.7 %collective-permute-start.21 = (bf16[4,64,2048]{2,1,0:T(8,128)(2,1)S(1)}, bf16[4,64,2048]{2,1,0:T(8,128)(2,1)}, u32[]{:S(2)}, u32[]{:S(2)}) collective-permute-start(bf16[4,64,2048]{2,1,0:T(8,128)(2,1)S(1)} %pad_maximum_fusion.1.refs_4_), channel_id=1, source_target_pairs={{0,4},{2,6},{4,0},{6,2},{8,12},{10,14},{12,8},{14,10},{16,20},{18,... | collective-permute-start | bytes 3145736 | tf_op jit(solution)/shard_map/ppermute | solution.py:47
  90.4 45.5 %collective-permute-start.2 = (bf16[528,1024]{1,0:T(8,128)(2,1)}, bf16[528,1024]{1,0:T(8,128)(2,1)}, u32[]{:S(2)}, u32[]{:S(2)}) collective-permute-start(bf16[528,1024]{1,0:T(8,128)(2,1)} %collective-permute-done.1.refs_0_), channel_id=1, source_target_pairs={{0,2},{2,0},{4,6},{6,4},{8,10},{10,8},{12,14},{14,12},{16,18},{18,... | collective-permute-start | bytes 3244040 | tf_op jit(solution)/shard_map/ppermute | solution.py:47
  91.1 17.4 %collective-permute-start.13 = (bf16[4,3,64,256]{3,2,1,0:T(8,128)(2,1)S(1)}, bf16[4,3,64,256]{3,2,1,0:T(8,128)(2,1)}, u32[]{:S(2)}, u32[]{:S(2)}) collective-permute-start(bf16[4,3,64,256]{3,2,1,0:T(8,128)(2,1)S(1)} %pad_maximum_fusion.5.refs_6_), channel_id=1, source_target_pairs={{0,2},{2,0},{4,6},{6,4},{8,10},{10,8},{12,14},{14,12},{16,18},{18,... | collective-permute-start | bytes 1179656 | tf_op jit(solution)/shard_map/ppermute | solution.py:47
  98.2 10.3 %collective-permute-start.7 = (bf16[4,3,64,256]{3,2,1,0:T(8,128)(2,1)S(1)}, bf16[4,3,64,256]{3,2,1,0:T(8,128)(2,1)}, u32[]{:S(2)}, u32[]{:S(2)}) collective-permute-start(bf16[4,3,64,256]{3,2,1,0:T(8,128)(2,1)S(1)} %pad_maximum_fusion.4.refs_2_), channel_id=1, source_target_pairs={{0,2},{2,0},{4,6},{6,4},{8,10},{10,8},{12,14},{14,12},{16,18},{18,... | collective-permute-start | bytes 1179656 | tf_op jit(solution)/shard_map/ppermute | solution.py:47
  106.6 1.5 copy-start.3
  106.6 27.2 %collective-permute-start.27 = (bf16[4,64,1024]{2,1,0:T(8,128)(2,1)S(1)}, bf16[4,64,1024]{2,1,0:T(8,128)(2,1)}, u32[]{:S(2)}, u32[]{:S(2)}) collective-permute-start(bf16[4,64,1024]{2,1,0:T(8,128)(2,1)S(1)} %pad_maximum_fusion.2.refs_8_), channel_id=1, source_target_pairs={{0,4},{2,6},{4,0},{6,2},{8,12},{10,14},{12,8},{14,10},{16,20},{18,... | collective-permute-start | bytes 1572872 | tf_op jit(solution)/shard_map/ppermute | solution.py:47
  108.5 25.4 %collective-permute-start.14 = (bf16[4,3,64,256]{3,2,1,0:T(8,128)(2,1)S(1)}, bf16[4,3,64,256]{3,2,1,0:T(8,128)(2,1)S(1)}, u32[]{:S(2)}, u32[]{:S(2)}) collective-permute-start(bf16[4,3,64,256]{3,2,1,0:T(8,128)(2,1)S(1)} %collective-permute-done.12.refs_7_), channel_id=1, source_target_pairs={{0,2},{2,0},{4,6},{6,4},{8,10},{10,8},{12,14},{14,12},{16,18},{18,... | collective-permute-start | bytes 1179656 | tf_op jit(solution)/shard_map/ppermute | solution.py:47
  108.6 26.8 %collective-permute-start.8 = (bf16[4,3,64,256]{3,2,1,0:T(8,128)(2,1)}, bf16[4,3,64,256]{3,2,1,0:T(8,128)(2,1)S(1)}, u32[]{:S(2)}, u32[]{:S(2)}) collective-permute-start(bf16[4,3,64,256]{3,2,1,0:T(8,128)(2,1)} %copy-done.3), channel_id=1, source_target_pairs={{0,2},{2,0},{4,6},{6,4},{8,10},{10,8},{12,14},{14,12},{16,18},{18,... | collective-permute-start | bytes 1179656 | tf_op jit(solution)/shard_map/ppermute | solution.py:47
  109.0 1.6 copy-start
  110.6 4.3 %copy-start.14 = (s32[1536]{0:T(1024)S(1)}, s32[1536]{0:T(1024)}, u32[]{:S(2)}) copy-start(s32[1536]{0:T(1024)} %copy-done.13) | copy-start | bytes 18436
  110.6 4.6 %copy-start.7 = (bf16[64,1024]{1,0:T(8,128)(2,1)S(1)}, bf16[64,1024]{1,0:T(8,128)(2,1)}, u32[]{:S(2)}) copy-start(bf16[64,1024]{1,0:T(8,128)(2,1)} %param.20) | copy-start | bytes 393220
  110.6 4.6 %copy-start.8 = (bf16[1,64,1024]{2,1,0:T(8,128)(2,1)S(1)}, bf16[1,64,1024]{2,1,0:T(8,128)(2,1)}, u32[]{:S(2)}) copy-start(bf16[1,64,1024]{2,1,0:T(8,128)(2,1)} %get-tuple-element.23) | copy-start | bytes 393220
  110.6 4.6 %copy-start.9 = (bf16[1,64,1024]{2,1,0:T(8,128)(2,1)S(1)}, bf16[1,64,1024]{2,1,0:T(8,128)(2,1)}, u32[]{:S(2)}) copy-start(bf16[1,64,1024]{2,1,0:T(8,128)(2,1)} %get-tuple-element.25) | copy-start | bytes 393220
  110.6 4.6 %copy-start.10 = (bf16[1,64,1024]{2,1,0:T(8,128)(2,1)S(1)}, bf16[1,64,1024]{2,1,0:T(8,128)(2,1)}, u32[]{:S(2)}) copy-start(bf16[1,64,1024]{2,1,0:T(8,128)(2,1)} %get-tuple-element.27) | copy-start | bytes 393220
  110.7 25.5 %copy-start.4 = (bf16[4,3,64,256]{3,2,1,0:T(8,128)(2,1)S(1)}, bf16[4,3,64,256]{3,2,1,0:T(8,128)(2,1)}, u32[]{:S(2)}) copy-start(bf16[4,3,64,256]{3,2,1,0:T(8,128)(2,1)} %copy-done.3) | copy-start | bytes 1179652
  133.9 34.0 %collective-permute-start.28 = (bf16[4,64,1024]{2,1,0:T(8,128)(2,1)S(1)}, bf16[4,64,1024]{2,1,0:T(8,128)(2,1)S(1)}, u32[]{:S(2)}, u32[]{:S(2)}) collective-permute-start(bf16[4,64,1024]{2,1,0:T(8,128)(2,1)S(1)} %pad_maximum_fusion.2.refs_8_), channel_id=1, source_target_pairs={{0,2},{2,0},{4,6},{6,4},{8,10},{10,8},{12,14},{14,12},{16,18},{18,... | collective-permute-start | bytes 1572872 | tf_op jit(solution)/shard_map/ppermute | solution.py:47
  133.9 34.6 %collective-permute-start.32 = (bf16[4,64,1024]{2,1,0:T(8,128)(2,1)S(1)}, bf16[4,64,1024]{2,1,0:T(8,128)(2,1)S(1)}, u32[]{:S(2)}, u32[]{:S(2)}) collective-permute-start(bf16[4,64,1024]{2,1,0:T(8,128)(2,1)S(1)} %pad_maximum_fusion.3.refs_8_), channel_id=1, source_target_pairs={{0,4},{2,6},{4,0},{6,2},{8,12},{10,14},{12,8},{14,10},{16,20},{18,... | collective-permute-start | bytes 1572872 | tf_op jit(solution)/shard_map/ppermute | solution.py:47
  135.4 41.2 %collective-permute-start.22 = (bf16[4,64,2048]{2,1,0:T(8,128)(2,1)S(1)}, bf16[4,64,2048]{2,1,0:T(8,128)(2,1)S(1)}, u32[]{:S(2)}, u32[]{:S(2)}) collective-permute-start(bf16[4,64,2048]{2,1,0:T(8,128)(2,1)S(1)} %pad_maximum_fusion.1.refs_4_), channel_id=1, source_target_pairs={{0,2},{2,0},{4,6},{6,4},{8,10},{10,8},{12,14},{14,12},{16,18},{18,... | collective-permute-start | bytes 3145736 | tf_op jit(solution)/shard_map/ppermute | solution.py:47
  135.6 40.9 %collective-permute-start.29 = (bf16[4,64,1024]{2,1,0:T(8,128)(2,1)}, bf16[4,64,1024]{2,1,0:T(8,128)(2,1)S(1)}, u32[]{:S(2)}, u32[]{:S(2)}) collective-permute-start(bf16[4,64,1024]{2,1,0:T(8,128)(2,1)} %collective-permute-done.27.refs_9_), channel_id=1, source_target_pairs={{0,2},{2,0},{4,6},{6,4},{8,10},{10,8},{12,14},{14,12},{16,18},{18,... | collective-permute-start | bytes 1572872 | tf_op jit(solution)/shard_map/ppermute | solution.py:47
  135.9 41.2 %collective-permute-start.23 = (bf16[4,64,2048]{2,1,0:T(8,128)(2,1)}, bf16[4,64,2048]{2,1,0:T(8,128)(2,1)S(1)}, u32[]{:S(2)}, u32[]{:S(2)}) collective-permute-start(bf16[4,64,2048]{2,1,0:T(8,128)(2,1)} %collective-permute-done.21.refs_5_), channel_id=1, source_target_pairs={{0,2},{2,0},{4,6},{6,4},{8,10},{10,8},{12,14},{14,12},{16,18},{18,... | collective-permute-start | bytes 3145736 | tf_op jit(solution)/shard_map/ppermute | solution.py:47
  167.9 12.1 %collective-permute-start.31 = (bf16[384,512]{1,0:T(8,128)(2,1)S(1)}, bf16[384,512]{1,0:T(8,128)(2,1)S(1)}, u32[]{:S(2)}, u32[]{:S(2)}) collective-permute-start(bf16[384,512]{1,0:T(8,128)(2,1)S(1)} %attend.7.refs_2_), channel_id=1, source_target_pairs={{0,1},{1,0},{2,3},{3,2},{4,5},{5,4},{6,7},{7,6},{8,9},{9,8},{10,11... | collective-permute-start | bytes 1179656 | tf_op jit(solution)/shard_map/ppermute | solution.py:60
  168.4 19.9 %collective-permute-start.30 = (bf16[384,512]{1,0:T(8,128)(2,1)S(1)}, bf16[384,512]{1,0:T(8,128)(2,1)S(1)}, u32[]{:S(2)}, u32[]{:S(2)}) collective-permute-start(bf16[384,512]{1,0:T(8,128)(2,1)S(1)} %attend.6.refs_0_), channel_id=1, source_target_pairs={{0,1},{1,0},{2,3},{3,2},{4,5},{5,4},{6,7},{7,6},{8,9},{9,8},{10,11... | collective-permute-start | bytes 1179656 | tf_op jit(solution)/shard_map/ppermute | solution.py:60
  176.5 36.7 %collective-permute-start.33 = (bf16[4,64,1024]{2,1,0:T(8,128)(2,1)S(1)}, bf16[4,64,1024]{2,1,0:T(8,128)(2,1)S(1)}, u32[]{:S(2)}, u32[]{:S(2)}) collective-permute-start(bf16[4,64,1024]{2,1,0:T(8,128)(2,1)S(1)} %pad_maximum_fusion.3.refs_8_), channel_id=1, source_target_pairs={{0,2},{2,0},{4,6},{6,4},{8,10},{10,8},{12,14},{14,12},{16,18},{18,... | collective-permute-start | bytes 1572872 | tf_op jit(solution)/shard_map/ppermute | solution.py:47
  176.6 36.7 %collective-permute-start.34 = (bf16[4,64,1024]{2,1,0:T(8,128)(2,1)S(1)}, bf16[4,64,1024]{2,1,0:T(8,128)(2,1)S(1)}, u32[]{:S(2)}, u32[]{:S(2)}) collective-permute-start(bf16[4,64,1024]{2,1,0:T(8,128)(2,1)S(1)} %collective-permute-done.32.refs_9_), channel_id=1, source_target_pairs={{0,2},{2,0},{4,6},{6,4},{8,10},{10,8},{12,14},{14,12},{16,18},{18,... | collective-permute-start | bytes 1572872 | tf_op jit(solution)/shard_map/ppermute | solution.py:47
  177.1 20.0 %collective-permute-start.16 = (bf16[384,512]{1,0:T(8,128)(2,1)S(1)}, bf16[384,512]{1,0:T(8,128)(2,1)S(1)}, u32[]{:S(2)}, u32[]{:S(2)}) collective-permute-start(bf16[384,512]{1,0:T(8,128)(2,1)S(1)} %attend.5.refs_2_), channel_id=1, source_target_pairs={{0,1},{1,0},{2,3},{3,2},{4,5},{5,4},{6,7},{7,6},{8,9},{9,8},{10,11... | collective-permute-start | bytes 1179656 | tf_op jit(solution)/shard_map/ppermute | solution.py:60
  179.9 24.6 %collective-permute-start.15 = (bf16[384,512]{1,0:T(8,128)(2,1)S(1)}, bf16[384,512]{1,0:T(8,128)(2,1)S(1)}, u32[]{:S(2)}, u32[]{:S(2)}) collective-permute-start(bf16[384,512]{1,0:T(8,128)(2,1)S(1)} %attend.4.refs_0_), channel_id=1, source_target_pairs={{0,1},{1,0},{2,3},{3,2},{4,5},{5,4},{6,7},{7,6},{8,9},{9,8},{10,11... | collective-permute-start | bytes 1179656 | tf_op jit(solution)/shard_map/ppermute | solution.py:60
  197.1 16.2 %copy-start.2 = (bf16[1,1024,1024]{2,1,0:T(8,128)(2,1)S(1)}, bf16[1,1024,1024]{2,1,0:T(8,128)(2,1)}, u32[]{:S(2)}) copy-start(bf16[1,1024,1024]{2,1,0:T(8,128)(2,1)} %param.21) | copy-start | bytes 6291460
  197.1 16.2 %copy-start.5 = (bf16[5,1024]{1,0:T(8,128)(2,1)S(1)}, bf16[5,1024]{1,0:T(8,128)(2,1)}, u32[]{:S(2)}) copy-start(bf16[5,1024]{1,0:T(8,128)(2,1)} %refs_12_.1) | copy-start | bytes 30724
